TPU v7x, 32 devices: a whole 2x2x4 slice. The times are simulated.
32 devices in a mesh: gx: 4 (over y, x), gy: 8 (over z, core).
Axes of the slice: x: 2, y: 2, z: 4, core: 2. Of those that a mesh axis runs over, the one named last changes fastest.
Arguments:
- replay_deter: float32 [8192, 2048], P(('gx', 'gy')), may hold values from -1 to 1
- replay_stoch: int32 [8192, 32], P(('gx', 'gy')), may hold values from 0 to 31
- send_rows: int32 [1024, 8], P(('gx', 'gy')), may hold values from 0 to 255
- send_counts: int32 [32, 32], P(('gx', 'gy')), may hold values from 0 to 8, as said below
- actions: int32 [8192, 4], P(('gx', 'gy')), may hold values from 0 to 17
- samples: int32 [8192, 4, 32], P(('gx', 'gy')), may hold values from 0 to 31
- w_stoch: bfloat16 [1024, 6144], P('gy'), may hold values from -1 to 1
- w_deter: bfloat16 [4, 512, 1536], P(None, 'gy'), may hold values from -0.25 to 0.25
- act_table: bfloat16 [18, 6144], replicated, may hold values from -3 to 3
- w_prior: bfloat16 [2048, 1024], P('gy'), may hold values from -0.037353516 to 0.037353516
Outputs:
- imagined: bfloat16 [8192, 4, 2048], P(('gx', 'gy'))
- log_prob: float32 [8192, 4, 32], P(('gx', 'gy'))
Inputs may be any that keep to these rules, and one draw needn't show every extreme that they name: `send_rows`: entries past a destination's count are unused. `send_counts`: each source's counts sum to exactly 128; every source sends 8 rows to some owner, and some owner receives 8 rows from every source.
All inputs are finite; a program needn't handle non-finite values.
Results may differ from a plain program's by a relative error of at most 0.0022.
Values may be sent and summed in bfloat16 or wider, within the bound.
No kernel may reach another device: no remote copies, remote signals or barrier semaphores. Data moves between devices by JAX's collectives and lax.ppermute only.
A program may use at most 128 MiB of HBM per device.

v0:
```python
import functools
import jax
import jax.numpy as jnp
from jax import lax
from jax.experimental import pallas as pl
from jax.experimental.pallas import tpu as pltpu
from jax.sharding import PartitionSpec as P


GROUPS = 32
CLASSES = 32
STEPS = 4
LANES = 128
SCALE = 32767.0
BF16 = jnp.bfloat16
F32 = jnp.float32
I32 = jnp.int32
I16 = jnp.int16


VMEM = pl.BlockSpec(memory_space=pltpu.VMEM)
SMEM = pl.BlockSpec(memory_space=pltpu.SMEM)
ANY = pl.BlockSpec(memory_space=pl.ANY)


def params(mib):
    return pltpu.CompilerParams(vmem_limit_bytes=mib * 2**20)


def swap_pairs(count, mask):
    return [(a, a ^ mask) for a in range(count)]


def tied(value, *others):
    return lax.optimization_barrier((value,) + others)[0]


def shard_of(chip, core, chips, n):
    return lax.rem(chip + chips - n // 2, chips) * 2 + (core ^ (n % 2))


def weights_kernel(idx, w_stoch, w_deter, out, sems):
    srows, cols = w_stoch.shape[0], out.shape[1]
    drows = w_deter.shape[1]
    at = pl.multiple_of(idx[0] * cols, cols)
    copies = [
        pltpu.make_async_copy(
            w_stoch.at[:, pl.ds(at, cols)], out.at[pl.ds(0, srows)], sems.at[0]
        ),
        pltpu.make_async_copy(w_deter.at[idx[0]], out.at[pl.ds(srows, drows)], sems.at[1]),
    ]
    for copy in copies:
        copy.start()
    for copy in copies:
        copy.wait()


def slot_map(chip, chips, run, shape, slot_dim):
    slot = lax.broadcasted_iota(I32, shape, slot_dim)
    place = lax.broadcasted_iota(I32, shape, 1 - slot_dim)
    part = shape[0] // chips
    chunk, rest = place // part, place % part
    return slot == ((rest // run) * chips + (chunk ^ chip)) * run + rest % run


def pack_kernel(chips, nx, cap, idx, rows_ref, counts, deter, stoch, samples, acts, *rest):
    outs = rest[: 2 * nx]
    known = rest[2 * nx]
    s_s, f_s = rest[2 * nx + 1 :]
    ix, chip, core = idx[0], idx[1], idx[2]
    slots = s_s.shape[0]
    half = slots // 2
    width = outs[0].shape[1] - LANES
    lane = lax.broadcasted_iota(I32, (1, LANES), 1)

    def one_dest(n, carry):
        l = n // (chips * nx)
        m = (n // nx) % chips
        o = n % nx
        dest = (o * chips + (m ^ chip)) * 2 + (l ^ core)
        count = counts[0, dest]
        for c in range(cap):
            src = rows_ref[dest, c]
            s_s[pl.ds(n * cap + c, 1), :] = deter[pl.ds(src, 1), :]
            flag = jnp.where(count > c, 1, 0)
            f_s[pl.ds(n * cap + c, 1), :] = jnp.where(
                lane == GROUPS, flag, stoch[pl.ds(src, 1), :]
            )
        return carry

    lax.fori_loop(0, slots // cap, one_dest, 0)
    for k in range(nx):
        at = pl.multiple_of((ix ^ k) * width, width)
        for l in range(2):
            part = s_s[l * half : (l + 1) * half, pl.ds(at, width)]
            out = outs[k * 2 + l]
            out[:, :width] = jnp.round(part * SCALE).astype(I32).astype(I16)
            out[:, width:] = f_s[l * half : (l + 1) * half, :].astype(I16)
    order = slot_map(chip, chips, 2 * cap, (slots, slots), 0)
    order = jnp.where(order, 1.0, 0.0).astype(BF16)
    tail = samples.shape[0]
    known[0:tail, :] = jnp.dot(
        samples[...].astype(F32).astype(BF16), order, preferred_element_type=F32
    ).astype(I32)
    known[tail:, :] = jnp.dot(
        acts[...].astype(F32).astype(BF16), order, preferred_element_type=F32
    ).astype(I32)


def fold_kernel(chips, run, *rest):
    pieces, outs = rest[:-chips], rest[-chips:]
    for m in range(chips):
        for n, piece in enumerate(pieces):
            outs[m][n] = piece[m * run : (m + 1) * run, :]


def place_kernel(chips, splits, idx, *rest):
    pieces, outs, sems = rest[: 2 * chips], rest[2 * chips : -1], rest[-1]
    copies = []
    for n, piece in enumerate(pieces):
        place = shard_of(idx[1], idx[2], chips, n)
        start = 0
        for o, run in enumerate(splits):
            copies.append(
                pltpu.make_async_copy(
                    piece.at[pl.ds(start, run)],
                    outs[o].at[pl.ds(pl.multiple_of(place * run, run), run)],
                    sems.at[n * len(splits) + o],
                )
            )
            start += run
    for copy in copies:
        copy.start()
    for copy in copies:
        copy.wait()


def gru_kernel(rows, cap, nx, m, idx, x, act_table, w_s, wd_s, *rest):
    given = rest[:nx]
    outs = rest[nx : 2 * nx]
    live, wa_s, oh_s, g_s, h_s, f_s, z_s = rest[2 * nx :]
    ix, core = idx[0], idx[2]
    width = wd_s.shape[0]
    kinds = w_s.shape[0]
    cols = w_s.shape[1]
    part = rows // nx
    wa_s[...] = jnp.zeros(wa_s.shape, BF16)
    wa_s[0 : act_table.shape[0], :] = act_table[:, pl.ds(pl.multiple_of(ix * cols, cols), cols)]
    for k in range(nx):
        for l in range(2):
            got = x[k * 2 + l].astype(I32).astype(F32)
            for o in range(nx):
                place = (ix ^ o) * part + (ix ^ k) * (2 * cap) + (core ^ l) * cap
                at = pl.ds(pl.multiple_of(place, cap), cap)
                h_s[at, :] = got[o * cap : (o + 1) * cap, :width] * (1.0 / SCALE)
                f_s[at, :] = got[o * cap : (o + 1) * cap, width:]
    turned = f_s[...].T
    live[...] = turned[GROUPS : GROUPS + 8, 0:part]
    tail = GROUPS * STEPS
    z_s[0:GROUPS, :] = turned[0:GROUPS, :].astype(I32)
    spot = slice(m * part, (m + 1) * part)
    z_s[GROUPS : GROUPS * STEPS, :] = jnp.concatenate(
        [g[0 : GROUPS * (STEPS - 1), spot] for g in given], 1
    )
    z_s[tail : tail + STEPS, :] = jnp.concatenate(
        [g[tail : tail + STEPS, spot] for g in given], 1
    )
    iota = lax.broadcasted_iota(I32, (CLASSES, rows), 0)
    for step in range(STEPS):
        for g in range(GROUPS + 1):
            row = step * GROUPS + g if g < GROUPS else tail + step
            hot = jnp.broadcast_to(z_s[row : row + 1, :], (CLASSES, rows)) == iota
            oh_s[g * CLASSES : (g + 1) * CLASSES, step * rows : (step + 1) * rows] = jnp.where(
                hot, 1.0, 0.0
            ).astype(BF16)
    dims = (((0,), (0,)), ((), ()))
    g_s[...] = lax.dot_general(
        oh_s[0:kinds, :], w_s[...], dims, preferred_element_type=F32
    ) + lax.dot_general(oh_s[kinds:, :], wa_s[...], dims, preferred_element_type=F32)
    keep = jnp.broadcast_to(f_s[:, GROUPS : GROUPS + 1], (rows, width)) > 0
    for step in range(STEPS):
        h = h_s[...]
        gates = g_s[step * rows : (step + 1) * rows, :] + jnp.dot(
            h.astype(BF16), wd_s[...], preferred_element_type=F32
        )
        reset = jax.nn.sigmoid(gates[:, :width])
        cand = jnp.tanh(reset * gates[:, width : 2 * width])
        update = jax.nn.sigmoid(gates[:, 2 * width :] - 1.0)
        h = update * cand + (1.0 - update) * h
        h_s[...] = h
        shown = jnp.where(keep, h, jnp.zeros_like(h)).astype(BF16)
        for k in range(nx):
            outs[k][step] = shown[k * part : (k + 1) * part, :]


def prior_kernel(nx, m, idx, known, live, wp_s, *rest):
    parts = rest[:nx]
    _, states, logp, st_s, out_sems = rest[nx:]
    ix, chip = idx[0], idx[1]
    width = parts[0].shape[2]
    count = parts[0].shape[1]
    for k in range(nx):
        at = pl.multiple_of((ix ^ k) * width, width)
        for step in range(STEPS):
            st_s[step, :, pl.ds(at, width)] = parts[k][step]
    outgo = []
    run = count // nx
    for step in range(STEPS):
        for a in range(nx):
            outgo.append(
                pltpu.make_async_copy(
                    st_s.at[step, pl.ds(a * run, run)],
                    states.at[step, a, chip ^ m],
                    out_sems.at[step * nx + a],
                )
            )
    for copy in outgo:
        copy.start()
    logits = jnp.zeros((STEPS * count, wp_s.shape[1]), F32)
    for k in range(nx):
        at = pl.multiple_of((ix ^ k) * width, width)
        part = parts[k][...].reshape(STEPS * count, width)
        logits = logits + jnp.dot(part, wp_s[pl.ds(at, width), :], preferred_element_type=F32)
    turned = logits.T
    spot = slice(m * count, (m + 1) * count)
    z = jnp.concatenate(
        [known[t * GROUPS : (t + 1) * GROUPS, spot] for t in range(STEPS)], 1
    )
    alive = jnp.concatenate([live[0:1, :]] * STEPS, 1) > 0
    iota = lax.broadcasted_iota(I32, (CLASSES, STEPS * count), 0)
    for g in range(GROUPS):
        own = turned[g * CLASSES : (g + 1) * CLASSES, :]
        total = jnp.log(jnp.sum(jnp.exp(own), 0, keepdims=True))
        hot = jnp.broadcast_to(z[g : g + 1, :], own.shape) == iota
        picked = jnp.sum(jnp.where(hot, own, jnp.zeros_like(own)), 0, keepdims=True)
        logp[g : g + 1, :] = jnp.where(alive, picked - total, jnp.zeros_like(total))
    for copy in outgo:
        copy.wait()


def order_kernel(chips, run, idx, *rest):
    logps, out = rest[:-1], rest[-1]
    slots = out.shape[2]
    part = slots // chips
    order = slot_map(idx[1], chips, run, (slots, slots), 1)
    order = jnp.where(order, 1.0, 0.0).astype(BF16)
    for step in range(STEPS):
        value = jnp.concatenate([p[:, step * part : (step + 1) * part] for p in logps], 1)
        total = jnp.zeros(value.shape, F32)
        for _ in range(3):
            piece = value.astype(BF16)
            total = total + jnp.dot(piece, order, preferred_element_type=F32)
            value = value - piece.astype(F32)
        out[step] = total


def fast_on_device(nx, ny):
    def on_device(
        replay_deter,
        replay_stoch,
        send_rows,
        send_counts,
        actions,
        samples,
        w_stoch,
        w_deter,
        act_table,
        w_prior,
    ):
        peers, cap = send_rows.shape
        slots = peers * cap
        deter = replay_deter.shape[1]
        blocks = w_deter.shape[0]
        width = deter // blocks
        cols = 3 * width
        chips = ny // 2
        part = nx * 2 * cap
        rows = nx * part
        lined = width + LANES
        ix = lax.axis_index("gx").astype(I32)
        iy = lax.axis_index("gy").astype(I32)
        idx = jnp.stack([ix, lax.shift_right_logical(iy, 1), iy & 1])
        ring = [(a, (a + 2) % ny) for a in range(ny)]
        partner = swap_pairs(ny, 1)

        def call(kernel, out_shape, ins, outs, scratch=(), mib=40, flops=0, **kwargs):
            def run(*args):
                return pl.pallas_call(
                    kernel,
                    out_shape=out_shape,
                    in_specs=ins,
                    out_specs=outs,
                    scratch_shapes=scratch,
                    compiler_params=params(mib),
                    cost_estimate=pl.CostEstimate(
                        flops=flops, transcendentals=0, bytes_accessed=2**20
                    ),
                    **kwargs,
                )(*args)

            return run

        srows, drows = w_stoch.shape[0], w_deter.shape[1]
        shard = call(
            weights_kernel,
            jax.ShapeDtypeStruct((srows + drows, cols), BF16),
            [SMEM, ANY, ANY],
            VMEM,
            [pltpu.SemaphoreType.DMA((2,))],
        )(idx, w_stoch, w_deter)
        stops = [shard]
        for _ in range(1, chips):
            stops.append(lax.ppermute(stops[-1], "gy", ring))
        pieces = []
        for piece in stops:
            pieces += [piece, lax.ppermute(piece, "gy", partner)]

        stoch = jnp.pad(replay_stoch, ((0, 0), (0, LANES - replay_stoch.shape[1])))
        samp = jnp.transpose(samples, (1, 2, 0)).reshape(-1, slots)
        *held, known = call(
            functools.partial(pack_kernel, chips, nx, cap),
            [jax.ShapeDtypeStruct((slots // 2, lined), I16)] * (2 * nx)
            + [jax.ShapeDtypeStruct((samp.shape[0] + STEPS, slots), I32)],
            [SMEM] * 3 + [VMEM] * 4,
            [VMEM] * (2 * nx + 1),
            [pltpu.VMEM((slots, deter), F32), pltpu.VMEM((slots, LANES), I32)],
        )(idx, send_rows, send_counts, replay_deter, stoch, samp, jnp.transpose(actions))
        for k in range(nx):
            for l in range(2):
                if k or l:
                    pairs = [
                        (a * ny + b, (a ^ k) * ny + (b ^ l)) for a in range(nx) for b in range(ny)
                    ]
                    n = k * 2 + l
                    held[n] = lax.ppermute(held[n], ("gx", "gy"), pairs)
        given = [known]
        for k in range(1, nx):
            given.append(lax.ppermute(known, "gx", swap_pairs(nx, k)))
        starts = call(
            functools.partial(fold_kernel, chips, nx * cap),
            [jax.ShapeDtypeStruct((2 * nx, nx * cap, lined), I16)] * chips,
            [VMEM] * (2 * nx),
            [VMEM] * chips,
        )(*held)
        starts = list(starts)
        for m in range(1, chips):
            starts[m] = lax.ppermute(starts[m], "gy", swap_pairs(ny, 2 * m))
        w_all, wd_all = call(
            functools.partial(place_kernel, chips, (srows, drows)),
            [
                jax.ShapeDtypeStruct((ny * srows, cols), BF16),
                jax.ShapeDtypeStruct((ny * drows, cols), BF16),
            ],
            [SMEM] + [ANY] * (2 * chips),
            [VMEM] * 2,
            [pltpu.SemaphoreType.DMA((4 * chips,))],
        )(idx, *pieces)

        parts = []
        for m in range(chips):
            *outs, live = call(
                functools.partial(gru_kernel, rows, cap, nx, m),
                [jax.ShapeDtypeStruct((STEPS, part, width), BF16)] * nx
                + [jax.ShapeDtypeStruct((8, part), F32)],
                [SMEM] + [VMEM] * (4 + nx),
                [VMEM] * (nx + 1),
                [
                    pltpu.VMEM((CLASSES, cols), BF16),
                    pltpu.VMEM((GROUPS * CLASSES + CLASSES, STEPS * rows), BF16),
                    pltpu.VMEM((STEPS * rows, cols), F32),
                    pltpu.VMEM((rows, width), F32),
                    pltpu.VMEM((rows, LANES), F32),
                    pltpu.VMEM((GROUPS * STEPS + 8, rows), I32),
                ],
                flops=2 * STEPS * rows * (GROUPS * CLASSES + width) * cols,
            )(idx, starts[m], act_table, w_all, wd_all, *given)
            got = [outs[0]]
            for k in range(1, nx):
                got.append(lax.ppermute(outs[k], "gx", swap_pairs(nx, k)))
            parts.append((live, got))

        piece = tied(w_prior, parts[0][0])
        pieces = []
        for m in range(chips):
            pieces += [piece, lax.ppermute(piece, "gy", partner)]
            if m + 1 < chips:
                piece = lax.ppermute(piece, "gy", ring)
        (wp_all,) = call(
            functools.partial(place_kernel, chips, (w_prior.shape[0],)),
            [jax.ShapeDtypeStruct((deter, GROUPS * CLASSES), BF16)],
            [SMEM] + [ANY] * (2 * chips),
            [VMEM],
            [pltpu.SemaphoreType.DMA((2 * chips,))],
        )(idx, *pieces)

        states = jnp.zeros((STEPS, nx, chips, 2 * cap, deter), BF16)
        logps = []
        for m in range(chips):
            live, got = parts[m]
            states, logp = call(
                functools.partial(prior_kernel, nx, m),
                [
                    jax.ShapeDtypeStruct(states.shape, BF16),
                    jax.ShapeDtypeStruct((GROUPS, STEPS * part), F32),
                ],
                [SMEM] + [VMEM] * (3 + nx) + [ANY],
                [ANY, VMEM],
                [
                    pltpu.VMEM((STEPS, part, deter), BF16),
                    pltpu.SemaphoreType.DMA((STEPS * nx,)),
                ],
                flops=2 * STEPS * part * deter * GROUPS * CLASSES,
                input_output_aliases={4 + nx: 0},
            )(idx, known, live, wp_all, *got, states)
            logps.append(logp)
        logp = call(
            functools.partial(order_kernel, chips, 2 * cap),
            jax.ShapeDtypeStruct((STEPS, GROUPS, slots), F32),
            [SMEM] + [VMEM] * chips,
            VMEM,
        )(idx, *logps)
        states = jnp.transpose(states.reshape(STEPS, slots, deter), (1, 0, 2))
        return (states, jnp.transpose(logp, (2, 0, 1)))

    return on_device


def ring_gather(shard, count, index):
    chips = count // 2
    chip, core = index // 2, index % 2
    full = jnp.zeros((count,) + shard.shape, shard.dtype)
    piece = shard
    for hop in range(chips):
        if hop:
            piece = lax.ppermute(piece, "gy", [(a, (a + 2) % count) for a in range(count)])
        other = lax.ppermute(piece, "gy", swap_pairs(count, 1))
        place = lax.rem(chip + chips - hop, chips) * 2
        full = lax.dynamic_update_index_in_dim(full, piece, place + core, 0)
        full = lax.dynamic_update_index_in_dim(full, other, place + 1 - core, 0)
    return full


def one_hot(values, count):
    hot = values[..., None] == jnp.arange(count, dtype=jnp.int32)
    return hot.reshape(values.shape[0], -1).astype(jnp.bfloat16)


def plain_on_device(nx, ny):
    def on_device(
        replay_deter,
        replay_stoch,
        send_rows,
        send_counts,
        actions,
        samples,
        w_stoch,
        w_deter,
        act_table,
        w_prior,
    ):
        peers, cap = send_rows.shape
        slots = peers * cap
        deter = replay_deter.shape[1]
        blocks = w_deter.shape[0]
        assert blocks == nx
        width = deter // blocks
        cols = 3 * width
        ix = lax.axis_index("gx")
        iy = lax.axis_index("gy")

        ws = lax.dynamic_slice_in_dim(w_stoch, ix * cols, cols, 1)
        wd = lax.dynamic_index_in_dim(w_deter, ix, 0, keepdims=False)
        wa = lax.dynamic_slice_in_dim(act_table, ix * cols, cols, 1)
        ws = ring_gather(ws, ny, iy).reshape(-1, cols)
        wd = ring_gather(wd, ny, iy).reshape(-1, cols)

        picks = send_rows.reshape(slots)
        start = replay_deter[picks].astype(jnp.float16).reshape(nx, ny, cap, blocks, width)
        mine = jnp.zeros((nx, ny, nx, cap, width), jnp.float16)
        for k in range(nx):
            part = lax.dynamic_index_in_dim(start, ix ^ k, 3, keepdims=False)
            if k:
                part = lax.ppermute(part, "gx", swap_pairs(nx, k))
            mine = lax.dynamic_update_index_in_dim(mine, part, ix ^ k, 2)
        rows = jnp.zeros((nx, nx, ny, cap, width), jnp.float16)
        for k in range(ny):
            part = lax.dynamic_index_in_dim(mine, iy ^ k, 1, keepdims=False)
            if k:
                part = lax.ppermute(part, "gy", swap_pairs(ny, k))
            rows = lax.dynamic_update_index_in_dim(rows, part, iy ^ k, 2)
        state = rows.reshape(nx * slots, width).astype(jnp.float32)

        first = replay_stoch[picks].reshape(nx, ny, cap * GROUPS)
        note = jnp.concatenate([first, send_counts[0].reshape(nx, ny, 1)], 2)
        note = jnp.transpose(note, (1, 0, 2)).astype(jnp.bfloat16)
        note = jnp.broadcast_to(note[None], (nx,) + note.shape).reshape(peers, nx, -1)
        note = lax.all_to_all(note, ("gx", "gy"), split_axis=0, concat_axis=0, tiled=True)
        note = note.astype(jnp.int32)
        first = jnp.transpose(note[:, :, : cap * GROUPS], (1, 0, 2)).reshape(nx * slots, GROUPS)
        counts = lax.dynamic_index_in_dim(note, ix, 1, keepdims=False)[:, cap * GROUPS]
        live = (jnp.arange(cap, dtype=jnp.int32)[None, :] < counts[:, None]).reshape(slots)

        known = jnp.concatenate([samples[:, : STEPS - 1].reshape(slots, -1), actions], 1)
        given = jnp.zeros((nx,) + known.shape, known.dtype)
        for k in range(nx):
            part = lax.ppermute(known, "gx", swap_pairs(nx, k)) if k else known
            given = lax.dynamic_update_index_in_dim(given, part, ix ^ k, 0)
        given = given.reshape(nx * slots, -1)

        wp = ring_gather(w_prior, ny, iy).reshape(deter, -1)

        log_prob = []
        states = []
        for step in range(STEPS):
            z = first if step == 0 else given[:, GROUPS * (step - 1) : GROUPS * step]
            act = given[:, GROUPS * (STEPS - 1) + step]
            gates = (
                jnp.dot(one_hot(z, CLASSES), ws, preferred_element_type=jnp.float32)
                + jnp.dot(
                    one_hot(act, act_table.shape[0]), wa, preferred_element_type=jnp.float32
                )
                + jnp.dot(state.astype(jnp.bfloat16), wd, preferred_element_type=jnp.float32)
            )
            reset = jax.nn.sigmoid(gates[:, :width])
            cand = jnp.tanh(reset * gates[:, width : 2 * width])
            update = jax.nn.sigmoid(gates[:, 2 * width :] - 1.0)
            state = update * cand + (1.0 - update) * state
            out = state.astype(jnp.bfloat16).reshape(nx, slots, width)
            whole = jnp.zeros((slots, deter), jnp.bfloat16)
            for k in range(nx):
                part = lax.dynamic_index_in_dim(out, ix ^ k, 0, keepdims=False)
                if k:
                    part = lax.ppermute(part, "gx", swap_pairs(nx, k))
                whole = lax.dynamic_update_slice_in_dim(whole, part, (ix ^ k) * width, 1)
            whole = jnp.where(live[:, None], whole, jnp.zeros_like(whole))
            states.append(whole)
            logits = jnp.dot(whole, wp, preferred_element_type=jnp.float32)
            logits = logits.reshape(slots, GROUPS, CLASSES)
            totals = jnp.log(jnp.sum(jnp.exp(logits), -1))
            hits = samples[:, step, :, None] == jnp.arange(CLASSES, dtype=jnp.int32)
            picked = jnp.sum(jnp.where(hits, logits, jnp.zeros_like(logits)), -1)
            log_prob.append(jnp.where(live[:, None], picked - totals, jnp.zeros_like(totals)))
        return (jnp.stack(states, 1), jnp.stack(log_prob, 1))

    return on_device


def solution(mesh):
    nx, ny = mesh.shape["gx"], mesh.shape["gy"]

    def on_device(*args):
        if args[2].shape[1] % 8 == 0 and ny == 8:
            return fast_on_device(nx, ny)(*args)
        return plain_on_device(nx, ny)(*args)

    in_specs = (
        P(("gx", "gy"), None),
        P(("gx", "gy"), None),
        P(("gx", "gy"), None),
        P(("gx", "gy"), None),
        P(("gx", "gy"), None),
        P(("gx", "gy"), None, None),
        P("gy", None),
        P(None, "gy", None),
        P(),
        P("gy", None),
    )
    out_specs = (P(("gx", "gy"), None, None), P(("gx", "gy"), None, None))
    return jax.shard_map(
        on_device, mesh=mesh, in_specs=in_specs, out_specs=out_specs, check_vma=False
    )
```

profile of v0, /device:TPU:0, one launch (start us, length us, event | category | flops | bytes accessed | tf_op | source)
XLA Modules:
  0.0 231.4 jit_solution(9740033083851264005)
XLA Ops:
  0.7 1.5 copy-done.1
  2.3 1.1 copy-done.2
  4.3 3.1 %collective-permute-start.9 = (bf16[192,1536]{1,0:T(8,128)(2,1)S(1)}, bf16[192,1536]{1,0:T(8,128)(2,1)S(1)}, u32[]{:S(2)}, u32[]{:S(2)}) collective-permute-start(bf16[192,1536]{1,0:T(8,128)(2,1)S(1)} %shard_map.115.rest_0_), channel_id=1, source_target_pairs={{0,2},{1,3},{2,4},{3,5},{4,6},{5,7},{6,0},{7,1},{8,10},{9,11},{10,... | collective-permute-start | bytes 1769480 | tf_op jit(solution)/shard_map/ppermute | solution.py:313
  7.4 15.4 %collective-permute-done.9.rest_2_ = bf16[192,1536]{1,0:T(8,128)(2,1)S(1)} collective-permute-done((bf16[192,1536]{1,0:T(8,128)(2,1)S(1)}, bf16[192,1536]{1,0:T(8,128)(2,1)S(1)}, u32[]{:S(2)}, u32[]{:S(2)}) %collective-permute-start.9) | collective-permute-done | bytes 589856 | tf_op jit(solution)/shard_map/ppermute | solution.py:313
  22.7 16.4 %collective-permute-done.11.rest_4_ = bf16[192,1536]{1,0:T(8,128)(2,1)} collective-permute-done((bf16[192,1536]{1,0:T(8,128)(2,1)S(1)}, bf16[192,1536]{1,0:T(8,128)(2,1)}, u32[]{:S(2)}, u32[]{:S(2)}) %collective-permute-start.11) | collective-permute-done | bytes 589856 | tf_op jit(solution)/shard_map/ppermute | solution.py:313
  40.8 0.9 copy-done.4
  43.0 3.3 %shard_map.113 = (s16[128,640]{1,0:T(8,128)(2,1)S(1)}, s16[128,640]{1,0:T(8,128)(2,1)S(1)}, s16[128,640]{1,0:T(8,128)(2,1)S(1)}, s16[128,640]{1,0:T(8,128)(2,1)S...) custom-call(s32[3]{0:T(128)S(1)} %pad_add_fusion.idx, ...), custom_call_target="tpu_custom_call" | custom-call | bytes 1048576 | tf_op jit(solution)/shard_map/pallas_call | solution.py:288
  46.4 1.3 collective-permute-start.1
  48.2 1.3 collective-permute-start.3
  49.6 3.9 %collective-permute-done.1.rest_2_ = s16[128,640]{1,0:T(8,128)(2,1)S(1)} collective-permute-done((s16[128,640]{1,0:T(8,128)(2,1)S(1)}, s16[128,640]{1,0:T(8,128)(2,1)S(1)}, u32[]{:S(2)}, u32[]{:S(2)}) %collective-permute-start.1) | collective-permute-done | bytes 163872 | tf_op jit(solution)/shard_map/ppermute | solution.py:335
  53.5 2.4 %collective-permute-done.2.rest_3_ = s16[128,640]{1,0:T(8,128)(2,1)S(1)} collective-permute-done((s16[128,640]{1,0:T(8,128)(2,1)S(1)}, s16[128,640]{1,0:T(8,128)(2,1)S(1)}, u32[]{:S(2)}, u32[]{:S(2)}) %collective-permute-start.2) | collective-permute-done | bytes 163872 | tf_op jit(solution)/shard_map/ppermute | solution.py:335
  55.9 1.3 collective-permute-start.4
  57.7 4.2 %collective-permute-done.4.rest_5_ = s16[128,640]{1,0:T(8,128)(2,1)S(1)} collective-permute-done((s16[128,640]{1,0:T(8,128)(2,1)S(1)}, s16[128,640]{1,0:T(8,128)(2,1)S(1)}, u32[]{:S(2)}, u32[]{:S(2)}) %collective-permute-start.4) | collective-permute-done | bytes 163872 | tf_op jit(solution)/shard_map/ppermute | solution.py:335
  61.9 2.2 collective-permute-start.5
  64.1 5.1 %collective-permute-done.5.rest_6_ = s16[128,640]{1,0:T(8,128)(2,1)S(1)} collective-permute-done((s16[128,640]{1,0:T(8,128)(2,1)S(1)}, s16[128,640]{1,0:T(8,128)(2,1)S(1)}, u32[]{:S(2)}, u32[]{:S(2)}) %collective-permute-start.5) | collective-permute-done | bytes 163872 | tf_op jit(solution)/shard_map/ppermute | solution.py:335
  69.3 1.3 collective-permute-start.6
  70.6 5.9 %collective-permute-done.6.rest_7_ = s16[128,640]{1,0:T(8,128)(2,1)S(1)} collective-permute-done((s16[128,640]{1,0:T(8,128)(2,1)S(1)}, s16[128,640]{1,0:T(8,128)(2,1)S(1)}, u32[]{:S(2)}, u32[]{:S(2)}) %collective-permute-start.6) | collective-permute-done | bytes 163872 | tf_op jit(solution)/shard_map/ppermute | solution.py:335
  76.5 2.0 collective-permute-start.17
  79.1 0.9 collective-permute-start.15
  80.2 4.0 %shard_map.116 = (bf16[1024,1536]{1,0:T(8,128)(2,1)S(1)}, bf16[512,1536]{1,0:T(8,128)(2,1)S(1)}) custom-call(s32[3]{0:T(128)S(1)} %pad_add_fusion.idx, bf16[192,1536]{1,0:T(8,128)(2,1)S(1)} %shard_map.115.rest_0_, bf16[192,1536]{1,0:T(8,128)(2,1)S(1)} %collective-permute-done.8.rest_1_, bf16[192,1536]{1,0:T(8,128)(2,1)S(1)} %collective-permute-done.9.rest_2_, ...), custom_call_target="tpu_custom_call" | custom-call | bytes 1048576 | tf_op jit(solution)/shard_map/pallas_call | solution.py:288
  84.2 1.8 collective-permute-done.16.rest_2_
  86.0 7.5 %shard_map.118 = (bf16[4,64,512]{2,1,0:T(8,128)(2,1)S(1)}, bf16[4,64,512]{2,1,0:T(8,128)(2,1)S(1)}, bf16[4,64,512]{2,1,0:T(8,128)(2,1)S(1)}, bf16[4,64,512]{2,1,0:T(8,128)(2,1)S(1)}, f32[8,64]{1,0:T(8,128)S(1)}) custom-call(s32[3]{0:T(128)S(1)} %pad_add_fusion.idx, s16[8,32,640]{2,1,0:T(8,128)(2,1)S(1)} %get-tuple-element.59.x, ...), custom_call_target="tpu_custom_call" | custom-call | flops 4831838208 | bytes 1048576 | tf_op jit(solution)/shard_map/pallas_call | solution.py:288
  93.6 15.9 %collective-permute-done.19.rest_2_ = bf16[256,1024]{1,0:T(8,128)(2,1)S(1)} collective-permute-done((bf16[256,1024]{1,0:T(8,128)(2,1)S(1)}, bf16[256,1024]{1,0:T(8,128)(2,1)S(1)}, u32[]{:S(2)}, u32[]{:S(2)}) %collective-permute-start.19) | collective-permute-done | bytes 524320 | tf_op jit(solution)/shard_map/ppermute | solution.py:387
  109.9 3.4 %collective-permute-start.7 = (s16[8,32,640]{2,1,0:T(8,128)(2,1)S(1)}, s16[8,32,640]{2,1,0:T(8,128)(2,1)S(1)}, u32[]{:S(2)}, u32[]{:S(2)}) collective-permute-start(s16[8,32,640]{2,1,0:T(8,128)(2,1)S(1)} %get-tuple-element.55), channel_id=1, source_target_pairs={{0,6},{1,7},{2,4},{3,5},{4,2},{5,3},{6,0},{7,1},{8,14},{9,15},{10,... | collective-permute-start | bytes 983048 | tf_op jit(solution)/shard_map/ppermute | solution.py:347
  113.9 12.2 %collective-permute-done.21.rest_4_ = bf16[256,1024]{1,0:T(8,128)(2,1)S(1)} collective-permute-done((bf16[256,1024]{1,0:T(8,128)(2,1)S(1)}, bf16[256,1024]{1,0:T(8,128)(2,1)S(1)}, u32[]{:S(2)}, u32[]{:S(2)}) %collective-permute-start.21) | collective-permute-done | bytes 524320 | tf_op jit(solution)/shard_map/ppermute | solution.py:387
  126.1 3.6 %collective-permute-done.32.x = s16[8,32,640]{2,1,0:T(8,128)(2,1)S(1)} collective-permute-done((s16[8,32,640]{2,1,0:T(8,128)(2,1)S(1)}, s16[8,32,640]{2,1,0:T(8,128)(2,1)S(1)}, u32[]{:S(2)}, u32[]{:S(2)}) %collective-permute-start.32) | collective-permute-done | bytes 327712 | tf_op jit(solution)/shard_map/ppermute | solution.py:347
  129.8 7.5 %shard_map.121 = (bf16[4,64,512]{2,1,0:T(8,128)(2,1)S(1)}, bf16[4,64,512]{2,1,0:T(8,128)(2,1)S(1)}, bf16[4,64,512]{2,1,0:T(8,128)(2,1)S(1)}, bf16[4,64,512]{2,1,0:T(8,128)(2,1)S(1)}, f32[8,64]{1,0:T(8,128)S(1)}) custom-call(s32[3]{0:T(128)S(1)} %pad_add_fusion.idx, s16[8,32,640]{2,1,0:T(8,128)(2,1)S(1)} %collective-permute-done.32.x, ...), custom_call_target="tpu_custom_call" | custom-call | flops 4831838208 | bytes 1048576 | tf_op jit(solution)/shard_map/pallas_call | solution.py:288
  137.3 0.9 collective-permute-start.33
  138.2 1.3 collective-permute-start.34
  140.3 23.6 %collective-permute-done.28.x = s16[8,32,640]{2,1,0:T(8,128)(2,1)S(1)} collective-permute-done((s16[8,32,640]{2,1,0:T(8,128)(2,1)S(1)}, s16[8,32,640]{2,1,0:T(8,128)(2,1)S(1)}, u32[]{:S(2)}, u32[]{:S(2)}) %collective-permute-start.28) | collective-permute-done | bytes 327712 | tf_op jit(solution)/shard_map/ppermute | solution.py:347
  163.9 1.6 collective-permute-start.35
  166.0 7.5 %shard_map.120 = (bf16[4,64,512]{2,1,0:T(8,128)(2,1)S(1)}, bf16[4,64,512]{2,1,0:T(8,128)(2,1)S(1)}, bf16[4,64,512]{2,1,0:T(8,128)(2,1)S(1)}, bf16[4,64,512]{2,1,0:T(8,128)(2,1)S(1)}, f32[8,64]{1,0:T(8,128)S(1)}) custom-call(s32[3]{0:T(128)S(1)} %pad_add_fusion.idx, s16[8,32,640]{2,1,0:T(8,128)(2,1)S(1)} %collective-permute-done.28.x, ...), custom_call_target="tpu_custom_call" | custom-call | flops 4831838208 | bytes 1048576 | tf_op jit(solution)/shard_map/pallas_call | solution.py:288
  173.5 0.9 collective-permute-start.29
  174.5 7.8 %collective-permute-done.29.rest_1_ = bf16[4,64,512]{2,1,0:T(8,128)(2,1)S(1)} collective-permute-done((bf16[4,64,512]{2,1,0:T(8,128)(2,1)S(1)}, bf16[4,64,512]{2,1,0:T(8,128)(2,1)S(1)}, u32[]{:S(2)}, u32[]{:S(2)}) %collective-permute-start.29) | collective-permute-done | bytes 262176 | tf_op jit(solution)/shard_map/ppermute | solution.py:379
  183.0 1.6 collective-permute-start.31
  184.6 1.2 collective-permute-start.36
  186.5 1.6 collective-permute-start.38
  188.1 7.8 %shard_map.117 = (bf16[4,64,512]{2,1,0:T(8,128)(2,1)S(1)}, bf16[4,64,512]{2,1,0:T(8,128)(2,1)S(1)}, bf16[4,64,512]{2,1,0:T(8,128)(2,1)S(1)}, bf16[4,64,512]{2,1,0:T(8,128)(2,1)S(1)}, f32[8,64]{1,0:T(8,128)S(1)}) custom-call(s32[3]{0:T(128)S(1)} %pad_add_fusion.idx, s16[8,32,640]{2,1,0:T(8,128)(2,1)S(1)} %collective-permute-done.7.x, ...), custom_call_target="tpu_custom_call" | custom-call | flops 4831838208 | bytes 1048576 | tf_op jit(solution)/shard_map/pallas_call | solution.py:288
  195.9 0.9 shard_map.119.wp_s
  196.8 1.7 collective-permute-done.36.rest_1_
  199.4 7.5 %collective-permute-done.37.rest_2_ = bf16[4,64,512]{2,1,0:T(8,128)(2,1)S(1)} collective-permute-done((bf16[4,64,512]{2,1,0:T(8,128)(2,1)S(1)}, bf16[4,64,512]{2,1,0:T(8,128)(2,1)S(1)}, u32[]{:S(2)}, u32[]{:S(2)}) %collective-permute-start.37) | collective-permute-done | bytes 262176 | tf_op jit(solution)/shard_map/ppermute | solution.py:379
  207.7 1.6 collective-permute-start.27
  209.8 3.7 %shard_map.122 = (bf16[4,4,4,16,2048]{4,3,2,1,0:T(8,128)(2,1)S(1)}, f32[32,256]{1,0:T(8,128)S(1)}) custom-call(s32[3]{0:T(128)S(1)} %pad_add_fusion.idx, s32[132,256]{1,0:T(8,128)S(1)} %get-tuple-element.46.rest_0_.known, f32[8,64]{1,0:T(8,128)S(1)} %get-tuple-element.60.live, ...), custom_call_target="tpu_custom_call", output_to_operand_aliasing={{0}: (8, {})} | custom-call | flops 1073741824 | bytes 1048576 | tf_op jit(solution)/shard_map/pallas_call | solution.py:288
  213.4 3.7 %shard_map.123 = (bf16[4,4,4,16,2048]{4,3,2,1,0:T(8,128)(2,1)S(1)}, f32[32,256]{1,0:T(8,128)S(1)}) custom-call(s32[3]{0:T(128)S(1)} %pad_add_fusion.idx, s32[132,256]{1,0:T(8,128)S(1)} %get-tuple-element.46.rest_0_.known, f32[8,64]{1,0:T(8,128)S(1)} %get-tuple-element.73.live, ...), custom_call_target="tpu_custom_call", output_to_operand_aliasing={{0}: (8, {})} | custom-call | flops 1073741824 | bytes 1048576 | tf_op jit(solution)/shard_map/pallas_call | solution.py:288
  217.1 3.7 %shard_map.124 = (bf16[4,4,4,16,2048]{4,3,2,1,0:T(8,128)(2,1)S(1)}, f32[32,256]{1,0:T(8,128)S(1)}) custom-call(s32[3]{0:T(128)S(1)} %pad_add_fusion.idx, s32[132,256]{1,0:T(8,128)S(1)} %get-tuple-element.46.rest_0_.known, f32[8,64]{1,0:T(8,128)S(1)} %get-tuple-element.67.live, ...), custom_call_target="tpu_custom_call", output_to_operand_aliasing={{0}: (8, {})} | custom-call | flops 1073741824 | bytes 1048576 | tf_op jit(solution)/shard_map/pallas_call | solution.py:288
  220.8 3.7 %shard_map.125 = (bf16[4,4,4,16,2048]{4,3,2,1,0:T(8,128)(2,1)S(1)}, f32[32,256]{1,0:T(8,128)S(1)}) custom-call(s32[3]{0:T(128)S(1)} %pad_add_fusion.idx, s32[132,256]{1,0:T(8,128)S(1)} %get-tuple-element.46.rest_0_.known, f32[8,64]{1,0:T(8,128)S(1)} %get-tuple-element.58.live, ...), custom_call_target="tpu_custom_call", output_to_operand_aliasing={{0}: (8, {})} | custom-call | flops 1073741824 | bytes 1048576 | tf_op jit(solution)/shard_map/pallas_call | solution.py:288
  224.5 5.3 %copy.20 = bf16[4,256,2048]{2,0,1:T(4,128)(2,1)} copy(bf16[4,256,2048]{2,1,0:T(8,128)(2,1)S(1)} %bitcast.12) | data formatting | bytes 8388608 | tf_op jit(solution)/shard_map/reshape | solution.py:422
  229.8 1.6 shard_map.126
  (66 shorter events, 11.8 us)
Async XLA Ops:
  0.6 40.1 %copy-start = (f32[256,2048]{1,0:T(8,128)S(1)}, f32[256,2048]{1,0:T(8,128)}, u32[]{:S(2)}) copy-start(f32[256,2048]{1,0:T(8,128)} %deter.1) | copy-start | bytes 6291460
  0.7 1.5 copy-start.1
  2.3 1.1 copy-start.2
  4.3 18.5 %collective-permute-start.9 = (bf16[192,1536]{1,0:T(8,128)(2,1)S(1)}, bf16[192,1536]{1,0:T(8,128)(2,1)S(1)}, u32[]{:S(2)}, u32[]{:S(2)}) collective-permute-start(bf16[192,1536]{1,0:T(8,128)(2,1)S(1)} %shard_map.115.rest_0_), channel_id=1, source_target_pairs={{0,2},{1,3},{2,4},{3,5},{4,6},{5,7},{6,0},{7,1},{8,10},{9,11},{10,... | collective-permute-start | bytes 1769480 | tf_op jit(solution)/shard_map/ppermute | solution.py:313
  22.7 16.4 %collective-permute-start.11 = (bf16[192,1536]{1,0:T(8,128)(2,1)S(1)}, bf16[192,1536]{1,0:T(8,128)(2,1)}, u32[]{:S(2)}, u32[]{:S(2)}) collective-permute-start(bf16[192,1536]{1,0:T(8,128)(2,1)S(1)} %collective-permute-done.9.rest_2_), channel_id=1, source_target_pairs={{0,2},{1,3},{2,4},{3,5},{4,6},{5,7},{6,0},{7,1},{8,10},{9,11},{10,... | collective-permute-start | bytes 1769480 | tf_op jit(solution)/shard_map/ppermute | solution.py:313
  39.1 18.2 %collective-permute-start.13 = (bf16[192,1536]{1,0:T(8,128)(2,1)}, bf16[192,1536]{1,0:T(8,128)(2,1)}, u32[]{:S(2)}, u32[]{:S(2)}) collective-permute-start(bf16[192,1536]{1,0:T(8,128)(2,1)} %collective-permute-done.11.rest_4_), channel_id=1, source_target_pairs={{0,2},{1,3},{2,4},{3,5},{4,6},{5,7},{6,0},{7,1},{8,10},{9,11},{10,... | collective-permute-start | bytes 1769480 | tf_op jit(solution)/shard_map/ppermute | solution.py:313
  40.8 0.9 copy-start.4
  41.7 0.7 copy-start.5
  42.4 0.7 copy-start.6
  43.0 43.0 %copy-start.7 = (bf16[18,6144]{1,0:T(8,128)(2,1)S(1)}, bf16[18,6144]{1,0:T(8,128)(2,1)}, u32[]{:S(2)}) copy-start(bf16[18,6144]{1,0:T(8,128)(2,1)} %act_table.7) | copy-start | bytes 663556
  46.3 3.2 %collective-permute-start = (s16[128,640]{1,0:T(8,128)(2,1)S(1)}, s16[128,640]{1,0:T(8,128)(2,1)S(1)}, u32[]{:S(2)}, u32[]{:S(2)}) collective-permute-start(s16[128,640]{1,0:T(8,128)(2,1)S(1)} %get-tuple-element.48), channel_id=1, source_target_pairs={{0,1},{1,0},{2,3},{3,2},{4,5},{5,4},{6,7},{7,6},{8,9},{9,8},{10,11... | collective-permute-start | bytes 491528 | tf_op jit(solution)/shard_map/ppermute | solution.py:335
  46.4 7.1 %collective-permute-start.1 = (s16[128,640]{1,0:T(8,128)(2,1)S(1)}, s16[128,640]{1,0:T(8,128)(2,1)S(1)}, u32[]{:S(2)}, u32[]{:S(2)}) collective-permute-start(s16[128,640]{1,0:T(8,128)(2,1)S(1)} %get-tuple-element.49), channel_id=1, source_target_pairs={{0,8},{1,9},{2,10},{3,11},{4,12},{5,13},{6,14},{7,15},{8,0},{9,1},... | collective-permute-start | bytes 491528 | tf_op jit(solution)/shard_map/ppermute | solution.py:335
  47.7 8.2 %collective-permute-start.2 = (s16[128,640]{1,0:T(8,128)(2,1)S(1)}, s16[128,640]{1,0:T(8,128)(2,1)S(1)}, u32[]{:S(2)}, u32[]{:S(2)}) collective-permute-start(s16[128,640]{1,0:T(8,128)(2,1)S(1)} %get-tuple-element.50), channel_id=1, source_target_pairs={{0,9},{1,8},{2,11},{3,10},{4,13},{5,12},{6,15},{7,14},{8,1},{9,0},... | collective-permute-start | bytes 491528 | tf_op jit(solution)/shard_map/ppermute | solution.py:335
  48.2 9.0 %collective-permute-start.3 = (s16[128,640]{1,0:T(8,128)(2,1)S(1)}, s16[128,640]{1,0:T(8,128)(2,1)S(1)}, u32[]{:S(2)}, u32[]{:S(2)}) collective-permute-start(s16[128,640]{1,0:T(8,128)(2,1)S(1)} %get-tuple-element.51), channel_id=1, source_target_pairs={{0,16},{1,17},{2,18},{3,19},{4,20},{5,21},{6,22},{7,23},{8,24},{9,... | collective-permute-start | bytes 491528 | tf_op jit(solution)/shard_map/ppermute | solution.py:335
  49.5 29.1 %collective-permute-start.8 = (bf16[192,1536]{1,0:T(8,128)(2,1)S(1)}, bf16[192,1536]{1,0:T(8,128)(2,1)S(1)}, u32[]{:S(2)}, u32[]{:S(2)}) collective-permute-start(bf16[192,1536]{1,0:T(8,128)(2,1)S(1)} %shard_map.115.rest_0_), channel_id=1, source_target_pairs={{0,1},{1,0},{2,3},{3,2},{4,5},{5,4},{6,7},{7,6},{8,9},{9,8},{10,11... | collective-permute-start | bytes 1769480 | tf_op jit(solution)/shard_map/ppermute | solution.py:316
  53.5 25.6 %collective-permute-start.10 = (bf16[192,1536]{1,0:T(8,128)(2,1)S(1)}, bf16[192,1536]{1,0:T(8,128)(2,1)S(1)}, u32[]{:S(2)}, u32[]{:S(2)}) collective-permute-start(bf16[192,1536]{1,0:T(8,128)(2,1)S(1)} %collective-permute-done.9.rest_2_), channel_id=1, source_target_pairs={{0,1},{1,0},{2,3},{3,2},{4,5},{5,4},{6,7},{7,6},{8,9},{9,8},{10,11... | collective-permute-start | bytes 1769480 | tf_op jit(solution)/shard_map/ppermute | solution.py:316
  55.9 6.0 %collective-permute-start.4 = (s16[128,640]{1,0:T(8,128)(2,1)S(1)}, s16[128,640]{1,0:T(8,128)(2,1)S(1)}, u32[]{:S(2)}, u32[]{:S(2)}) collective-permute-start(s16[128,640]{1,0:T(8,128)(2,1)S(1)} %get-tuple-element.52), channel_id=1, source_target_pairs={{0,17},{1,16},{2,19},{3,18},{4,21},{5,20},{6,23},{7,22},{8,25},{9,... | collective-permute-start | bytes 491528 | tf_op jit(solution)/shard_map/ppermute | solution.py:335
  57.2 22.9 %collective-permute-start.12 = (bf16[192,1536]{1,0:T(8,128)(2,1)}, bf16[192,1536]{1,0:T(8,128)(2,1)S(1)}, u32[]{:S(2)}, u32[]{:S(2)}) collective-permute-start(bf16[192,1536]{1,0:T(8,128)(2,1)} %collective-permute-done.11.rest_4_), channel_id=1, source_target_pairs={{0,1},{1,0},{2,3},{3,2},{4,5},{5,4},{6,7},{7,6},{8,9},{9,8},{10,11... | collective-permute-start | bytes 1769480 | tf_op jit(solution)/shard_map/ppermute | solution.py:316
  57.4 22.8 %collective-permute-start.14 = (bf16[192,1536]{1,0:T(8,128)(2,1)}, bf16[192,1536]{1,0:T(8,128)(2,1)S(1)}, u32[]{:S(2)}, u32[]{:S(2)}) collective-permute-start(bf16[192,1536]{1,0:T(8,128)(2,1)} %collective-permute-done.13.rest_6_), channel_id=1, source_target_pairs={{0,1},{1,0},{2,3},{3,2},{4,5},{5,4},{6,7},{7,6},{8,9},{9,8},{10,11... | collective-permute-start | bytes 1769480 | tf_op jit(solution)/shard_map/ppermute | solution.py:316
  61.9 7.4 %collective-permute-start.5 = (s16[128,640]{1,0:T(8,128)(2,1)S(1)}, s16[128,640]{1,0:T(8,128)(2,1)S(1)}, u32[]{:S(2)}, u32[]{:S(2)}) collective-permute-start(s16[128,640]{1,0:T(8,128)(2,1)S(1)} %get-tuple-element.53), channel_id=1, source_target_pairs={{0,24},{1,25},{2,26},{3,27},{4,28},{5,29},{6,30},{7,31},{8,16},{9,... | collective-permute-start | bytes 491528 | tf_op jit(solution)/shard_map/ppermute | solution.py:335
  69.3 7.3 %collective-permute-start.6 = (s16[128,640]{1,0:T(8,128)(2,1)S(1)}, s16[128,640]{1,0:T(8,128)(2,1)S(1)}, u32[]{:S(2)}, u32[]{:S(2)}) collective-permute-start(s16[128,640]{1,0:T(8,128)(2,1)S(1)} %get-tuple-element.54), channel_id=1, source_target_pairs={{0,25},{1,24},{2,27},{3,26},{4,29},{5,28},{6,31},{7,30},{8,17},{9,... | collective-permute-start | bytes 491528 | tf_op jit(solution)/shard_map/ppermute | solution.py:335
  76.5 7.7 %collective-permute-start.17 = (s32[132,256]{1,0:T(8,128)S(1)}, s32[132,256]{1,0:T(8,128)S(1)}, u32[]{:S(2)}, u32[]{:S(2)}) collective-permute-start(s32[132,256]{1,0:T(8,128)S(1)} %get-tuple-element.46.rest_0_.known), channel_id=1, source_target_pairs={{0,24},{8,16},{16,8},{24,0},{1,25},{9,17},{17,9},{25,1},{2,26},{10... | collective-permute-start | bytes 405512 | tf_op jit(solution)/shard_map/ppermute | solution.py:338
  78.6 7.4 %collective-permute-start.16 = (s32[132,256]{1,0:T(8,128)S(1)}, s32[132,256]{1,0:T(8,128)S(1)}, u32[]{:S(2)}, u32[]{:S(2)}) collective-permute-start(s32[132,256]{1,0:T(8,128)S(1)} %get-tuple-element.46.rest_0_.known), channel_id=1, source_target_pairs={{0,16},{8,24},{16,0},{24,8},{1,17},{9,25},{17,1},{25,9},{2,18},{10... | collective-permute-start | bytes 405512 | tf_op jit(solution)/shard_map/ppermute | solution.py:338
  79.1 6.9 %collective-permute-start.15 = (s32[132,256]{1,0:T(8,128)S(1)}, s32[132,256]{1,0:T(8,128)S(1)}, u32[]{:S(2)}, u32[]{:S(2)}) collective-permute-start(s32[132,256]{1,0:T(8,128)S(1)} %get-tuple-element.46.rest_0_.known), channel_id=1, source_target_pairs={{0,8},{8,0},{16,24},{24,16},{1,9},{9,1},{17,25},{25,17},{2,10},{10... | collective-permute-start | bytes 405512 | tf_op jit(solution)/shard_map/ppermute | solution.py:338
  86.0 7.5 %copy-start.3 = (bf16[256,1024]{1,0:T(8,128)(2,1)S(1)}, bf16[256,1024]{1,0:T(8,128)(2,1)}, u32[]{:S(2)}) copy-start(bf16[256,1024]{1,0:T(8,128)(2,1)} %rest_0_) | copy-start | bytes 1572868
  93.5 16.0 %collective-permute-start.19 = (bf16[256,1024]{1,0:T(8,128)(2,1)S(1)}, bf16[256,1024]{1,0:T(8,128)(2,1)S(1)}, u32[]{:S(2)}, u32[]{:S(2)}) collective-permute-start(bf16[256,1024]{1,0:T(8,128)(2,1)S(1)} %copy-done.3), channel_id=1, source_target_pairs={{0,2},{1,3},{2,4},{3,5},{4,6},{5,7},{6,0},{7,1},{8,10},{9,11},{10,... | collective-permute-start | bytes 1572872 | tf_op jit(solution)/shard_map/ppermute | solution.py:387
  109.5 16.6 %collective-permute-start.21 = (bf16[256,1024]{1,0:T(8,128)(2,1)S(1)}, bf16[256,1024]{1,0:T(8,128)(2,1)S(1)}, u32[]{:S(2)}, u32[]{:S(2)}) collective-permute-start(bf16[256,1024]{1,0:T(8,128)(2,1)S(1)} %collective-permute-done.19.rest_2_), channel_id=1, source_target_pairs={{0,2},{1,3},{2,4},{3,5},{4,6},{5,7},{6,0},{7,1},{8,10},{9,11},{10,... | collective-permute-start | bytes 1572872 | tf_op jit(solution)/shard_map/ppermute | solution.py:387
  109.5 20.3 %collective-permute-start.32 = (s16[8,32,640]{2,1,0:T(8,128)(2,1)S(1)}, s16[8,32,640]{2,1,0:T(8,128)(2,1)S(1)}, u32[]{:S(2)}, u32[]{:S(2)}) collective-permute-start(s16[8,32,640]{2,1,0:T(8,128)(2,1)S(1)} %get-tuple-element.72), channel_id=1, source_target_pairs={{0,2},{1,3},{2,0},{3,1},{4,6},{5,7},{6,4},{7,5},{8,10},{9,11},{10,... | collective-permute-start | bytes 983048 | tf_op jit(solution)/shard_map/ppermute | solution.py:347
  109.9 30.4 %collective-permute-start.7 = (s16[8,32,640]{2,1,0:T(8,128)(2,1)S(1)}, s16[8,32,640]{2,1,0:T(8,128)(2,1)S(1)}, u32[]{:S(2)}, u32[]{:S(2)}) collective-permute-start(s16[8,32,640]{2,1,0:T(8,128)(2,1)S(1)} %get-tuple-element.55), channel_id=1, source_target_pairs={{0,6},{1,7},{2,4},{3,5},{4,2},{5,3},{6,0},{7,1},{8,14},{9,15},{10,... | collective-permute-start | bytes 983048 | tf_op jit(solution)/shard_map/ppermute | solution.py:347
  113.3 50.5 %collective-permute-start.28 = (s16[8,32,640]{2,1,0:T(8,128)(2,1)S(1)}, s16[8,32,640]{2,1,0:T(8,128)(2,1)S(1)}, u32[]{:S(2)}, u32[]{:S(2)}) collective-permute-start(s16[8,32,640]{2,1,0:T(8,128)(2,1)S(1)} %get-tuple-element.66), channel_id=1, source_target_pairs={{0,4},{1,5},{2,6},{3,7},{4,0},{5,1},{6,2},{7,3},{8,12},{9,13},{10,... | collective-permute-start | bytes 983048 | tf_op jit(solution)/shard_map/ppermute | solution.py:347
  126.1 39.8 %collective-permute-start.23 = (bf16[256,1024]{1,0:T(8,128)(2,1)S(1)}, bf16[256,1024]{1,0:T(8,128)(2,1)S(1)}, u32[]{:S(2)}, u32[]{:S(2)}) collective-permute-start(bf16[256,1024]{1,0:T(8,128)(2,1)S(1)} %collective-permute-done.21.rest_4_), channel_id=1, source_target_pairs={{0,2},{1,3},{2,4},{3,5},{4,6},{5,7},{6,0},{7,1},{8,10},{9,11},{10,... | collective-permute-start | bytes 1572872 | tf_op jit(solution)/shard_map/ppermute | solution.py:387
  137.3 28.1 %collective-permute-start.33 = (bf16[4,64,512]{2,1,0:T(8,128)(2,1)S(1)}, bf16[4,64,512]{2,1,0:T(8,128)(2,1)S(1)}, u32[]{:S(2)}, u32[]{:S(2)}) collective-permute-start(bf16[4,64,512]{2,1,0:T(8,128)(2,1)S(1)} %get-tuple-element.75), channel_id=1, source_target_pairs={{0,8},{8,0},{16,24},{24,16},{1,9},{9,1},{17,25},{25,17},{2,10},{10... | collective-permute-start | bytes 786440 | tf_op jit(solution)/shard_map/ppermute | solution.py:379
  138.2 27.2 %collective-permute-start.34 = (bf16[4,64,512]{2,1,0:T(8,128)(2,1)S(1)}, bf16[4,64,512]{2,1,0:T(8,128)(2,1)S(1)}, u32[]{:S(2)}, u32[]{:S(2)}) collective-permute-start(bf16[4,64,512]{2,1,0:T(8,128)(2,1)S(1)} %get-tuple-element.76), channel_id=1, source_target_pairs={{0,16},{8,24},{16,0},{24,8},{1,17},{9,25},{17,1},{25,9},{2,18},{10... | collective-permute-start | bytes 786440 | tf_op jit(solution)/shard_map/ppermute | solution.py:379
  140.3 42.7 %collective-permute-start.18 = (bf16[256,1024]{1,0:T(8,128)(2,1)S(1)}, bf16[256,1024]{1,0:T(8,128)(2,1)S(1)}, u32[]{:S(2)}, u32[]{:S(2)}) collective-permute-start(bf16[256,1024]{1,0:T(8,128)(2,1)S(1)} %copy-done.3), channel_id=1, source_target_pairs={{0,1},{1,0},{2,3},{3,2},{4,5},{5,4},{6,7},{7,6},{8,9},{9,8},{10,11... | collective-permute-start | bytes 1572872 | tf_op jit(solution)/shard_map/ppermute | solution.py:385
  163.9 9.7 %collective-permute-start.35 = (bf16[4,64,512]{2,1,0:T(8,128)(2,1)S(1)}, bf16[4,64,512]{2,1,0:T(8,128)(2,1)S(1)}, u32[]{:S(2)}, u32[]{:S(2)}) collective-permute-start(bf16[4,64,512]{2,1,0:T(8,128)(2,1)S(1)} %get-tuple-element.77), channel_id=1, source_target_pairs={{0,24},{8,16},{16,8},{24,0},{1,25},{9,17},{17,9},{25,1},{2,26},{10... | collective-permute-start | bytes 786440 | tf_op jit(solution)/shard_map/ppermute | solution.py:379
  165.4 19.2 %collective-permute-start.20 = (bf16[256,1024]{1,0:T(8,128)(2,1)S(1)}, bf16[256,1024]{1,0:T(8,128)(2,1)S(1)}, u32[]{:S(2)}, u32[]{:S(2)}) collective-permute-start(bf16[256,1024]{1,0:T(8,128)(2,1)S(1)} %collective-permute-done.19.rest_2_), channel_id=1, source_target_pairs={{0,1},{1,0},{2,3},{3,2},{4,5},{5,4},{6,7},{7,6},{8,9},{9,8},{10,11... | collective-permute-start | bytes 1572872 | tf_op jit(solution)/shard_map/ppermute | solution.py:385
  165.4 20.3 %collective-permute-start.22 = (bf16[256,1024]{1,0:T(8,128)(2,1)S(1)}, bf16[256,1024]{1,0:T(8,128)(2,1)S(1)}, u32[]{:S(2)}, u32[]{:S(2)}) collective-permute-start(bf16[256,1024]{1,0:T(8,128)(2,1)S(1)} %collective-permute-done.21.rest_4_), channel_id=1, source_target_pairs={{0,1},{1,0},{2,3},{3,2},{4,5},{5,4},{6,7},{7,6},{8,9},{9,8},{10,11... | collective-permute-start | bytes 1572872 | tf_op jit(solution)/shard_map/ppermute | solution.py:385
  166.0 20.6 %collective-permute-start.24 = (bf16[256,1024]{1,0:T(8,128)(2,1)S(1)}, bf16[256,1024]{1,0:T(8,128)(2,1)S(1)}, u32[]{:S(2)}, u32[]{:S(2)}) collective-permute-start(bf16[256,1024]{1,0:T(8,128)(2,1)S(1)} %collective-permute-done.23.rest_6_), channel_id=1, source_target_pairs={{0,1},{1,0},{2,3},{3,2},{4,5},{5,4},{6,7},{7,6},{8,9},{9,8},{10,11... | collective-permute-start | bytes 1572872 | tf_op jit(solution)/shard_map/ppermute | solution.py:385
  173.5 8.7 %collective-permute-start.29 = (bf16[4,64,512]{2,1,0:T(8,128)(2,1)S(1)}, bf16[4,64,512]{2,1,0:T(8,128)(2,1)S(1)}, u32[]{:S(2)}, u32[]{:S(2)}) collective-permute-start(bf16[4,64,512]{2,1,0:T(8,128)(2,1)S(1)} %get-tuple-element.69), channel_id=1, source_target_pairs={{0,8},{8,0},{16,24},{24,16},{1,9},{9,1},{17,25},{25,17},{2,10},{10... | collective-permute-start | bytes 786440 | tf_op jit(solution)/shard_map/ppermute | solution.py:379
  182.3 34.8 %collective-permute-start.30 = (bf16[4,64,512]{2,1,0:T(8,128)(2,1)S(1)}, bf16[4,64,512]{2,1,0:T(8,128)(2,1)S(1)}, u32[]{:S(2)}, u32[]{:S(2)}) collective-permute-start(bf16[4,64,512]{2,1,0:T(8,128)(2,1)S(1)} %get-tuple-element.70), channel_id=1, source_target_pairs={{0,16},{8,24},{16,0},{24,8},{1,17},{9,25},{17,1},{25,9},{2,18},{10... | collective-permute-start | bytes 786440 | tf_op jit(solution)/shard_map/ppermute | solution.py:379
  183.0 34.1 %collective-permute-start.31 = (bf16[4,64,512]{2,1,0:T(8,128)(2,1)S(1)}, bf16[4,64,512]{2,1,0:T(8,128)(2,1)S(1)}, u32[]{:S(2)}, u32[]{:S(2)}) collective-permute-start(bf16[4,64,512]{2,1,0:T(8,128)(2,1)S(1)} %get-tuple-element.71), channel_id=1, source_target_pairs={{0,24},{8,16},{16,8},{24,0},{1,25},{9,17},{17,9},{25,1},{2,26},{10... | collective-permute-start | bytes 786440 | tf_op jit(solution)/shard_map/ppermute | solution.py:379
  184.6 13.9 %collective-permute-start.36 = (bf16[4,64,512]{2,1,0:T(8,128)(2,1)S(1)}, bf16[4,64,512]{2,1,0:T(8,128)(2,1)S(1)}, u32[]{:S(2)}, u32[]{:S(2)}) collective-permute-start(bf16[4,64,512]{2,1,0:T(8,128)(2,1)S(1)} %get-tuple-element.79), channel_id=1, source_target_pairs={{0,8},{8,0},{16,24},{24,16},{1,9},{9,1},{17,25},{25,17},{2,10},{10... | collective-permute-start | bytes 786440 | tf_op jit(solution)/shard_map/ppermute | solution.py:379
  185.8 21.1 %collective-permute-start.37 = (bf16[4,64,512]{2,1,0:T(8,128)(2,1)S(1)}, bf16[4,64,512]{2,1,0:T(8,128)(2,1)S(1)}, u32[]{:S(2)}, u32[]{:S(2)}) collective-permute-start(bf16[4,64,512]{2,1,0:T(8,128)(2,1)S(1)} %get-tuple-element.80), channel_id=1, source_target_pairs={{0,16},{8,24},{16,0},{24,8},{1,17},{9,25},{17,1},{25,9},{2,18},{10... | collective-permute-start | bytes 786440 | tf_op jit(solution)/shard_map/ppermute | solution.py:379
  186.5 21.1 %collective-permute-start.38 = (bf16[4,64,512]{2,1,0:T(8,128)(2,1)S(1)}, bf16[4,64,512]{2,1,0:T(8,128)(2,1)S(1)}, u32[]{:S(2)}, u32[]{:S(2)}) collective-permute-start(bf16[4,64,512]{2,1,0:T(8,128)(2,1)S(1)} %get-tuple-element.81), channel_id=1, source_target_pairs={{0,24},{8,16},{16,8},{24,0},{1,25},{9,17},{17,9},{25,1},{2,26},{10... | collective-permute-start | bytes 786440 | tf_op jit(solution)/shard_map/ppermute | solution.py:379
  198.5 22.3 %collective-permute-start.25 = (bf16[4,64,512]{2,1,0:T(8,128)(2,1)S(1)}, bf16[4,64,512]{2,1,0:T(8,128)(2,1)S(1)}, u32[]{:S(2)}, u32[]{:S(2)}) collective-permute-start(bf16[4,64,512]{2,1,0:T(8,128)(2,1)S(1)} %get-tuple-element.63), channel_id=1, source_target_pairs={{0,8},{8,0},{16,24},{24,16},{1,9},{9,1},{17,25},{25,17},{2,10},{10... | collective-permute-start | bytes 786440 | tf_op jit(solution)/shard_map/ppermute | solution.py:379
  206.9 13.9 %collective-permute-start.26 = (bf16[4,64,512]{2,1,0:T(8,128)(2,1)S(1)}, bf16[4,64,512]{2,1,0:T(8,128)(2,1)S(1)}, u32[]{:S(2)}, u32[]{:S(2)}) collective-permute-start(bf16[4,64,512]{2,1,0:T(8,128)(2,1)S(1)} %get-tuple-element.64), channel_id=1, source_target_pairs={{0,16},{8,24},{16,0},{24,8},{1,17},{9,25},{17,1},{25,9},{2,18},{10... | collective-permute-start | bytes 786440 | tf_op jit(solution)/shard_map/ppermute | solution.py:379
  207.7 13.1 %collective-permute-start.27 = (bf16[4,64,512]{2,1,0:T(8,128)(2,1)S(1)}, bf16[4,64,512]{2,1,0:T(8,128)(2,1)S(1)}, u32[]{:S(2)}, u32[]{:S(2)}) collective-permute-start(bf16[4,64,512]{2,1,0:T(8,128)(2,1)S(1)} %get-tuple-element.65), channel_id=1, source_target_pairs={{0,24},{8,16},{16,8},{24,0},{1,25},{9,17},{17,9},{25,1},{2,26},{10... | collective-permute-start | bytes 786440 | tf_op jit(solution)/shard_map/ppermute | solution.py:379
where the time goes:
time: 232 us; the launch traced here: 231 us
  waiting for transfers between devices  128 us (55%)
  Pallas kernels  55.7 us (24%)
  starting transfers between devices  34 us (15%)
  local copies, waits for them, and re-layouts  12.3 us (5%)
    pallas_call x14, Pallas kernels, run(): pl.pallas_call(kernel, out_shape=out_shape, in_specs=ins, out_specs=outs,...  55.7 us
    ppermute x3, waiting for transfers between devices, on_device(): stops.append(lax.ppermute(stops[-1], 'gy', ring))  31.7 us
    ppermute x3, waiting for transfers between devices, on_device(): piece = lax.ppermute(piece, 'gy', ring)  28.2 us
    ppermute x3, waiting for transfers between devices, on_device(): starts[m] = lax.ppermute(starts[m], 'gy', swap_pairs(ny, 2 * m))  28 us
    ppermute x7, waiting for transfers between devices, on_device(): held[n] = lax.ppermute(held[n], ('gx', 'gy'), pairs)  21.6 us
    ppermute x12, waiting for transfers between devices, on_device(): got.append(lax.ppermute(outs[k], 'gx', swap_pairs(nx, k)))  17 us
    ppermute x12, starting transfers between devices, on_device(): got.append(lax.ppermute(outs[k], 'gx', swap_pairs(nx, k)))  13.7 us
    ppermute x7, starting transfers between devices, on_device(): held[n] = lax.ppermute(held[n], ('gx', 'gy'), pairs)  8.06 us
  transfers between devices with their start and end apart: 39, of which 16 were waited for; matrix products, arithmetic and copies ran while one was open for 1% of the time, Pallas kernels for 18%

commit v1 on v0

--- a/solution.py
+++ b/solution.py
@@ -21,6 +21,7 @@
 VMEM = pl.BlockSpec(memory_space=pltpu.VMEM)
 SMEM = pl.BlockSpec(memory_space=pltpu.SMEM)
 ANY = pl.BlockSpec(memory_space=pl.ANY)
+HBM = pl.BlockSpec(memory_space=pltpu.HBM)
 
 
 def params(mib):
@@ -31,23 +32,23 @@
     return [(a, a ^ mask) for a in range(count)]
 
 
-def tied(value, *others):
-    return lax.optimization_barrier((value,) + others)[0]
-
-
 def shard_of(chip, core, chips, n):
     return lax.rem(chip + chips - n // 2, chips) * 2 + (core ^ (n % 2))
 
 
-def weights_kernel(idx, w_stoch, w_deter, out, sems):
+def weights_kernel(idx, w_stoch, w_deter, w_prior, out, quarter, sems):
     srows, cols = w_stoch.shape[0], out.shape[1]
     drows = w_deter.shape[1]
+    wide = quarter.shape[1]
     at = pl.multiple_of(idx[0] * cols, cols)
     copies = [
         pltpu.make_async_copy(
             w_stoch.at[:, pl.ds(at, cols)], out.at[pl.ds(0, srows)], sems.at[0]
         ),
         pltpu.make_async_copy(w_deter.at[idx[0]], out.at[pl.ds(srows, drows)], sems.at[1]),
+        pltpu.make_async_copy(
+            w_prior.at[:, pl.ds(pl.multiple_of(idx[0] * wide, wide), wide)], quarter, sems.at[2]
+        ),
     ]
     for copy in copies:
         copy.start()
@@ -66,12 +67,13 @@
 def pack_kernel(chips, nx, cap, idx, rows_ref, counts, deter, stoch, samples, acts, *rest):
     outs = rest[: 2 * nx]
     known = rest[2 * nx]
-    s_s, f_s = rest[2 * nx + 1 :]
+    s_s, f_s, p_s = rest[2 * nx + 1 :]
     ix, chip, core = idx[0], idx[1], idx[2]
     slots = s_s.shape[0]
     half = slots // 2
     width = outs[0].shape[1] - LANES
     lane = lax.broadcasted_iota(I32, (1, LANES), 1)
+    spot = lax.broadcasted_iota(I32, (1, deter.shape[0]), 1)
 
     def one_dest(n, carry):
         l = n // (chips * nx)
@@ -80,22 +82,28 @@
         dest = (o * chips + (m ^ chip)) * 2 + (l ^ core)
         count = counts[0, dest]
         for c in range(cap):
-            src = rows_ref[dest, c]
+            src = rows_ref[c, dest]
             s_s[pl.ds(n * cap + c, 1), :] = deter[pl.ds(src, 1), :]
-            flag = jnp.where(count > c, 1, 0)
+            p_s[pl.ds(n * cap + c, 1), :] = jnp.where(spot == src, 1.0, 0.0)
             f_s[pl.ds(n * cap + c, 1), :] = jnp.where(
-                lane == GROUPS, flag, stoch[pl.ds(src, 1), :]
+                lane == GROUPS, jnp.where(count > c, 1.0, 0.0), 0.0
             )
         return carry
 
     lax.fori_loop(0, slots // cap, one_dest, 0)
+    f_s[:, 0 : stoch.shape[0]] = lax.dot_general(
+        p_s[...].astype(BF16),
+        stoch[...].astype(F32).astype(BF16),
+        (((1,), (1,)), ((), ())),
+        preferred_element_type=F32,
+    )
     for k in range(nx):
         at = pl.multiple_of((ix ^ k) * width, width)
         for l in range(2):
             part = s_s[l * half : (l + 1) * half, pl.ds(at, width)]
             out = outs[k * 2 + l]
             out[:, :width] = jnp.round(part * SCALE).astype(I32).astype(I16)
-            out[:, width:] = f_s[l * half : (l + 1) * half, :].astype(I16)
+            out[:, width:] = f_s[l * half : (l + 1) * half, :].astype(I32).astype(I16)
     order = slot_map(chip, chips, 2 * cap, (slots, slots), 0)
     order = jnp.where(order, 1.0, 0.0).astype(BF16)
     tail = samples.shape[0]
@@ -114,18 +122,20 @@
             outs[m][n] = piece[m * run : (m + 1) * run, :]
 
 
-def place_kernel(chips, splits, idx, *rest):
-    pieces, outs, sems = rest[: 2 * chips], rest[2 * chips : -1], rest[-1]
+def place_kernel(chips, splits, first, held, idx, *rest):
+    count = len(splits)
+    outs, sems = rest[-1 - count : -1], rest[-1]
+    pieces = rest[: len(rest) - 1 - count - held]
     copies = []
     for n, piece in enumerate(pieces):
-        place = shard_of(idx[1], idx[2], chips, n)
+        place = shard_of(idx[1], idx[2], chips, n + first)
         start = 0
         for o, run in enumerate(splits):
             copies.append(
                 pltpu.make_async_copy(
                     piece.at[pl.ds(start, run)],
                     outs[o].at[pl.ds(pl.multiple_of(place * run, run), run)],
-                    sems.at[n * len(splits) + o],
+                    sems.at[n * count + o],
                 )
             )
             start += run
@@ -133,6 +143,25 @@
         copy.start()
     for copy in copies:
         copy.wait()
+
+
+def column_kernel(chips, run, idx, *rest):
+    pieces, out = rest[:-1], rest[-1]
+    for hop, piece in enumerate(pieces):
+        place = lax.rem(idx[1] + chips - hop, chips) * run
+        out[pl.ds(pl.multiple_of(place, run), run), :] = piece[...]
+
+
+def prior_weights_kernel(chips, nx, run, idx, *rest):
+    pieces, out = rest[:-1], rest[-1]
+    wide = out.shape[1] // nx
+    for n, piece in enumerate(pieces):
+        at = pl.multiple_of((idx[0] ^ (n // 2)) * wide, wide)
+        for z in range(chips):
+            place = (z * 2 + (idx[2] ^ (n % 2))) * run
+            out[pl.ds(pl.multiple_of(place, run), run), pl.ds(at, wide)] = piece[
+                z * run : (z + 1) * run, :
+            ]
 
 
 def gru_kernel(rows, cap, nx, m, idx, x, act_table, w_s, wd_s, *rest):
@@ -195,25 +224,21 @@
 
 def prior_kernel(nx, m, idx, known, live, wp_s, *rest):
     parts = rest[:nx]
-    _, states, logp, st_s, out_sems = rest[nx:]
+    states, logp, st_s, out_sems = rest[-4:]
     ix, chip = idx[0], idx[1]
     width = parts[0].shape[2]
     count = parts[0].shape[1]
     for k in range(nx):
         at = pl.multiple_of((ix ^ k) * width, width)
-        for step in range(STEPS):
-            st_s[step, :, pl.ds(at, width)] = parts[k][step]
+        st_s[:, :, pl.ds(at, width)] = jnp.transpose(parts[k][...], (1, 0, 2))
     outgo = []
     run = count // nx
-    for step in range(STEPS):
-        for a in range(nx):
-            outgo.append(
-                pltpu.make_async_copy(
-                    st_s.at[step, pl.ds(a * run, run)],
-                    states.at[step, a, chip ^ m],
-                    out_sems.at[step * nx + a],
-                )
+    for a in range(nx):
+        outgo.append(
+            pltpu.make_async_copy(
+                st_s.at[pl.ds(a * run, run)], states.at[a, chip ^ m], out_sems.at[a]
             )
+        )
     for copy in outgo:
         copy.start()
     logits = jnp.zeros((STEPS * count, wp_s.shape[1]), F32)
@@ -300,31 +325,51 @@
 
             return run
 
-        srows, drows = w_stoch.shape[0], w_deter.shape[1]
-        shard = call(
+        srows, drows, prows = w_stoch.shape[0], w_deter.shape[1], w_prior.shape[0]
+        wide = w_prior.shape[1] // nx
+        shard, quarter = call(
             weights_kernel,
-            jax.ShapeDtypeStruct((srows + drows, cols), BF16),
-            [SMEM, ANY, ANY],
-            VMEM,
-            [pltpu.SemaphoreType.DMA((2,))],
-        )(idx, w_stoch, w_deter)
-        stops = [shard]
+            [
+                jax.ShapeDtypeStruct((srows + drows, cols), BF16),
+                jax.ShapeDtypeStruct((prows, wide), BF16),
+            ],
+            [SMEM, HBM, HBM, HBM],
+            [VMEM, VMEM],
+            [pltpu.SemaphoreType.DMA((3,))],
+        )(idx, *(pltpu.with_memory_space_constraint(w, pltpu.HBM) for w in (w_stoch, w_deter, w_prior)))
+        stops, quarters = [shard], [quarter]
         for _ in range(1, chips):
             stops.append(lax.ppermute(stops[-1], "gy", ring))
+            quarters.append(lax.ppermute(quarters[-1], "gy", ring))
         pieces = []
         for piece in stops:
             pieces += [piece, lax.ppermute(piece, "gy", partner)]
-
-        stoch = jnp.pad(replay_stoch, ((0, 0), (0, LANES - replay_stoch.shape[1])))
+        column = call(
+            functools.partial(column_kernel, chips, prows),
+            jax.ShapeDtypeStruct((chips * prows, wide), BF16),
+            [SMEM] + [VMEM] * chips,
+            VMEM,
+        )(idx, *quarters)
+        priors = []
+        for k in range(nx):
+            piece = lax.ppermute(column, "gx", swap_pairs(nx, k)) if k else column
+            priors += [piece, lax.ppermute(piece, "gy", partner)]
+
+        stoch = jnp.transpose(replay_stoch)
         samp = jnp.transpose(samples, (1, 2, 0)).reshape(-1, slots)
+        acts = jnp.transpose(actions)
         *held, known = call(
             functools.partial(pack_kernel, chips, nx, cap),
             [jax.ShapeDtypeStruct((slots // 2, lined), I16)] * (2 * nx)
             + [jax.ShapeDtypeStruct((samp.shape[0] + STEPS, slots), I32)],
             [SMEM] * 3 + [VMEM] * 4,
             [VMEM] * (2 * nx + 1),
-            [pltpu.VMEM((slots, deter), F32), pltpu.VMEM((slots, LANES), I32)],
-        )(idx, send_rows, send_counts, replay_deter, stoch, samp, jnp.transpose(actions))
+            [
+                pltpu.VMEM((slots, deter), F32),
+                pltpu.VMEM((slots, LANES), F32),
+                pltpu.VMEM((slots, replay_deter.shape[0]), F32),
+            ],
+        )(idx, jnp.transpose(send_rows), send_counts, replay_deter, stoch, samp, acts)
         for k in range(nx):
             for l in range(2):
                 if k or l:
@@ -345,16 +390,21 @@
         starts = list(starts)
         for m in range(1, chips):
             starts[m] = lax.ppermute(starts[m], "gy", swap_pairs(ny, 2 * m))
-        w_all, wd_all = call(
-            functools.partial(place_kernel, chips, (srows, drows)),
-            [
-                jax.ShapeDtypeStruct((ny * srows, cols), BF16),
-                jax.ShapeDtypeStruct((ny * drows, cols), BF16),
-            ],
-            [SMEM] + [ANY] * (2 * chips),
-            [VMEM] * 2,
-            [pltpu.SemaphoreType.DMA((4 * chips,))],
-        )(idx, *pieces)
+        placed = []
+        early = 2 * chips - 2
+        for first, some in ((0, pieces[:early]), (early, pieces[early:])):
+            placed = call(
+                functools.partial(place_kernel, chips, (srows, drows), first, len(placed)),
+                [
+                    jax.ShapeDtypeStruct((ny * srows, cols), BF16),
+                    jax.ShapeDtypeStruct((ny * drows, cols), BF16),
+                ],
+                [SMEM] + [ANY] * len(some) + [VMEM] * len(placed),
+                [VMEM] * 2,
+                [pltpu.SemaphoreType.DMA((2 * len(some),))],
+                input_output_aliases={len(some) + 1 + n: n for n in range(len(placed))},
+            )(idx, *some, *placed)
+        w_all, wd_all = placed
 
         parts = []
         for m in range(chips):
@@ -379,39 +429,34 @@
                 got.append(lax.ppermute(outs[k], "gx", swap_pairs(nx, k)))
             parts.append((live, got))
 
-        piece = tied(w_prior, parts[0][0])
-        pieces = []
-        for m in range(chips):
-            pieces += [piece, lax.ppermute(piece, "gy", partner)]
-            if m + 1 < chips:
-                piece = lax.ppermute(piece, "gy", ring)
-        (wp_all,) = call(
-            functools.partial(place_kernel, chips, (w_prior.shape[0],)),
-            [jax.ShapeDtypeStruct((deter, GROUPS * CLASSES), BF16)],
-            [SMEM] + [ANY] * (2 * chips),
-            [VMEM],
-            [pltpu.SemaphoreType.DMA((2 * chips,))],
-        )(idx, *pieces)
-
-        states = jnp.zeros((STEPS, nx, chips, 2 * cap, deter), BF16)
+        wp_all = call(
+            functools.partial(prior_weights_kernel, chips, nx, prows),
+            jax.ShapeDtypeStruct((deter, GROUPS * CLASSES), BF16),
+            [SMEM] + [VMEM] * (2 * nx),
+            VMEM,
+        )(idx, *priors)
+
+        shape = (nx, chips, 2 * cap, STEPS, deter)
+        states = []
         logps = []
         for m in range(chips):
             live, got = parts[m]
-            states, logp = call(
+            filled, logp = call(
                 functools.partial(prior_kernel, nx, m),
                 [
-                    jax.ShapeDtypeStruct(states.shape, BF16),
+                    jax.ShapeDtypeStruct(shape, BF16),
                     jax.ShapeDtypeStruct((GROUPS, STEPS * part), F32),
                 ],
-                [SMEM] + [VMEM] * (3 + nx) + [ANY],
+                [SMEM] + [VMEM] * (3 + nx) + [ANY] * len(states),
                 [ANY, VMEM],
                 [
-                    pltpu.VMEM((STEPS, part, deter), BF16),
-                    pltpu.SemaphoreType.DMA((STEPS * nx,)),
+                    pltpu.VMEM((part, STEPS, deter), BF16),
+                    pltpu.SemaphoreType.DMA((nx,)),
                 ],
                 flops=2 * STEPS * part * deter * GROUPS * CLASSES,
-                input_output_aliases={4 + nx: 0},
-            )(idx, known, live, wp_all, *got, states)
+                input_output_aliases={4 + nx: 0} if states else {},
+            )(idx, known, live, wp_all, *got, *states)
+            states = [filled]
             logps.append(logp)
         logp = call(
             functools.partial(order_kernel, chips, 2 * cap),
@@ -419,8 +464,7 @@
             [SMEM] + [VMEM] * chips,
             VMEM,
         )(idx, *logps)
-        states = jnp.transpose(states.reshape(STEPS, slots, deter), (1, 0, 2))
-        return (states, jnp.transpose(logp, (2, 0, 1)))
+        return (filled.reshape(slots, STEPS, deter), jnp.transpose(logp, (2, 0, 1)))
 
     return on_device
 

time: 232 us -> 187 us (0.81)
  waiting for transfers between devices: 128 us -> 78.5 us
  starting transfers between devices: 34 us -> 46 us
  local copies, waits for them, and re-layouts: 12.3 us -> 3.7 us
    ppermute x3, waiting for transfers between devices: 31.7 us -> 0.01 us  [on_device(): stops.append(lax.ppermute(stops[-1], 'gy', ring))]
    ppermute x3, waiting for transfers between devices: 28 us -> 10.2 us  [on_device(): starts[m] = lax.ppermute(starts[m], 'gy', swap_pairs(ny, 2 * m))]
    ppermute x3 -> x10, waiting for transfers between devices: 28.2 us -> 45.5 us  [the longest x3 23.3 us: on_device(): quarters.append(lax.ppermute(quarters[-1], 'gy', ring))]
    ppermute x12, waiting for transfers between devices: 17 us -> 8.83 us  [on_device(): got.append(lax.ppermute(outs[k], 'gx', swap_pairs(nx, k)))]
    ppermute x7, waiting for transfers between devices: 21.6 us -> 13.9 us  [on_device(): held[n] = lax.ppermute(held[n], ('gx', 'gy'), pairs)]
    ppermute x3 -> x10, starting transfers between devices: 0.06 us -> 5.91 us  [the longest x3 3.53 us: on_device(): piece = lax.ppermute(column, 'gx', swap_pairs(nx, k)) if k else column]
    reshape x1 -> x0, local copies, waits for them, and re-layouts: 5.25 us -> none  [on_device(): states = jnp.transpose(states.reshape(STEPS, slots, deter), (1, 0, 2))]
    unnamed x18 -> x14, local copies, waits for them, and re-layouts: 6.54 us -> 3.7 us
  transfers between devices with their start and end apart: 39 -> 42, of which waited for: 16 -> 13; matrix products, arithmetic and copies ran while one was open for 1% -> 0% of each run, Pallas kernels for 18% -> 27%
where the time goes in v1:
time: 187 us
  waiting for transfers between devices  78.5 us (42%)
  Pallas kernels  57.4 us (31%)
  starting transfers between devices  46 us (25%)
  local copies, waits for them, and re-layouts  3.7 us (2%)
    pallas_call x16, Pallas kernels, run(): pl.pallas_call(kernel, out_shape=out_shape, in_specs=ins, out_specs=outs,...  57.4 us
    ppermute x3, waiting for transfers between devices, on_device(): quarters.append(lax.ppermute(quarters[-1], 'gy', ring))  23.3 us
    ppermute x3, waiting for transfers between devices, on_device(): piece = lax.ppermute(column, 'gx', swap_pairs(nx, k)) if k else column  22.2 us
    ppermute x12, starting transfers between devices, on_device(): got.append(lax.ppermute(outs[k], 'gx', swap_pairs(nx, k)))  15.8 us
    ppermute x7, waiting for transfers between devices, on_device(): held[n] = lax.ppermute(held[n], ('gx', 'gy'), pairs)  13.9 us
    ppermute x7, starting transfers between devices, on_device(): held[n] = lax.ppermute(held[n], ('gx', 'gy'), pairs)  10.6 us
    ppermute x3, waiting for transfers between devices, on_device(): starts[m] = lax.ppermute(starts[m], 'gy', swap_pairs(ny, 2 * m))  10.2 us
    ppermute x12, waiting for transfers between devices, on_device(): got.append(lax.ppermute(outs[k], 'gx', swap_pairs(nx, k)))  8.83 us
  transfers between devices with their start and end apart: 42, of which 13 were waited for; matrix products, arithmetic and copies ran while one was open for 0% of the time, Pallas kernels for 27%

profile of v1, /device:TPU:0, one launch (start us, length us, event | category | flops | bytes accessed | tf_op | source)
XLA Modules:
  0.0 186.6 jit_solution(18100063148761831384)
XLA Ops:
  0.7 1.7 shard_map.115
  2.4 3.1 %collective-permute-start.8 = (bf16[192,1536]{1,0:T(8,128)(2,1)S(1)}, bf16[192,1536]{1,0:T(8,128)(2,1)S(1)}, u32[]{:S(2)}, u32[]{:S(2)}) collective-permute-start(bf16[192,1536]{1,0:T(8,128)(2,1)S(1)} %get-tuple-element.59.rest_0_), channel_id=1, source_target_pairs={{0,2},{1,3},{2,4},{3,5},{4,6},{5,7},{6,0},{7,1},{8,10},{9,11},{10,... | collective-permute-start | bytes 1769480 | tf_op jit(solution)/shard_map/ppermute | solution.py:342
  5.5 1.6 collective-permute-start.18
  7.1 16.6 %collective-permute-done.18.rest_1_ = bf16[256,256]{1,0:T(8,128)(2,1)S(1)} collective-permute-done((bf16[256,256]{1,0:T(8,128)(2,1)S(1)}, bf16[256,256]{1,0:T(8,128)(2,1)S(1)}, u32[]{:S(2)}, u32[]{:S(2)}) %collective-permute-start.18) | collective-permute-done | bytes 131104 | tf_op jit(solution)/shard_map/ppermute | solution.py:343
  23.7 6.8 %collective-permute-done.19.rest_2_ = bf16[256,256]{1,0:T(8,128)(2,1)S(1)} collective-permute-done((bf16[256,256]{1,0:T(8,128)(2,1)S(1)}, bf16[256,256]{1,0:T(8,128)(2,1)S(1)}, u32[]{:S(2)}, u32[]{:S(2)}) %collective-permute-start.19) | collective-permute-done | bytes 131104 | tf_op jit(solution)/shard_map/ppermute | solution.py:343
  34.2 3.3 %shard_map.113 = (s16[128,640]{1,0:T(8,128)(2,1)S(1)}, s16[128,640]{1,0:T(8,128)(2,1)S(1)}, s16[128,640]{1,0:T(8,128)(2,1)S(1)}, s16[128,640]{1,0:T(8,128)(2,1)S...) custom-call(s32[3]{0:T(128)S(1)} %pad_add_fusion.idx, ...), custom_call_target="tpu_custom_call" | custom-call | bytes 1048576 | tf_op jit(solution)/shard_map/pallas_call | solution.py:313
  37.6 1.6 collective-permute-start.1
  40.7 4.0 %collective-permute-done.1.rest_2_ = s16[128,640]{1,0:T(8,128)(2,1)S(1)} collective-permute-done((s16[128,640]{1,0:T(8,128)(2,1)S(1)}, s16[128,640]{1,0:T(8,128)(2,1)S(1)}, u32[]{:S(2)}, u32[]{:S(2)}) %collective-permute-start.1) | collective-permute-done | bytes 163872 | tf_op jit(solution)/shard_map/ppermute | solution.py:380
  44.7 1.5 collective-permute-start.3
  46.2 0.9 collective-permute-done.2.rest_3_
  47.1 1.8 collective-permute-start.4
  48.9 1.1 collective-permute-done.3.rest_4_
  50.0 2.4 %collective-permute-start.5 = (s16[128,640]{1,0:T(8,128)(2,1)S(1)}, s16[128,640]{1,0:T(8,128)(2,1)S(1)}, u32[]{:S(2)}, u32[]{:S(2)}) collective-permute-start(s16[128,640]{1,0:T(8,128)(2,1)S(1)} %get-tuple-element.56), channel_id=1, source_target_pairs={{0,24},{1,25},{2,26},{3,27},{4,28},{5,29},{6,30},{7,31},{8,16},{9,... | collective-permute-start | bytes 491528 | tf_op jit(solution)/shard_map/ppermute | solution.py:380
  52.5 3.9 %collective-permute-done.4.rest_5_ = s16[128,640]{1,0:T(8,128)(2,1)S(1)} collective-permute-done((s16[128,640]{1,0:T(8,128)(2,1)S(1)}, s16[128,640]{1,0:T(8,128)(2,1)S(1)}, u32[]{:S(2)}, u32[]{:S(2)}) %collective-permute-start.4) | collective-permute-done | bytes 163872 | tf_op jit(solution)/shard_map/ppermute | solution.py:380
  56.4 2.6 %collective-permute-start.6 = (s16[128,640]{1,0:T(8,128)(2,1)S(1)}, s16[128,640]{1,0:T(8,128)(2,1)S(1)}, u32[]{:S(2)}, u32[]{:S(2)}) collective-permute-start(s16[128,640]{1,0:T(8,128)(2,1)S(1)} %get-tuple-element.57), channel_id=1, source_target_pairs={{0,25},{1,24},{2,27},{3,26},{4,29},{5,28},{6,31},{7,30},{8,17},{9,... | collective-permute-start | bytes 491528 | tf_op jit(solution)/shard_map/ppermute | solution.py:380
  59.7 4.0 %collective-permute-done.6.rest_7_ = s16[128,640]{1,0:T(8,128)(2,1)S(1)} collective-permute-done((s16[128,640]{1,0:T(8,128)(2,1)S(1)}, s16[128,640]{1,0:T(8,128)(2,1)S(1)}, u32[]{:S(2)}, u32[]{:S(2)}) %collective-permute-start.6) | collective-permute-done | bytes 163872 | tf_op jit(solution)/shard_map/ppermute | solution.py:380
  64.5 1.5 collective-permute-start.24
  66.0 1.4 collective-permute-start.26
  67.4 8.6 %collective-permute-done.22.rest_2_ = bf16[1024,256]{1,0:T(8,128)(2,1)S(1)} collective-permute-done((bf16[1024,256]{1,0:T(8,128)(2,1)S(1)}, bf16[1024,256]{1,0:T(8,128)(2,1)S(1)}, u32[]{:S(2)}, u32[]{:S(2)}) %collective-permute-start.22) | collective-permute-done | bytes 524320 | tf_op jit(solution)/shard_map/ppermute | solution.py:355
  75.9 13.6 %collective-permute-done.24.rest_4_ = bf16[1024,256]{1,0:T(8,128)(2,1)S(1)} collective-permute-done((bf16[1024,256]{1,0:T(8,128)(2,1)S(1)}, bf16[1024,256]{1,0:T(8,128)(2,1)S(1)}, u32[]{:S(2)}, u32[]{:S(2)}) %collective-permute-start.24) | collective-permute-done | bytes 524320 | tf_op jit(solution)/shard_map/ppermute | solution.py:355
  90.7 2.7 %collective-permute-start.31 = (s16[8,32,640]{2,1,0:T(8,128)(2,1)S(1)}, s16[8,32,640]{2,1,0:T(8,128)(2,1)S(1)}, u32[]{:S(2)}, u32[]{:S(2)}) collective-permute-start(s16[8,32,640]{2,1,0:T(8,128)(2,1)S(1)} %get-tuple-element.70), channel_id=1, source_target_pairs={{0,4},{1,5},{2,6},{3,7},{4,0},{5,1},{6,2},{7,3},{8,12},{9,13},{10,... | collective-permute-start | bytes 983048 | tf_op jit(solution)/shard_map/ppermute | solution.py:392
  94.0 1.5 collective-permute-start.16
  95.5 1.4 collective-permute-start.17
  96.9 1.1 shard_map.120.wp_s
  98.1 3.3 %shard_map.116 = (bf16[1024,1536]{1,0:T(8,128)(2,1)S(1)}, bf16[512,1536]{1,0:T(8,128)(2,1)S(1)}) custom-call(s32[3]{0:T(128)S(1)} %pad_add_fusion.idx, bf16[192,1536]{1,0:T(8,128)(2,1)S(1)} %get-tuple-element.59.rest_0_, bf16[192,1536]{1,0:T(8,128)(2,1)S(1)} %collective-permute-done.12.rest_1_, bf16[192,1536]{1,0:T(8,128)(2,1)S(1)} %collective-permute-done.8.rest_2_, ...), custom_call_target="tpu_custom_call" | custom-call | bytes 1048576 | tf_op jit(solution)/shard_map/pallas_call | solution.py:313
  101.4 2.9 %collective-permute-start.7 = (s16[8,32,640]{2,1,0:T(8,128)(2,1)S(1)}, s16[8,32,640]{2,1,0:T(8,128)(2,1)S(1)}, u32[]{:S(2)}, u32[]{:S(2)}) collective-permute-start(s16[8,32,640]{2,1,0:T(8,128)(2,1)S(1)} %get-tuple-element.58), channel_id=1, source_target_pairs={{0,6},{1,7},{2,4},{3,5},{4,2},{5,3},{6,0},{7,1},{8,14},{9,15},{10,... | collective-permute-start | bytes 983048 | tf_op jit(solution)/shard_map/ppermute | solution.py:392
  104.3 1.7 shard_map.117
  106.1 10.2 %collective-permute-done.31.x = s16[8,32,640]{2,1,0:T(8,128)(2,1)S(1)} collective-permute-done((s16[8,32,640]{2,1,0:T(8,128)(2,1)S(1)}, s16[8,32,640]{2,1,0:T(8,128)(2,1)S(1)}, u32[]{:S(2)}, u32[]{:S(2)}) %collective-permute-start.31) | collective-permute-done | bytes 327712 | tf_op jit(solution)/shard_map/ppermute | solution.py:392
  116.3 7.6 %shard_map.121 = (bf16[4,64,512]{2,1,0:T(8,128)(2,1)S(1)}, bf16[4,64,512]{2,1,0:T(8,128)(2,1)S(1)}, bf16[4,64,512]{2,1,0:T(8,128)(2,1)S(1)}, bf16[4,64,512]{2,1,0:T(8,128)(2,1)S(1)}, f32[8,64]{1,0:T(8,128)S(1)}) custom-call(s32[3]{0:T(128)S(1)} %pad_add_fusion.idx, s16[8,32,640]{2,1,0:T(8,128)(2,1)S(1)} %collective-permute-done.31.x, ...), custom_call_target="tpu_custom_call" | custom-call | flops 4831838208 | bytes 1048576 | tf_op jit(solution)/shard_map/pallas_call | solution.py:313
  123.9 1.5 collective-permute-start.32
  125.4 7.6 %shard_map.122 = (bf16[4,64,512]{2,1,0:T(8,128)(2,1)S(1)}, bf16[4,64,512]{2,1,0:T(8,128)(2,1)S(1)}, bf16[4,64,512]{2,1,0:T(8,128)(2,1)S(1)}, bf16[4,64,512]{2,1,0:T(8,128)(2,1)S(1)}, f32[8,64]{1,0:T(8,128)S(1)}) custom-call(s32[3]{0:T(128)S(1)} %pad_add_fusion.idx, s16[8,32,640]{2,1,0:T(8,128)(2,1)S(1)} %collective-permute-done.35.x, ...), custom_call_target="tpu_custom_call" | custom-call | flops 4831838208 | bytes 1048576 | tf_op jit(solution)/shard_map/pallas_call | solution.py:313
  133.6 1.5 collective-permute-start.37
  135.1 1.4 collective-permute-start.38
  136.5 7.8 %shard_map.123 = (bf16[4,64,512]{2,1,0:T(8,128)(2,1)S(1)}, bf16[4,64,512]{2,1,0:T(8,128)(2,1)S(1)}, bf16[4,64,512]{2,1,0:T(8,128)(2,1)S(1)}, bf16[4,64,512]{2,1,0:T(8,128)(2,1)S(1)}, f32[8,64]{1,0:T(8,128)S(1)}) custom-call(s32[3]{0:T(128)S(1)} %pad_add_fusion.idx, s16[8,32,640]{2,1,0:T(8,128)(2,1)S(1)} %get-tuple-element.82.x, ...), custom_call_target="tpu_custom_call" | custom-call | flops 4831838208 | bytes 1048576 | tf_op jit(solution)/shard_map/pallas_call | solution.py:313
  144.3 1.5 collective-permute-start.33
  146.4 1.4 collective-permute-start.39
  147.8 2.2 %collective-permute-start.40 = (bf16[4,64,512]{2,1,0:T(8,128)(2,1)S(1)}, bf16[4,64,512]{2,1,0:T(8,128)(2,1)S(1)}, u32[]{:S(2)}, u32[]{:S(2)}) collective-permute-start(bf16[4,64,512]{2,1,0:T(8,128)(2,1)S(1)} %get-tuple-element.86), channel_id=1, source_target_pairs={{0,16},{8,24},{16,0},{24,8},{1,17},{9,25},{17,1},{25,9},{2,18},{10... | collective-permute-start | bytes 786440 | tf_op jit(solution)/shard_map/ppermute | solution.py:429
  150.0 2.0 %collective-permute-start.41 = (bf16[4,64,512]{2,1,0:T(8,128)(2,1)S(1)}, bf16[4,64,512]{2,1,0:T(8,128)(2,1)S(1)}, u32[]{:S(2)}, u32[]{:S(2)}) collective-permute-start(bf16[4,64,512]{2,1,0:T(8,128)(2,1)S(1)} %get-tuple-element.87), channel_id=1, source_target_pairs={{0,24},{8,16},{16,8},{24,0},{1,25},{9,17},{17,9},{25,1},{2,26},{10... | collective-permute-start | bytes 786440 | tf_op jit(solution)/shard_map/ppermute | solution.py:429
  152.0 7.6 %shard_map.118 = (bf16[4,64,512]{2,1,0:T(8,128)(2,1)S(1)}, bf16[4,64,512]{2,1,0:T(8,128)(2,1)S(1)}, bf16[4,64,512]{2,1,0:T(8,128)(2,1)S(1)}, bf16[4,64,512]{2,1,0:T(8,128)(2,1)S(1)}, f32[8,64]{1,0:T(8,128)S(1)}) custom-call(s32[3]{0:T(128)S(1)} %pad_add_fusion.idx, s16[8,32,640]{2,1,0:T(8,128)(2,1)S(1)} %collective-permute-done.7.x, ...), custom_call_target="tpu_custom_call" | custom-call | flops 4831838208 | bytes 1048576 | tf_op jit(solution)/shard_map/pallas_call | solution.py:313
  159.6 1.1 collective-permute-done.39.rest_1_
  161.3 7.0 %collective-permute-done.40.rest_2_ = bf16[4,64,512]{2,1,0:T(8,128)(2,1)S(1)} collective-permute-done((bf16[4,64,512]{2,1,0:T(8,128)(2,1)S(1)}, bf16[4,64,512]{2,1,0:T(8,128)(2,1)S(1)}, u32[]{:S(2)}, u32[]{:S(2)}) %collective-permute-start.40) | collective-permute-done | bytes 262176 | tf_op jit(solution)/shard_map/ppermute | solution.py:429
  168.3 1.0 collective-permute-start.29
  169.3 1.4 collective-permute-start.30
  170.7 3.3 %shard_map.124 = (bf16[4,4,16,4,2048]{4,3,2,1,0:T(4,128)(2,1)}, f32[32,256]{1,0:T(8,128)S(1)}) custom-call(s32[3]{0:T(128)S(1)} %pad_add_fusion.idx, s32[132,256]{1,0:T(8,128)S(1)} %get-tuple-element.49.rest_0_.known, f32[8,64]{1,0:T(8,128)S(1)} %get-tuple-element.83.live, bf16[2048,1024]{1,0:T(8,128)(2,1)S(1)} %shard_map.120.wp_s, ...), custom_call_target="tpu_custom_call" | custom-call | flops 1073741824 | bytes 1048576 | tf_op jit(solution)/shard_map/pallas_call | solution.py:313
  174.0 3.6 %shard_map.125 = (bf16[4,4,16,4,2048]{4,3,2,1,0:T(4,128)(2,1)}, f32[32,256]{1,0:T(8,128)S(1)}) custom-call(s32[3]{0:T(128)S(1)} %pad_add_fusion.idx, s32[132,256]{1,0:T(8,128)S(1)} %get-tuple-element.49.rest_0_.known, f32[8,64]{1,0:T(8,128)S(1)} %get-tuple-element.77.live, bf16[2048,1024]{1,0:T(8,128)(2,1)S(1)} %shard_map.120.wp_s, ...), custom_call_target="tpu_custom_call", output_to_operand_aliasing={{0}: (8, {})} | custom-call | flops 1073741824 | bytes 1048576 | tf_op jit(solution)/shard_map/pallas_call | solution.py:313
  177.6 3.3 %shard_map.126 = (bf16[4,4,16,4,2048]{4,3,2,1,0:T(4,128)(2,1)}, f32[32,256]{1,0:T(8,128)S(1)}) custom-call(s32[3]{0:T(128)S(1)} %pad_add_fusion.idx, s32[132,256]{1,0:T(8,128)S(1)} %get-tuple-element.49.rest_0_.known, f32[8,64]{1,0:T(8,128)S(1)} %get-tuple-element.71.live, bf16[2048,1024]{1,0:T(8,128)(2,1)S(1)} %shard_map.120.wp_s, ...), custom_call_target="tpu_custom_call", output_to_operand_aliasing={{0}: (8, {})} | custom-call | flops 1073741824 | bytes 1048576 | tf_op jit(solution)/shard_map/pallas_call | solution.py:313
  181.7 3.3 %shard_map.127 = (bf16[4,4,16,4,2048]{4,3,2,1,0:T(4,128)(2,1)}, f32[32,256]{1,0:T(8,128)S(1)}) custom-call(s32[3]{0:T(128)S(1)} %pad_add_fusion.idx, s32[132,256]{1,0:T(8,128)S(1)} %get-tuple-element.49.rest_0_.known, f32[8,64]{1,0:T(8,128)S(1)} %get-tuple-element.64.live, bf16[2048,1024]{1,0:T(8,128)(2,1)S(1)} %shard_map.120.wp_s, ...), custom_call_target="tpu_custom_call", output_to_operand_aliasing={{0}: (8, {})} | custom-call | flops 1073741824 | bytes 1048576 | tf_op jit(solution)/shard_map/pallas_call | solution.py:313
  185.0 1.6 shard_map.128
  (67 shorter events, 11.2 us)
Async XLA Ops:
  0.6 29.8 %copy-start = (f32[256,2048]{1,0:T(8,128)S(1)}, f32[256,2048]{1,0:T(8,128)}, u32[]{:S(2)}) copy-start(f32[256,2048]{1,0:T(8,128)} %deter.1) | copy-start | bytes 6291460
  2.4 36.9 %collective-permute-start.8 = (bf16[192,1536]{1,0:T(8,128)(2,1)S(1)}, bf16[192,1536]{1,0:T(8,128)(2,1)S(1)}, u32[]{:S(2)}, u32[]{:S(2)}) collective-permute-start(bf16[192,1536]{1,0:T(8,128)(2,1)S(1)} %get-tuple-element.59.rest_0_), channel_id=1, source_target_pairs={{0,2},{1,3},{2,4},{3,5},{4,6},{5,7},{6,0},{7,1},{8,10},{9,11},{10,... | collective-permute-start | bytes 1769480 | tf_op jit(solution)/shard_map/ppermute | solution.py:342
  5.5 18.2 %collective-permute-start.18 = (bf16[256,256]{1,0:T(8,128)(2,1)S(1)}, bf16[256,256]{1,0:T(8,128)(2,1)S(1)}, u32[]{:S(2)}, u32[]{:S(2)}) collective-permute-start(bf16[256,256]{1,0:T(8,128)(2,1)S(1)} %get-tuple-element.65.rest_0_), channel_id=1, source_target_pairs={{0,2},{1,3},{2,4},{3,5},{4,6},{5,7},{6,0},{7,1},{8,10},{9,11},{10,... | collective-permute-start | bytes 393224 | tf_op jit(solution)/shard_map/ppermute | solution.py:343
  23.7 6.8 %collective-permute-start.19 = (bf16[256,256]{1,0:T(8,128)(2,1)S(1)}, bf16[256,256]{1,0:T(8,128)(2,1)S(1)}, u32[]{:S(2)}, u32[]{:S(2)}) collective-permute-start(bf16[256,256]{1,0:T(8,128)(2,1)S(1)} %collective-permute-done.18.rest_1_), channel_id=1, source_target_pairs={{0,2},{1,3},{2,4},{3,5},{4,6},{5,7},{6,0},{7,1},{8,10},{9,11},{10,... | collective-permute-start | bytes 393224 | tf_op jit(solution)/shard_map/ppermute | solution.py:343
  30.5 8.8 %collective-permute-start.20 = (bf16[256,256]{1,0:T(8,128)(2,1)S(1)}, bf16[256,256]{1,0:T(8,128)(2,1)S(1)}, u32[]{:S(2)}, u32[]{:S(2)}) collective-permute-start(bf16[256,256]{1,0:T(8,128)(2,1)S(1)} %collective-permute-done.19.rest_2_), channel_id=1, source_target_pairs={{0,2},{1,3},{2,4},{3,5},{4,6},{5,7},{6,0},{7,1},{8,10},{9,11},{10,... | collective-permute-start | bytes 393224 | tf_op jit(solution)/shard_map/ppermute | solution.py:343
  30.5 0.9 copy-start.1
  31.4 0.8 copy-start.2
  32.1 0.7 copy-start.3
  32.8 0.7 copy-start.4
  37.5 3.0 %collective-permute-start = (s16[128,640]{1,0:T(8,128)(2,1)S(1)}, s16[128,640]{1,0:T(8,128)(2,1)S(1)}, u32[]{:S(2)}, u32[]{:S(2)}) collective-permute-start(s16[128,640]{1,0:T(8,128)(2,1)S(1)} %get-tuple-element.51), channel_id=1, source_target_pairs={{0,1},{1,0},{2,3},{3,2},{4,5},{5,4},{6,7},{7,6},{8,9},{9,8},{10,11... | collective-permute-start | bytes 491528 | tf_op jit(solution)/shard_map/ppermute | solution.py:380
  37.6 7.1 %collective-permute-start.1 = (s16[128,640]{1,0:T(8,128)(2,1)S(1)}, s16[128,640]{1,0:T(8,128)(2,1)S(1)}, u32[]{:S(2)}, u32[]{:S(2)}) collective-permute-start(s16[128,640]{1,0:T(8,128)(2,1)S(1)} %get-tuple-element.52), channel_id=1, source_target_pairs={{0,8},{1,9},{2,10},{3,11},{4,12},{5,13},{6,14},{7,15},{8,0},{9,1},... | collective-permute-start | bytes 491528 | tf_op jit(solution)/shard_map/ppermute | solution.py:380
  39.1 25.3 %collective-permute-start.12 = (bf16[192,1536]{1,0:T(8,128)(2,1)S(1)}, bf16[192,1536]{1,0:T(8,128)(2,1)S(1)}, u32[]{:S(2)}, u32[]{:S(2)}) collective-permute-start(bf16[192,1536]{1,0:T(8,128)(2,1)S(1)} %get-tuple-element.59.rest_0_), channel_id=1, source_target_pairs={{0,1},{1,0},{2,3},{3,2},{4,5},{5,4},{6,7},{7,6},{8,9},{9,8},{10,11... | collective-permute-start | bytes 1769480 | tf_op jit(solution)/shard_map/ppermute | solution.py:346
  39.3 28.1 %collective-permute-start.9 = (bf16[192,1536]{1,0:T(8,128)(2,1)S(1)}, bf16[192,1536]{1,0:T(8,128)(2,1)S(1)}, u32[]{:S(2)}, u32[]{:S(2)}) collective-permute-start(bf16[192,1536]{1,0:T(8,128)(2,1)S(1)} %collective-permute-done.8.rest_2_), channel_id=1, source_target_pairs={{0,2},{1,3},{2,4},{3,5},{4,6},{5,7},{6,0},{7,1},{8,10},{9,11},{10,... | collective-permute-start | bytes 1769480 | tf_op jit(solution)/shard_map/ppermute | solution.py:342
  39.3 7.8 %collective-permute-start.2 = (s16[128,640]{1,0:T(8,128)(2,1)S(1)}, s16[128,640]{1,0:T(8,128)(2,1)S(1)}, u32[]{:S(2)}, u32[]{:S(2)}) collective-permute-start(s16[128,640]{1,0:T(8,128)(2,1)S(1)} %get-tuple-element.53), channel_id=1, source_target_pairs={{0,9},{1,8},{2,11},{3,10},{4,13},{5,12},{6,15},{7,14},{8,1},{9,0},... | collective-permute-start | bytes 491528 | tf_op jit(solution)/shard_map/ppermute | solution.py:380
  40.5 25.5 %collective-permute-start.21 = (bf16[1024,256]{1,0:T(8,128)(2,1)S(1)}, bf16[1024,256]{1,0:T(8,128)(2,1)S(1)}, u32[]{:S(2)}, u32[]{:S(2)}) collective-permute-start(bf16[1024,256]{1,0:T(8,128)(2,1)S(1)} %shard_map.119.rest_0_), channel_id=1, source_target_pairs={{0,1},{1,0},{2,3},{3,2},{4,5},{5,4},{6,7},{7,6},{8,9},{9,8},{10,11... | collective-permute-start | bytes 1572872 | tf_op jit(solution)/shard_map/ppermute | solution.py:356
  44.7 5.3 %collective-permute-start.3 = (s16[128,640]{1,0:T(8,128)(2,1)S(1)}, s16[128,640]{1,0:T(8,128)(2,1)S(1)}, u32[]{:S(2)}, u32[]{:S(2)}) collective-permute-start(s16[128,640]{1,0:T(8,128)(2,1)S(1)} %get-tuple-element.54), channel_id=1, source_target_pairs={{0,16},{1,17},{2,18},{3,19},{4,20},{5,21},{6,22},{7,23},{8,24},{9,... | collective-permute-start | bytes 491528 | tf_op jit(solution)/shard_map/ppermute | solution.py:380
  47.1 9.2 %collective-permute-start.4 = (s16[128,640]{1,0:T(8,128)(2,1)S(1)}, s16[128,640]{1,0:T(8,128)(2,1)S(1)}, u32[]{:S(2)}, u32[]{:S(2)}) collective-permute-start(s16[128,640]{1,0:T(8,128)(2,1)S(1)} %get-tuple-element.55), channel_id=1, source_target_pairs={{0,17},{1,16},{2,19},{3,18},{4,21},{5,20},{6,23},{7,22},{8,25},{9,... | collective-permute-start | bytes 491528 | tf_op jit(solution)/shard_map/ppermute | solution.py:380
  50.0 9.0 %collective-permute-start.5 = (s16[128,640]{1,0:T(8,128)(2,1)S(1)}, s16[128,640]{1,0:T(8,128)(2,1)S(1)}, u32[]{:S(2)}, u32[]{:S(2)}) collective-permute-start(s16[128,640]{1,0:T(8,128)(2,1)S(1)} %get-tuple-element.56), channel_id=1, source_target_pairs={{0,24},{1,25},{2,26},{3,27},{4,28},{5,29},{6,30},{7,31},{8,16},{9,... | collective-permute-start | bytes 491528 | tf_op jit(solution)/shard_map/ppermute | solution.py:380
  56.4 7.2 %collective-permute-start.6 = (s16[128,640]{1,0:T(8,128)(2,1)S(1)}, s16[128,640]{1,0:T(8,128)(2,1)S(1)}, u32[]{:S(2)}, u32[]{:S(2)}) collective-permute-start(s16[128,640]{1,0:T(8,128)(2,1)S(1)} %get-tuple-element.57), channel_id=1, source_target_pairs={{0,25},{1,24},{2,27},{3,26},{4,29},{5,28},{6,31},{7,30},{8,17},{9,... | collective-permute-start | bytes 491528 | tf_op jit(solution)/shard_map/ppermute | solution.py:380
  59.0 16.9 %collective-permute-start.22 = (bf16[1024,256]{1,0:T(8,128)(2,1)S(1)}, bf16[1024,256]{1,0:T(8,128)(2,1)S(1)}, u32[]{:S(2)}, u32[]{:S(2)}) collective-permute-start(bf16[1024,256]{1,0:T(8,128)(2,1)S(1)} %shard_map.119.rest_0_), channel_id=1, source_target_pairs={{0,8},{8,0},{16,24},{24,16},{1,9},{9,1},{17,25},{25,17},{2,10},{10... | collective-permute-start | bytes 1572872 | tf_op jit(solution)/shard_map/ppermute | solution.py:355
  63.6 26.4 %collective-permute-start.13 = (bf16[192,1536]{1,0:T(8,128)(2,1)S(1)}, bf16[192,1536]{1,0:T(8,128)(2,1)S(1)}, u32[]{:S(2)}, u32[]{:S(2)}) collective-permute-start(bf16[192,1536]{1,0:T(8,128)(2,1)S(1)} %collective-permute-done.8.rest_2_), channel_id=1, source_target_pairs={{0,1},{1,0},{2,3},{3,2},{4,5},{5,4},{6,7},{7,6},{8,9},{9,8},{10,11... | collective-permute-start | bytes 1769480 | tf_op jit(solution)/shard_map/ppermute | solution.py:346
  64.5 25.1 %collective-permute-start.24 = (bf16[1024,256]{1,0:T(8,128)(2,1)S(1)}, bf16[1024,256]{1,0:T(8,128)(2,1)S(1)}, u32[]{:S(2)}, u32[]{:S(2)}) collective-permute-start(bf16[1024,256]{1,0:T(8,128)(2,1)S(1)} %shard_map.119.rest_0_), channel_id=1, source_target_pairs={{0,16},{8,24},{16,0},{24,8},{1,17},{9,25},{17,1},{25,9},{2,18},{10... | collective-permute-start | bytes 1572872 | tf_op jit(solution)/shard_map/ppermute | solution.py:355
  66.0 23.6 %collective-permute-start.26 = (bf16[1024,256]{1,0:T(8,128)(2,1)S(1)}, bf16[1024,256]{1,0:T(8,128)(2,1)S(1)}, u32[]{:S(2)}, u32[]{:S(2)}) collective-permute-start(bf16[1024,256]{1,0:T(8,128)(2,1)S(1)} %shard_map.119.rest_0_), channel_id=1, source_target_pairs={{0,24},{8,16},{16,8},{24,0},{1,25},{9,17},{17,9},{25,1},{2,26},{10... | collective-permute-start | bytes 1572872 | tf_op jit(solution)/shard_map/ppermute | solution.py:355
  67.4 22.8 %collective-permute-start.10 = (bf16[192,1536]{1,0:T(8,128)(2,1)S(1)}, bf16[192,1536]{1,0:T(8,128)(2,1)S(1)}, u32[]{:S(2)}, u32[]{:S(2)}) collective-permute-start(bf16[192,1536]{1,0:T(8,128)(2,1)S(1)} %collective-permute-done.9.rest_4_), channel_id=1, source_target_pairs={{0,2},{1,3},{2,4},{3,5},{4,6},{5,7},{6,0},{7,1},{8,10},{9,11},{10,... | collective-permute-start | bytes 1769480 | tf_op jit(solution)/shard_map/ppermute | solution.py:342
  75.9 14.7 %collective-permute-start.23 = (bf16[1024,256]{1,0:T(8,128)(2,1)S(1)}, bf16[1024,256]{1,0:T(8,128)(2,1)S(1)}, u32[]{:S(2)}, u32[]{:S(2)}) collective-permute-start(bf16[1024,256]{1,0:T(8,128)(2,1)S(1)} %collective-permute-done.22.rest_2_), channel_id=1, source_target_pairs={{0,1},{1,0},{2,3},{3,2},{4,5},{5,4},{6,7},{7,6},{8,9},{9,8},{10,11... | collective-permute-start | bytes 1572872 | tf_op jit(solution)/shard_map/ppermute | solution.py:356
  89.5 6.0 %collective-permute-start.14 = (bf16[192,1536]{1,0:T(8,128)(2,1)S(1)}, bf16[192,1536]{1,0:T(8,128)(2,1)S(1)}, u32[]{:S(2)}, u32[]{:S(2)}) collective-permute-start(bf16[192,1536]{1,0:T(8,128)(2,1)S(1)} %collective-permute-done.9.rest_4_), channel_id=1, source_target_pairs={{0,1},{1,0},{2,3},{3,2},{4,5},{5,4},{6,7},{7,6},{8,9},{9,8},{10,11... | collective-permute-start | bytes 1769480 | tf_op jit(solution)/shard_map/ppermute | solution.py:346
  89.5 3.9 %collective-permute-start.25 = (bf16[1024,256]{1,0:T(8,128)(2,1)S(1)}, bf16[1024,256]{1,0:T(8,128)(2,1)S(1)}, u32[]{:S(2)}, u32[]{:S(2)}) collective-permute-start(bf16[1024,256]{1,0:T(8,128)(2,1)S(1)} %collective-permute-done.24.rest_4_), channel_id=1, source_target_pairs={{0,1},{1,0},{2,3},{3,2},{4,5},{5,4},{6,7},{7,6},{8,9},{9,8},{10,11... | collective-permute-start | bytes 1572872 | tf_op jit(solution)/shard_map/ppermute | solution.py:356
  90.1 3.9 %collective-permute-start.27 = (bf16[1024,256]{1,0:T(8,128)(2,1)S(1)}, bf16[1024,256]{1,0:T(8,128)(2,1)S(1)}, u32[]{:S(2)}, u32[]{:S(2)}) collective-permute-start(bf16[1024,256]{1,0:T(8,128)(2,1)S(1)} %collective-permute-done.26.rest_6_), channel_id=1, source_target_pairs={{0,1},{1,0},{2,3},{3,2},{4,5},{5,4},{6,7},{7,6},{8,9},{9,8},{10,11... | collective-permute-start | bytes 1572872 | tf_op jit(solution)/shard_map/ppermute | solution.py:356
  90.1 11.3 %collective-permute-start.11 = (bf16[192,1536]{1,0:T(8,128)(2,1)S(1)}, bf16[192,1536]{1,0:T(8,128)(2,1)S(1)}, u32[]{:S(2)}, u32[]{:S(2)}) collective-permute-start(bf16[192,1536]{1,0:T(8,128)(2,1)S(1)} %collective-permute-done.10.rest_0_), channel_id=1, source_target_pairs={{0,1},{1,0},{2,3},{3,2},{4,5},{5,4},{6,7},{7,6},{8,9},{9,8},{10,11... | collective-permute-start | bytes 1769480 | tf_op jit(solution)/shard_map/ppermute | solution.py:346
  90.7 25.6 %collective-permute-start.31 = (s16[8,32,640]{2,1,0:T(8,128)(2,1)S(1)}, s16[8,32,640]{2,1,0:T(8,128)(2,1)S(1)}, u32[]{:S(2)}, u32[]{:S(2)}) collective-permute-start(s16[8,32,640]{2,1,0:T(8,128)(2,1)S(1)} %get-tuple-element.70), channel_id=1, source_target_pairs={{0,4},{1,5},{2,6},{3,7},{4,0},{5,1},{6,2},{7,3},{8,12},{9,13},{10,... | collective-permute-start | bytes 983048 | tf_op jit(solution)/shard_map/ppermute | solution.py:392
  93.4 12.6 %collective-permute-start.15 = (s32[132,256]{1,0:T(8,128)S(1)}, s32[132,256]{1,0:T(8,128)S(1)}, u32[]{:S(2)}, u32[]{:S(2)}) collective-permute-start(s32[132,256]{1,0:T(8,128)S(1)} %get-tuple-element.49.rest_0_.known), channel_id=1, source_target_pairs={{0,8},{8,0},{16,24},{24,16},{1,9},{9,1},{17,25},{25,17},{2,10},{10... | collective-permute-start | bytes 405512 | tf_op jit(solution)/shard_map/ppermute | solution.py:383
  94.0 12.1 %collective-permute-start.16 = (s32[132,256]{1,0:T(8,128)S(1)}, s32[132,256]{1,0:T(8,128)S(1)}, u32[]{:S(2)}, u32[]{:S(2)}) collective-permute-start(s32[132,256]{1,0:T(8,128)S(1)} %get-tuple-element.49.rest_0_.known), channel_id=1, source_target_pairs={{0,16},{8,24},{16,0},{24,8},{1,17},{9,25},{17,1},{25,9},{2,18},{10... | collective-permute-start | bytes 405512 | tf_op jit(solution)/shard_map/ppermute | solution.py:383
  95.5 10.6 %collective-permute-start.17 = (s32[132,256]{1,0:T(8,128)S(1)}, s32[132,256]{1,0:T(8,128)S(1)}, u32[]{:S(2)}, u32[]{:S(2)}) collective-permute-start(s32[132,256]{1,0:T(8,128)S(1)} %get-tuple-element.49.rest_0_.known), channel_id=1, source_target_pairs={{0,24},{8,16},{16,8},{24,0},{1,25},{9,17},{17,9},{25,1},{2,26},{10... | collective-permute-start | bytes 405512 | tf_op jit(solution)/shard_map/ppermute | solution.py:383
  101.4 14.9 %copy-start.6 = (bf16[18,6144]{1,0:T(8,128)(2,1)S(1)}, bf16[18,6144]{1,0:T(8,128)(2,1)}, u32[]{:S(2)}) copy-start(bf16[18,6144]{1,0:T(8,128)(2,1)} %act_table.7) | copy-start | bytes 663556
  101.4 42.8 %collective-permute-start.7 = (s16[8,32,640]{2,1,0:T(8,128)(2,1)S(1)}, s16[8,32,640]{2,1,0:T(8,128)(2,1)S(1)}, u32[]{:S(2)}, u32[]{:S(2)}) collective-permute-start(s16[8,32,640]{2,1,0:T(8,128)(2,1)S(1)} %get-tuple-element.58), channel_id=1, source_target_pairs={{0,6},{1,7},{2,4},{3,5},{4,2},{5,3},{6,0},{7,1},{8,14},{9,15},{10,... | collective-permute-start | bytes 983048 | tf_op jit(solution)/shard_map/ppermute | solution.py:392
  106.0 19.4 %collective-permute-start.35 = (s16[8,32,640]{2,1,0:T(8,128)(2,1)S(1)}, s16[8,32,640]{2,1,0:T(8,128)(2,1)S(1)}, u32[]{:S(2)}, u32[]{:S(2)}) collective-permute-start(s16[8,32,640]{2,1,0:T(8,128)(2,1)S(1)} %get-tuple-element.76), channel_id=1, source_target_pairs={{0,2},{1,3},{2,0},{3,1},{4,6},{5,7},{6,4},{7,5},{8,10},{9,11},{10,... | collective-permute-start | bytes 983048 | tf_op jit(solution)/shard_map/ppermute | solution.py:392
  123.9 21.9 %collective-permute-start.32 = (bf16[4,64,512]{2,1,0:T(8,128)(2,1)S(1)}, bf16[4,64,512]{2,1,0:T(8,128)(2,1)S(1)}, u32[]{:S(2)}, u32[]{:S(2)}) collective-permute-start(bf16[4,64,512]{2,1,0:T(8,128)(2,1)S(1)} %get-tuple-element.73), channel_id=1, source_target_pairs={{0,8},{8,0},{16,24},{24,16},{1,9},{9,1},{17,25},{25,17},{2,10},{10... | collective-permute-start | bytes 786440 | tf_op jit(solution)/shard_map/ppermute | solution.py:429
  132.9 13.5 %collective-permute-start.36 = (bf16[4,64,512]{2,1,0:T(8,128)(2,1)S(1)}, bf16[4,64,512]{2,1,0:T(8,128)(2,1)S(1)}, u32[]{:S(2)}, u32[]{:S(2)}) collective-permute-start(bf16[4,64,512]{2,1,0:T(8,128)(2,1)S(1)} %get-tuple-element.79), channel_id=1, source_target_pairs={{0,8},{8,0},{16,24},{24,16},{1,9},{9,1},{17,25},{25,17},{2,10},{10... | collective-permute-start | bytes 786440 | tf_op jit(solution)/shard_map/ppermute | solution.py:429
  133.6 14.2 %collective-permute-start.37 = (bf16[4,64,512]{2,1,0:T(8,128)(2,1)S(1)}, bf16[4,64,512]{2,1,0:T(8,128)(2,1)S(1)}, u32[]{:S(2)}, u32[]{:S(2)}) collective-permute-start(bf16[4,64,512]{2,1,0:T(8,128)(2,1)S(1)} %get-tuple-element.80), channel_id=1, source_target_pairs={{0,16},{8,24},{16,0},{24,8},{1,17},{9,25},{17,1},{25,9},{2,18},{10... | collective-permute-start | bytes 786440 | tf_op jit(solution)/shard_map/ppermute | solution.py:429
  135.1 14.9 %collective-permute-start.38 = (bf16[4,64,512]{2,1,0:T(8,128)(2,1)S(1)}, bf16[4,64,512]{2,1,0:T(8,128)(2,1)S(1)}, u32[]{:S(2)}, u32[]{:S(2)}) collective-permute-start(bf16[4,64,512]{2,1,0:T(8,128)(2,1)S(1)} %get-tuple-element.81), channel_id=1, source_target_pairs={{0,24},{8,16},{16,8},{24,0},{1,25},{9,17},{17,9},{25,1},{2,26},{10... | collective-permute-start | bytes 786440 | tf_op jit(solution)/shard_map/ppermute | solution.py:429
  144.3 33.3 %collective-permute-start.33 = (bf16[4,64,512]{2,1,0:T(8,128)(2,1)S(1)}, bf16[4,64,512]{2,1,0:T(8,128)(2,1)S(1)}, u32[]{:S(2)}, u32[]{:S(2)}) collective-permute-start(bf16[4,64,512]{2,1,0:T(8,128)(2,1)S(1)} %get-tuple-element.74), channel_id=1, source_target_pairs={{0,16},{8,24},{16,0},{24,8},{1,17},{9,25},{17,1},{25,9},{2,18},{10... | collective-permute-start | bytes 786440 | tf_op jit(solution)/shard_map/ppermute | solution.py:429
  145.8 31.8 %collective-permute-start.34 = (bf16[4,64,512]{2,1,0:T(8,128)(2,1)S(1)}, bf16[4,64,512]{2,1,0:T(8,128)(2,1)S(1)}, u32[]{:S(2)}, u32[]{:S(2)}) collective-permute-start(bf16[4,64,512]{2,1,0:T(8,128)(2,1)S(1)} %get-tuple-element.75), channel_id=1, source_target_pairs={{0,24},{8,16},{16,8},{24,0},{1,25},{9,17},{17,9},{25,1},{2,26},{10... | collective-permute-start | bytes 786440 | tf_op jit(solution)/shard_map/ppermute | solution.py:429
  146.4 14.2 %collective-permute-start.39 = (bf16[4,64,512]{2,1,0:T(8,128)(2,1)S(1)}, bf16[4,64,512]{2,1,0:T(8,128)(2,1)S(1)}, u32[]{:S(2)}, u32[]{:S(2)}) collective-permute-start(bf16[4,64,512]{2,1,0:T(8,128)(2,1)S(1)} %get-tuple-element.85), channel_id=1, source_target_pairs={{0,8},{8,0},{16,24},{24,16},{1,9},{9,1},{17,25},{25,17},{2,10},{10... | collective-permute-start | bytes 786440 | tf_op jit(solution)/shard_map/ppermute | solution.py:429
  147.8 20.4 %collective-permute-start.40 = (bf16[4,64,512]{2,1,0:T(8,128)(2,1)S(1)}, bf16[4,64,512]{2,1,0:T(8,128)(2,1)S(1)}, u32[]{:S(2)}, u32[]{:S(2)}) collective-permute-start(bf16[4,64,512]{2,1,0:T(8,128)(2,1)S(1)} %get-tuple-element.86), channel_id=1, source_target_pairs={{0,16},{8,24},{16,0},{24,8},{1,17},{9,25},{17,1},{25,9},{2,18},{10... | collective-permute-start | bytes 786440 | tf_op jit(solution)/shard_map/ppermute | solution.py:429
  150.0 19.2 %collective-permute-start.41 = (bf16[4,64,512]{2,1,0:T(8,128)(2,1)S(1)}, bf16[4,64,512]{2,1,0:T(8,128)(2,1)S(1)}, u32[]{:S(2)}, u32[]{:S(2)}) collective-permute-start(bf16[4,64,512]{2,1,0:T(8,128)(2,1)S(1)} %get-tuple-element.87), channel_id=1, source_target_pairs={{0,24},{8,16},{16,8},{24,0},{1,25},{9,17},{17,9},{25,1},{2,26},{10... | collective-permute-start | bytes 786440 | tf_op jit(solution)/shard_map/ppermute | solution.py:429
  160.7 20.3 %collective-permute-start.28 = (bf16[4,64,512]{2,1,0:T(8,128)(2,1)S(1)}, bf16[4,64,512]{2,1,0:T(8,128)(2,1)S(1)}, u32[]{:S(2)}, u32[]{:S(2)}) collective-permute-start(bf16[4,64,512]{2,1,0:T(8,128)(2,1)S(1)} %get-tuple-element.67), channel_id=1, source_target_pairs={{0,8},{8,0},{16,24},{24,16},{1,9},{9,1},{17,25},{25,17},{2,10},{10... | collective-permute-start | bytes 786440 | tf_op jit(solution)/shard_map/ppermute | solution.py:429
  168.3 13.4 %collective-permute-start.29 = (bf16[4,64,512]{2,1,0:T(8,128)(2,1)S(1)}, bf16[4,64,512]{2,1,0:T(8,128)(2,1)S(1)}, u32[]{:S(2)}, u32[]{:S(2)}) collective-permute-start(bf16[4,64,512]{2,1,0:T(8,128)(2,1)S(1)} %get-tuple-element.68), channel_id=1, source_target_pairs={{0,16},{8,24},{16,0},{24,8},{1,17},{9,25},{17,1},{25,9},{2,18},{10... | collective-permute-start | bytes 786440 | tf_op jit(solution)/shard_map/ppermute | solution.py:429
  169.3 12.4 %collective-permute-start.30 = (bf16[4,64,512]{2,1,0:T(8,128)(2,1)S(1)}, bf16[4,64,512]{2,1,0:T(8,128)(2,1)S(1)}, u32[]{:S(2)}, u32[]{:S(2)}) collective-permute-start(bf16[4,64,512]{2,1,0:T(8,128)(2,1)S(1)} %get-tuple-element.69), channel_id=1, source_target_pairs={{0,24},{8,16},{16,8},{24,0},{1,25},{9,17},{17,9},{25,1},{2,26},{10... | collective-permute-start | bytes 786440 | tf_op jit(solution)/shard_map/ppermute | solution.py:429
  (1 other events, 0.7 us)

commit v2 on v1

--- a/solution.py
+++ b/solution.py
@@ -36,16 +36,12 @@
     return lax.rem(chip + chips - n // 2, chips) * 2 + (core ^ (n % 2))
 
 
-def weights_kernel(idx, w_stoch, w_deter, w_prior, out, quarter, sems):
-    srows, cols = w_stoch.shape[0], out.shape[1]
-    drows = w_deter.shape[1]
-    wide = quarter.shape[1]
+def weights_kernel(idx, w_stoch, w_deter, w_prior, stoch, deter, quarter, sems):
+    cols, wide = stoch.shape[1], quarter.shape[1]
     at = pl.multiple_of(idx[0] * cols, cols)
     copies = [
-        pltpu.make_async_copy(
-            w_stoch.at[:, pl.ds(at, cols)], out.at[pl.ds(0, srows)], sems.at[0]
-        ),
-        pltpu.make_async_copy(w_deter.at[idx[0]], out.at[pl.ds(srows, drows)], sems.at[1]),
+        pltpu.make_async_copy(w_stoch.at[:, pl.ds(at, cols)], stoch, sems.at[0]),
+        pltpu.make_async_copy(w_deter.at[idx[0]], deter, sems.at[1]),
         pltpu.make_async_copy(
             w_prior.at[:, pl.ds(pl.multiple_of(idx[0] * wide, wide), wide)], quarter, sems.at[2]
         ),
@@ -107,12 +103,13 @@
     order = slot_map(chip, chips, 2 * cap, (slots, slots), 0)
     order = jnp.where(order, 1.0, 0.0).astype(BF16)
     tail = samples.shape[0]
+    known[tail + STEPS :, :] = jnp.zeros((known.shape[0] - tail - STEPS, slots), I16)
     known[0:tail, :] = jnp.dot(
         samples[...].astype(F32).astype(BF16), order, preferred_element_type=F32
-    ).astype(I32)
-    known[tail:, :] = jnp.dot(
+    ).astype(I32).astype(I16)
+    known[tail : tail + STEPS, :] = jnp.dot(
         acts[...].astype(F32).astype(BF16), order, preferred_element_type=F32
-    ).astype(I32)
+    ).astype(I32).astype(I16)
 
 
 def fold_kernel(chips, run, *rest):
@@ -122,27 +119,15 @@
             outs[m][n] = piece[m * run : (m + 1) * run, :]
 
 
-def place_kernel(chips, splits, first, held, idx, *rest):
-    count = len(splits)
-    outs, sems = rest[-1 - count : -1], rest[-1]
-    pieces = rest[: len(rest) - 1 - count - held]
-    copies = []
-    for n, piece in enumerate(pieces):
-        place = shard_of(idx[1], idx[2], chips, n + first)
-        start = 0
-        for o, run in enumerate(splits):
-            copies.append(
-                pltpu.make_async_copy(
-                    piece.at[pl.ds(start, run)],
-                    outs[o].at[pl.ds(pl.multiple_of(place * run, run), run)],
-                    sems.at[n * count + o],
-                )
-            )
-            start += run
-    for copy in copies:
-        copy.start()
-    for copy in copies:
-        copy.wait()
+def place_kernel(chips, runs, first, held, idx, *rest):
+    count = len(runs)
+    outs = rest[-count:]
+    pieces = rest[: len(rest) - count - held]
+    each = len(pieces) // count
+    for o, run in enumerate(runs):
+        for n in range(each):
+            place = shard_of(idx[1], idx[2], chips, n + first) * run
+            outs[o][pl.ds(pl.multiple_of(place, run), run), :] = pieces[o * each + n][...]
 
 
 def column_kernel(chips, run, idx, *rest):
@@ -189,10 +174,10 @@
     z_s[0:GROUPS, :] = turned[0:GROUPS, :].astype(I32)
     spot = slice(m * part, (m + 1) * part)
     z_s[GROUPS : GROUPS * STEPS, :] = jnp.concatenate(
-        [g[0 : GROUPS * (STEPS - 1), spot] for g in given], 1
+        [g[0 : GROUPS * (STEPS - 1), spot].astype(I32) for g in given], 1
     )
     z_s[tail : tail + STEPS, :] = jnp.concatenate(
-        [g[tail : tail + STEPS, spot] for g in given], 1
+        [g[tail : tail + 16, spot].astype(I32)[:STEPS] for g in given], 1
     )
     iota = lax.broadcasted_iota(I32, (CLASSES, rows), 0)
     for step in range(STEPS):
@@ -249,7 +234,7 @@
     turned = logits.T
     spot = slice(m * count, (m + 1) * count)
     z = jnp.concatenate(
-        [known[t * GROUPS : (t + 1) * GROUPS, spot] for t in range(STEPS)], 1
+        [known[t * GROUPS : (t + 1) * GROUPS, spot].astype(I32) for t in range(STEPS)], 1
     )
     alive = jnp.concatenate([live[0:1, :]] * STEPS, 1) > 0
     iota = lax.broadcasted_iota(I32, (CLASSES, STEPS * count), 0)
@@ -308,7 +293,7 @@
         ring = [(a, (a + 2) % ny) for a in range(ny)]
         partner = swap_pairs(ny, 1)
 
-        def call(kernel, out_shape, ins, outs, scratch=(), mib=40, flops=0, **kwargs):
+        def call(kernel, out_shape, ins, outs, scratch=(), mib=16, flops=0, **kwargs):
             def run(*args):
                 return pl.pallas_call(
                     kernel,
@@ -327,29 +312,33 @@
 
         srows, drows, prows = w_stoch.shape[0], w_deter.shape[1], w_prior.shape[0]
         wide = w_prior.shape[1] // nx
-        shard, quarter = call(
+        own = call(
             weights_kernel,
             [
-                jax.ShapeDtypeStruct((srows + drows, cols), BF16),
+                jax.ShapeDtypeStruct((srows, cols), BF16),
+                jax.ShapeDtypeStruct((drows, cols), BF16),
                 jax.ShapeDtypeStruct((prows, wide), BF16),
             ],
             [SMEM, HBM, HBM, HBM],
-            [VMEM, VMEM],
+            [VMEM] * 3,
             [pltpu.SemaphoreType.DMA((3,))],
         )(idx, *(pltpu.with_memory_space_constraint(w, pltpu.HBM) for w in (w_stoch, w_deter, w_prior)))
-        stops, quarters = [shard], [quarter]
-        for _ in range(1, chips):
-            stops.append(lax.ppermute(stops[-1], "gy", ring))
-            quarters.append(lax.ppermute(quarters[-1], "gy", ring))
-        pieces = []
-        for piece in stops:
-            pieces += [piece, lax.ppermute(piece, "gy", partner)]
+        stops = {}
+        for name, shard in zip("sdp", own):
+            stops[name] = [shard]
+            for _ in range(1, chips):
+                stops[name].append(lax.ppermute(stops[name][-1], "gy", ring))
+        pieces = {}
+        for name in "sd":
+            pieces[name] = []
+            for piece in stops[name]:
+                pieces[name] += [piece, lax.ppermute(piece, "gy", partner)]
         column = call(
             functools.partial(column_kernel, chips, prows),
             jax.ShapeDtypeStruct((chips * prows, wide), BF16),
             [SMEM] + [VMEM] * chips,
             VMEM,
-        )(idx, *quarters)
+        )(idx, *stops["p"])
         priors = []
         for k in range(nx):
             piece = lax.ppermute(column, "gx", swap_pairs(nx, k)) if k else column
@@ -361,7 +350,7 @@
         *held, known = call(
             functools.partial(pack_kernel, chips, nx, cap),
             [jax.ShapeDtypeStruct((slots // 2, lined), I16)] * (2 * nx)
-            + [jax.ShapeDtypeStruct((samp.shape[0] + STEPS, slots), I32)],
+            + [jax.ShapeDtypeStruct((samp.shape[0] + 16, slots), I16)],
             [SMEM] * 3 + [VMEM] * 4,
             [VMEM] * (2 * nx + 1),
             [
@@ -392,16 +381,16 @@
             starts[m] = lax.ppermute(starts[m], "gy", swap_pairs(ny, 2 * m))
         placed = []
         early = 2 * chips - 2
-        for first, some in ((0, pieces[:early]), (early, pieces[early:])):
+        for first, end in ((0, early), (early, 2 * chips)):
+            some = pieces["s"][first:end] + pieces["d"][first:end]
             placed = call(
                 functools.partial(place_kernel, chips, (srows, drows), first, len(placed)),
                 [
                     jax.ShapeDtypeStruct((ny * srows, cols), BF16),
                     jax.ShapeDtypeStruct((ny * drows, cols), BF16),
                 ],
-                [SMEM] + [ANY] * len(some) + [VMEM] * len(placed),
+                [SMEM] + [VMEM] * (len(some) + len(placed)),
                 [VMEM] * 2,
-                [pltpu.SemaphoreType.DMA((2 * len(some),))],
                 input_output_aliases={len(some) + 1 + n: n for n in range(len(placed))},
             )(idx, *some, *placed)
         w_all, wd_all = placed

time: 187 us -> 184 us (0.984)
  Pallas kernels: 57.4 us -> 52.5 us
  waiting for transfers between devices: 78.5 us -> 82.8 us
  starting transfers between devices: 46 us -> 42 us
    ppermute x7, waiting for transfers between devices: 13.9 us -> 5.62 us  [on_device(): held[n] = lax.ppermute(held[n], ('gx', 'gy'), pairs)]
    ppermute x10 -> x17, waiting for transfers between devices: 23.4 us -> 29.9 us  [the longest x9 29.9 us: on_device(): stops[name].append(lax.ppermute(stops[name][-1], 'gy', ring))]
    pallas_call x16, Pallas kernels: 57.4 us -> 52.5 us  [run(): pl.pallas_call(kernel, out_shape=out_shape, in_specs=ins, out_specs=outs,...]
    ppermute x7, starting transfers between devices: 10.6 us -> 6.09 us  [on_device(): held[n] = lax.ppermute(held[n], ('gx', 'gy'), pairs)]
    ppermute x3, waiting for transfers between devices: 10.2 us -> 13.5 us  [on_device(): starts[m] = lax.ppermute(starts[m], 'gy', swap_pairs(ny, 2 * m))]
    ppermute x10 -> x17, starting transfers between devices: 6.14 us -> 9.22 us  [the longest x9 7.2 us: on_device(): stops[name].append(lax.ppermute(stops[name][-1], 'gy', ring))]
    ppermute x12, waiting for transfers between devices: 8.83 us -> 11.7 us  [on_device(): got.append(lax.ppermute(outs[k], 'gx', swap_pairs(nx, k)))]
    ppermute x3, starting transfers between devices: 5.71 us -> 3.63 us  [on_device(): starts[m] = lax.ppermute(starts[m], 'gy', swap_pairs(ny, 2 * m))]
  transfers between devices with their start and end apart: 42 -> 49, of which waited for: 13 -> 14; matrix products, arithmetic and copies ran while one was open for 0% -> 0% of each run, Pallas kernels for 27% -> 24%
where the time goes in v2:
time: 184 us
  waiting for transfers between devices  82.8 us (45%)
  Pallas kernels  52.5 us (29%)
  starting transfers between devices  42 us (23%)
  local copies, waits for them, and re-layouts  5.29 us (3%)
    pallas_call x16, Pallas kernels, run(): pl.pallas_call(kernel, out_shape=out_shape, in_specs=ins, out_specs=outs,...  52.5 us
    ppermute x9, waiting for transfers between devices, on_device(): stops[name].append(lax.ppermute(stops[name][-1], 'gy', ring))  29.9 us
    ppermute x3, waiting for transfers between devices, on_device(): piece = lax.ppermute(column, 'gx', swap_pairs(nx, k)) if k else column  22.1 us
    ppermute x12, starting transfers between devices, on_device(): got.append(lax.ppermute(outs[k], 'gx', swap_pairs(nx, k)))  15.4 us
    ppermute x3, waiting for transfers between devices, on_device(): starts[m] = lax.ppermute(starts[m], 'gy', swap_pairs(ny, 2 * m))  13.5 us
    ppermute x12, waiting for transfers between devices, on_device(): got.append(lax.ppermute(outs[k], 'gx', swap_pairs(nx, k)))  11.7 us
    ppermute x9, starting transfers between devices, on_device(): stops[name].append(lax.ppermute(stops[name][-1], 'gy', ring))  7.2 us
    ppermute x7, starting transfers between devices, on_device(): held[n] = lax.ppermute(held[n], ('gx', 'gy'), pairs)  6.09 us
  transfers between devices with their start and end apart: 49, of which 14 were waited for; matrix products, arithmetic and copies ran while one was open for 0% of the time, Pallas kernels for 24%

profile of v2, /device:TPU:0, one launch (start us, length us, event | category | flops | bytes accessed | tf_op | source)
XLA Modules:
  0.0 183.5 jit_solution(8947209206521012144)
XLA Ops:
  0.7 1.6 copy-done
  6.0 3.3 %shard_map.113 = (s16[128,640]{1,0:T(8,128)(2,1)S(1)}, s16[128,640]{1,0:T(8,128)(2,1)S(1)}, s16[128,640]{1,0:T(8,128)(2,1)S(1)}, s16[128,640]{1,0:T(8,128)(2,1)S...) custom-call(s32[3]{0:T(128)S(1)} %pad_add_fusion.idx, ...), custom_call_target="tpu_custom_call" | custom-call | bytes 1048576 | tf_op jit(solution)/shard_map/pallas_call | solution.py:298
  9.9 1.7 shard_map.115
  11.6 2.6 %collective-permute-start.25 = (bf16[256,256]{1,0:T(8,128)(2,1)S(1)}, bf16[256,256]{1,0:T(8,128)(2,1)S(1)}, u32[]{:S(2)}, u32[]{:S(2)}) collective-permute-start(bf16[256,256]{1,0:T(8,128)(2,1)S(1)} %get-tuple-element.67.rest_0_), channel_id=1, source_target_pairs={{0,2},{1,3},{2,4},{3,5},{4,6},{5,7},{6,0},{7,1},{8,10},{9,11},{10,... | collective-permute-start | bytes 393224 | tf_op jit(solution)/shard_map/ppermute | solution.py:330
  14.2 1.5 collective-permute-start.1
  15.8 1.6 collective-permute-start.8
  17.4 3.0 %collective-permute-done.25.rest_1_ = bf16[256,256]{1,0:T(8,128)(2,1)S(1)} collective-permute-done((bf16[256,256]{1,0:T(8,128)(2,1)S(1)}, bf16[256,256]{1,0:T(8,128)(2,1)S(1)}, u32[]{:S(2)}, u32[]{:S(2)}) %collective-permute-start.25) | collective-permute-done | bytes 131104 | tf_op jit(solution)/shard_map/ppermute | solution.py:330
  20.4 1.5 collective-permute-start.3
  21.9 1.4 collective-permute-done.2.rest_3_
  23.3 2.4 %collective-permute-start.5 = (s16[128,640]{1,0:T(8,128)(2,1)S(1)}, s16[128,640]{1,0:T(8,128)(2,1)S(1)}, u32[]{:S(2)}, u32[]{:S(2)}) collective-permute-start(s16[128,640]{1,0:T(8,128)(2,1)S(1)} %get-tuple-element.57), channel_id=1, source_target_pairs={{0,24},{1,25},{2,26},{3,27},{4,28},{5,29},{6,30},{7,31},{8,16},{9,... | collective-permute-start | bytes 491528 | tf_op jit(solution)/shard_map/ppermute | solution.py:369
  25.7 1.7 collective-permute-done.3.rest_4_
  27.5 5.9 %collective-permute-done.12.rest_8_ = bf16[64,1536]{1,0:T(8,128)(2,1)S(1)} collective-permute-done((bf16[64,1536]{1,0:T(8,128)(2,1)S(1)}, bf16[64,1536]{1,0:T(8,128)(2,1)S(1)}, u32[]{:S(2)}, u32[]{:S(2)}) %collective-permute-start.12) | collective-permute-done | bytes 196640 | tf_op jit(solution)/shard_map/ppermute | solution.py:330
  33.4 2.5 %collective-permute-done.4.rest_5_ = s16[128,640]{1,0:T(8,128)(2,1)S(1)} collective-permute-done((s16[128,640]{1,0:T(8,128)(2,1)S(1)}, s16[128,640]{1,0:T(8,128)(2,1)S(1)}, u32[]{:S(2)}, u32[]{:S(2)}) %collective-permute-start.4) | collective-permute-done | bytes 163872 | tf_op jit(solution)/shard_map/ppermute | solution.py:369
  36.8 1.0 collective-permute-start.26
  37.8 2.0 %collective-permute-start.9 = (bf16[128,1536]{1,0:T(8,128)(2,1)S(1)}, bf16[128,1536]{1,0:T(8,128)(2,1)S(1)}, u32[]{:S(2)}, u32[]{:S(2)}) collective-permute-start(bf16[128,1536]{1,0:T(8,128)(2,1)S(1)} %collective-permute-done.8.rest_2_), channel_id=1, source_target_pairs={{0,2},{1,3},{2,4},{3,5},{4,6},{5,7},{6,0},{7,1},{8,10},{9,11},{10,... | collective-permute-start | bytes 1179656 | tf_op jit(solution)/shard_map/ppermute | solution.py:330
  39.8 3.2 %collective-permute-done.13.rest_10_ = bf16[64,1536]{1,0:T(8,128)(2,1)S(1)} collective-permute-done((bf16[64,1536]{1,0:T(8,128)(2,1)S(1)}, bf16[64,1536]{1,0:T(8,128)(2,1)S(1)}, u32[]{:S(2)}, u32[]{:S(2)}) %collective-permute-start.13) | collective-permute-done | bytes 196640 | tf_op jit(solution)/shard_map/ppermute | solution.py:330
  43.0 2.8 %collective-permute-done.26.rest_2_ = bf16[256,256]{1,0:T(8,128)(2,1)S(1)} collective-permute-done((bf16[256,256]{1,0:T(8,128)(2,1)S(1)}, bf16[256,256]{1,0:T(8,128)(2,1)S(1)}, u32[]{:S(2)}, u32[]{:S(2)}) %collective-permute-start.26) | collective-permute-done | bytes 131104 | tf_op jit(solution)/shard_map/ppermute | solution.py:330
  45.8 14.9 %collective-permute-done.27.rest_3_ = bf16[256,256]{1,0:T(8,128)(2,1)S(1)} collective-permute-done((bf16[256,256]{1,0:T(8,128)(2,1)S(1)}, bf16[256,256]{1,0:T(8,128)(2,1)S(1)}, u32[]{:S(2)}, u32[]{:S(2)}) %collective-permute-start.27) | collective-permute-done | bytes 131104 | tf_op jit(solution)/shard_map/ppermute | solution.py:330
  63.2 1.5 collective-permute-start.31
  64.7 1.2 collective-permute-start.33
  66.0 11.2 %collective-permute-done.29.rest_2_ = bf16[1024,256]{1,0:T(8,128)(2,1)S(1)} collective-permute-done((bf16[1024,256]{1,0:T(8,128)(2,1)S(1)}, bf16[1024,256]{1,0:T(8,128)(2,1)S(1)}, u32[]{:S(2)}, u32[]{:S(2)}) %collective-permute-start.29) | collective-permute-done | bytes 524320 | tf_op jit(solution)/shard_map/ppermute | solution.py:344
  77.2 10.8 %collective-permute-done.31.rest_4_ = bf16[1024,256]{1,0:T(8,128)(2,1)S(1)} collective-permute-done((bf16[1024,256]{1,0:T(8,128)(2,1)S(1)}, bf16[1024,256]{1,0:T(8,128)(2,1)S(1)}, u32[]{:S(2)}, u32[]{:S(2)}) %collective-permute-start.31) | collective-permute-done | bytes 524320 | tf_op jit(solution)/shard_map/ppermute | solution.py:344
  88.8 1.2 collective-permute-start.22
  90.1 1.4 collective-permute-start.23
  93.2 1.1 shard_map.120.wp_s
  94.3 1.0 collective-permute-start.7
  96.0 2.5 %collective-permute-start.42 = (s16[8,32,640]{2,1,0:T(8,128)(2,1)S(1)}, s16[8,32,640]{2,1,0:T(8,128)(2,1)S(1)}, u32[]{:S(2)}, u32[]{:S(2)}) collective-permute-start(s16[8,32,640]{2,1,0:T(8,128)(2,1)S(1)} %get-tuple-element.78), channel_id=1, source_target_pairs={{0,2},{1,3},{2,0},{3,1},{4,6},{5,7},{6,4},{7,5},{8,10},{9,11},{10,... | collective-permute-start | bytes 983048 | tf_op jit(solution)/shard_map/ppermute | solution.py:381
  98.5 13.5 %collective-permute-done.38.x = s16[8,32,640]{2,1,0:T(8,128)(2,1)S(1)} collective-permute-done((s16[8,32,640]{2,1,0:T(8,128)(2,1)S(1)}, s16[8,32,640]{2,1,0:T(8,128)(2,1)S(1)}, u32[]{:S(2)}, u32[]{:S(2)}) %collective-permute-start.38) | collective-permute-done | bytes 327712 | tf_op jit(solution)/shard_map/ppermute | solution.py:381
  112.0 7.3 %shard_map.121 = (bf16[4,64,512]{2,1,0:T(8,128)(2,1)S(1)}, bf16[4,64,512]{2,1,0:T(8,128)(2,1)S(1)}, bf16[4,64,512]{2,1,0:T(8,128)(2,1)S(1)}, bf16[4,64,512]{2,1,0:T(8,128)(2,1)S(1)}, f32[8,64]{1,0:T(8,128)S(1)}) custom-call(s32[3]{0:T(128)S(1)} %pad_add_fusion.idx, s16[8,32,640]{2,1,0:T(8,128)(2,1)S(1)} %collective-permute-done.38.x, ...), custom_call_target="tpu_custom_call" | custom-call | flops 4831838208 | bytes 1048576 | tf_op jit(solution)/shard_map/pallas_call | solution.py:298
  120.1 7.5 %shard_map.122 = (bf16[4,64,512]{2,1,0:T(8,128)(2,1)S(1)}, bf16[4,64,512]{2,1,0:T(8,128)(2,1)S(1)}, bf16[4,64,512]{2,1,0:T(8,128)(2,1)S(1)}, bf16[4,64,512]{2,1,0:T(8,128)(2,1)S(1)}, f32[8,64]{1,0:T(8,128)S(1)}) custom-call(s32[3]{0:T(128)S(1)} %pad_add_fusion.idx, s16[8,32,640]{2,1,0:T(8,128)(2,1)S(1)} %collective-permute-done.42.x, ...), custom_call_target="tpu_custom_call" | custom-call | flops 4831838208 | bytes 1048576 | tf_op jit(solution)/shard_map/pallas_call | solution.py:298
  127.6 1.3 collective-permute-start.43
  129.0 1.5 collective-permute-start.44
  131.2 7.3 %shard_map.123 = (bf16[4,64,512]{2,1,0:T(8,128)(2,1)S(1)}, bf16[4,64,512]{2,1,0:T(8,128)(2,1)S(1)}, bf16[4,64,512]{2,1,0:T(8,128)(2,1)S(1)}, bf16[4,64,512]{2,1,0:T(8,128)(2,1)S(1)}, f32[8,64]{1,0:T(8,128)S(1)}) custom-call(s32[3]{0:T(128)S(1)} %pad_add_fusion.idx, s16[8,32,640]{2,1,0:T(8,128)(2,1)S(1)} %get-tuple-element.84.x, ...), custom_call_target="tpu_custom_call" | custom-call | flops 4831838208 | bytes 1048576 | tf_op jit(solution)/shard_map/pallas_call | solution.py:298
  138.5 1.5 collective-permute-start.40
  139.9 1.3 collective-permute-start.41
  142.0 5.2 %collective-permute-done.44.rest_2_ = bf16[4,64,512]{2,1,0:T(8,128)(2,1)S(1)} collective-permute-done((bf16[4,64,512]{2,1,0:T(8,128)(2,1)S(1)}, bf16[4,64,512]{2,1,0:T(8,128)(2,1)S(1)}, u32[]{:S(2)}, u32[]{:S(2)}) %collective-permute-start.44) | collective-permute-done | bytes 262176 | tf_op jit(solution)/shard_map/ppermute | solution.py:418
  147.2 3.0 %collective-permute-start.47 = (bf16[4,64,512]{2,1,0:T(8,128)(2,1)S(1)}, bf16[4,64,512]{2,1,0:T(8,128)(2,1)S(1)}, u32[]{:S(2)}, u32[]{:S(2)}) collective-permute-start(bf16[4,64,512]{2,1,0:T(8,128)(2,1)S(1)} %get-tuple-element.88), channel_id=1, source_target_pairs={{0,16},{8,24},{16,0},{24,8},{1,17},{9,25},{17,1},{25,9},{2,18},{10... | collective-permute-start | bytes 786440 | tf_op jit(solution)/shard_map/ppermute | solution.py:418
  150.2 7.3 %shard_map.118 = (bf16[4,64,512]{2,1,0:T(8,128)(2,1)S(1)}, bf16[4,64,512]{2,1,0:T(8,128)(2,1)S(1)}, bf16[4,64,512]{2,1,0:T(8,128)(2,1)S(1)}, bf16[4,64,512]{2,1,0:T(8,128)(2,1)S(1)}, f32[8,64]{1,0:T(8,128)S(1)}) custom-call(s32[3]{0:T(128)S(1)} %pad_add_fusion.idx, s16[8,32,640]{2,1,0:T(8,128)(2,1)S(1)} %collective-permute-done.7.x, ...), custom_call_target="tpu_custom_call" | custom-call | flops 4831838208 | bytes 1048576 | tf_op jit(solution)/shard_map/pallas_call | solution.py:298
  157.5 1.8 collective-permute-start.35
  159.2 5.5 %collective-permute-done.47.rest_2_ = bf16[4,64,512]{2,1,0:T(8,128)(2,1)S(1)} collective-permute-done((bf16[4,64,512]{2,1,0:T(8,128)(2,1)S(1)}, bf16[4,64,512]{2,1,0:T(8,128)(2,1)S(1)}, u32[]{:S(2)}, u32[]{:S(2)}) %collective-permute-start.47) | collective-permute-done | bytes 262176 | tf_op jit(solution)/shard_map/ppermute | solution.py:418
  164.7 1.5 collective-permute-start.36
  166.2 1.2 collective-permute-start.37
  167.4 3.3 %shard_map.124 = (bf16[4,4,16,4,2048]{4,3,2,1,0:T(4,128)(2,1)}, f32[32,256]{1,0:T(8,128)S(1)}) custom-call(s32[3]{0:T(128)S(1)} %pad_add_fusion.idx, s16[144,256]{1,0:T(8,128)(2,1)S(1)} %get-tuple-element.50.rest_0_.known, f32[8,64]{1,0:T(8,128)S(1)} %get-tuple-element.85.live, bf16[2048,1024]{1,0:T(8,128)(2,1)S(1)} %shard_map.120.wp_s, ...), custom_call_target="tpu_custom_call" | custom-call | flops 1073741824 | bytes 1048576 | tf_op jit(solution)/shard_map/pallas_call | solution.py:298
  170.8 3.4 %shard_map.125 = (bf16[4,4,16,4,2048]{4,3,2,1,0:T(4,128)(2,1)}, f32[32,256]{1,0:T(8,128)S(1)}) custom-call(s32[3]{0:T(128)S(1)} %pad_add_fusion.idx, s16[144,256]{1,0:T(8,128)(2,1)S(1)} %get-tuple-element.50.rest_0_.known, f32[8,64]{1,0:T(8,128)S(1)} %get-tuple-element.79.live, ...), custom_call_target="tpu_custom_call", output_to_operand_aliasing={{0}: (8, {})} | custom-call | flops 1073741824 | bytes 1048576 | tf_op jit(solution)/shard_map/pallas_call | solution.py:298
  174.2 3.4 %shard_map.126 = (bf16[4,4,16,4,2048]{4,3,2,1,0:T(4,128)(2,1)}, f32[32,256]{1,0:T(8,128)S(1)}) custom-call(s32[3]{0:T(128)S(1)} %pad_add_fusion.idx, s16[144,256]{1,0:T(8,128)(2,1)S(1)} %get-tuple-element.50.rest_0_.known, f32[8,64]{1,0:T(8,128)S(1)} %get-tuple-element.73.live, ...), custom_call_target="tpu_custom_call", output_to_operand_aliasing={{0}: (8, {})} | custom-call | flops 1073741824 | bytes 1048576 | tf_op jit(solution)/shard_map/pallas_call | solution.py:298
  177.5 1.1 collective-permute-done.36.rest_2_
  178.6 3.3 %shard_map.127 = (bf16[4,4,16,4,2048]{4,3,2,1,0:T(4,128)(2,1)}, f32[32,256]{1,0:T(8,128)S(1)}) custom-call(s32[3]{0:T(128)S(1)} %pad_add_fusion.idx, s16[144,256]{1,0:T(8,128)(2,1)S(1)} %get-tuple-element.50.rest_0_.known, f32[8,64]{1,0:T(8,128)S(1)} %get-tuple-element.66.live, ...), custom_call_target="tpu_custom_call", output_to_operand_aliasing={{0}: (8, {})} | custom-call | flops 1073741824 | bytes 1048576 | tf_op jit(solution)/shard_map/pallas_call | solution.py:298
  181.9 1.6 shard_map.128
  (81 shorter events, 13.3 us)
Async XLA Ops:
  9.3 11.1 %collective-permute-start = (s16[128,640]{1,0:T(8,128)(2,1)S(1)}, s16[128,640]{1,0:T(8,128)(2,1)S(1)}, u32[]{:S(2)}, u32[]{:S(2)}) collective-permute-start(s16[128,640]{1,0:T(8,128)(2,1)S(1)} %get-tuple-element.52), channel_id=1, source_target_pairs={{0,1},{1,0},{2,3},{3,2},{4,5},{5,4},{6,7},{7,6},{8,9},{9,8},{10,11... | collective-permute-start | bytes 491528 | tf_op jit(solution)/shard_map/ppermute | solution.py:369
  11.6 8.8 %collective-permute-start.25 = (bf16[256,256]{1,0:T(8,128)(2,1)S(1)}, bf16[256,256]{1,0:T(8,128)(2,1)S(1)}, u32[]{:S(2)}, u32[]{:S(2)}) collective-permute-start(bf16[256,256]{1,0:T(8,128)(2,1)S(1)} %get-tuple-element.67.rest_0_), channel_id=1, source_target_pairs={{0,2},{1,3},{2,4},{3,5},{4,6},{5,7},{6,0},{7,1},{8,10},{9,11},{10,... | collective-permute-start | bytes 393224 | tf_op jit(solution)/shard_map/ppermute | solution.py:330
  14.2 7.7 %collective-permute-start.1 = (s16[128,640]{1,0:T(8,128)(2,1)S(1)}, s16[128,640]{1,0:T(8,128)(2,1)S(1)}, u32[]{:S(2)}, u32[]{:S(2)}) collective-permute-start(s16[128,640]{1,0:T(8,128)(2,1)S(1)} %get-tuple-element.53), channel_id=1, source_target_pairs={{0,8},{1,9},{2,10},{3,11},{4,12},{5,13},{6,14},{7,15},{8,0},{9,1},... | collective-permute-start | bytes 491528 | tf_op jit(solution)/shard_map/ppermute | solution.py:369
  15.7 7.6 %collective-permute-start.2 = (s16[128,640]{1,0:T(8,128)(2,1)S(1)}, s16[128,640]{1,0:T(8,128)(2,1)S(1)}, u32[]{:S(2)}, u32[]{:S(2)}) collective-permute-start(s16[128,640]{1,0:T(8,128)(2,1)S(1)} %get-tuple-element.54), channel_id=1, source_target_pairs={{0,9},{1,8},{2,11},{3,10},{4,13},{5,12},{6,15},{7,14},{8,1},{9,0},... | collective-permute-start | bytes 491528 | tf_op jit(solution)/shard_map/ppermute | solution.py:369
  15.8 22.0 %collective-permute-start.8 = (bf16[128,1536]{1,0:T(8,128)(2,1)S(1)}, bf16[128,1536]{1,0:T(8,128)(2,1)S(1)}, u32[]{:S(2)}, u32[]{:S(2)}) collective-permute-start(bf16[128,1536]{1,0:T(8,128)(2,1)S(1)} %get-tuple-element.60.rest_0_), channel_id=1, source_target_pairs={{0,2},{1,3},{2,4},{3,5},{4,6},{5,7},{6,0},{7,1},{8,10},{9,11},{10,... | collective-permute-start | bytes 1179656 | tf_op jit(solution)/shard_map/ppermute | solution.py:330
  20.4 13.0 %collective-permute-start.12 = (bf16[64,1536]{1,0:T(8,128)(2,1)S(1)}, bf16[64,1536]{1,0:T(8,128)(2,1)S(1)}, u32[]{:S(2)}, u32[]{:S(2)}) collective-permute-start(bf16[64,1536]{1,0:T(8,128)(2,1)S(1)} %get-tuple-element.61.rest_6_), channel_id=1, source_target_pairs={{0,2},{1,3},{2,4},{3,5},{4,6},{5,7},{6,0},{7,1},{8,10},{9,11},{10,... | collective-permute-start | bytes 589832 | tf_op jit(solution)/shard_map/ppermute | solution.py:330
  20.4 7.1 %collective-permute-start.3 = (s16[128,640]{1,0:T(8,128)(2,1)S(1)}, s16[128,640]{1,0:T(8,128)(2,1)S(1)}, u32[]{:S(2)}, u32[]{:S(2)}) collective-permute-start(s16[128,640]{1,0:T(8,128)(2,1)S(1)} %get-tuple-element.55), channel_id=1, source_target_pairs={{0,16},{1,17},{2,18},{3,19},{4,20},{5,21},{6,22},{7,23},{8,24},{9,... | collective-permute-start | bytes 491528 | tf_op jit(solution)/shard_map/ppermute | solution.py:369
  21.9 14.0 %collective-permute-start.4 = (s16[128,640]{1,0:T(8,128)(2,1)S(1)}, s16[128,640]{1,0:T(8,128)(2,1)S(1)}, u32[]{:S(2)}, u32[]{:S(2)}) collective-permute-start(s16[128,640]{1,0:T(8,128)(2,1)S(1)} %get-tuple-element.56), channel_id=1, source_target_pairs={{0,17},{1,16},{2,19},{3,18},{4,21},{5,20},{6,23},{7,22},{8,25},{9,... | collective-permute-start | bytes 491528 | tf_op jit(solution)/shard_map/ppermute | solution.py:369
  23.3 13.5 %collective-permute-start.5 = (s16[128,640]{1,0:T(8,128)(2,1)S(1)}, s16[128,640]{1,0:T(8,128)(2,1)S(1)}, u32[]{:S(2)}, u32[]{:S(2)}) collective-permute-start(s16[128,640]{1,0:T(8,128)(2,1)S(1)} %get-tuple-element.57), channel_id=1, source_target_pairs={{0,24},{1,25},{2,26},{3,27},{4,28},{5,29},{6,30},{7,31},{8,16},{9,... | collective-permute-start | bytes 491528 | tf_op jit(solution)/shard_map/ppermute | solution.py:369
  27.5 10.3 %collective-permute-start.6 = (s16[128,640]{1,0:T(8,128)(2,1)S(1)}, s16[128,640]{1,0:T(8,128)(2,1)S(1)}, u32[]{:S(2)}, u32[]{:S(2)}) collective-permute-start(s16[128,640]{1,0:T(8,128)(2,1)S(1)} %get-tuple-element.58), channel_id=1, source_target_pairs={{0,25},{1,24},{2,27},{3,26},{4,29},{5,28},{6,31},{7,30},{8,17},{9,... | collective-permute-start | bytes 491528 | tf_op jit(solution)/shard_map/ppermute | solution.py:369
  33.4 9.6 %collective-permute-start.13 = (bf16[64,1536]{1,0:T(8,128)(2,1)S(1)}, bf16[64,1536]{1,0:T(8,128)(2,1)S(1)}, u32[]{:S(2)}, u32[]{:S(2)}) collective-permute-start(bf16[64,1536]{1,0:T(8,128)(2,1)S(1)} %collective-permute-done.12.rest_8_), channel_id=1, source_target_pairs={{0,2},{1,3},{2,4},{3,5},{4,6},{5,7},{6,0},{7,1},{8,10},{9,11},{10,... | collective-permute-start | bytes 589832 | tf_op jit(solution)/shard_map/ppermute | solution.py:330
  35.9 25.9 %collective-permute-start.16 = (bf16[128,1536]{1,0:T(8,128)(2,1)S(1)}, bf16[128,1536]{1,0:T(8,128)(2,1)S(1)}, u32[]{:S(2)}, u32[]{:S(2)}) collective-permute-start(bf16[128,1536]{1,0:T(8,128)(2,1)S(1)} %get-tuple-element.60.rest_0_), channel_id=1, source_target_pairs={{0,1},{1,0},{2,3},{3,2},{4,5},{5,4},{6,7},{7,6},{8,9},{9,8},{10,11... | collective-permute-start | bytes 1179656 | tf_op jit(solution)/shard_map/ppermute | solution.py:335
  36.8 9.0 %collective-permute-start.26 = (bf16[256,256]{1,0:T(8,128)(2,1)S(1)}, bf16[256,256]{1,0:T(8,128)(2,1)S(1)}, u32[]{:S(2)}, u32[]{:S(2)}) collective-permute-start(bf16[256,256]{1,0:T(8,128)(2,1)S(1)} %collective-permute-done.25.rest_1_), channel_id=1, source_target_pairs={{0,2},{1,3},{2,4},{3,5},{4,6},{5,7},{6,0},{7,1},{8,10},{9,11},{10,... | collective-permute-start | bytes 393224 | tf_op jit(solution)/shard_map/ppermute | solution.py:330
  37.8 8.0 %collective-permute-start.19 = (bf16[64,1536]{1,0:T(8,128)(2,1)S(1)}, bf16[64,1536]{1,0:T(8,128)(2,1)S(1)}, u32[]{:S(2)}, u32[]{:S(2)}) collective-permute-start(bf16[64,1536]{1,0:T(8,128)(2,1)S(1)} %get-tuple-element.61.rest_6_), channel_id=1, source_target_pairs={{0,1},{1,0},{2,3},{3,2},{4,5},{5,4},{6,7},{7,6},{8,9},{9,8},{10,11... | collective-permute-start | bytes 589832 | tf_op jit(solution)/shard_map/ppermute | solution.py:335
  37.8 25.3 %collective-permute-start.9 = (bf16[128,1536]{1,0:T(8,128)(2,1)S(1)}, bf16[128,1536]{1,0:T(8,128)(2,1)S(1)}, u32[]{:S(2)}, u32[]{:S(2)}) collective-permute-start(bf16[128,1536]{1,0:T(8,128)(2,1)S(1)} %collective-permute-done.8.rest_2_), channel_id=1, source_target_pairs={{0,2},{1,3},{2,4},{3,5},{4,6},{5,7},{6,0},{7,1},{8,10},{9,11},{10,... | collective-permute-start | bytes 1179656 | tf_op jit(solution)/shard_map/ppermute | solution.py:330
  43.0 17.7 %collective-permute-start.14 = (bf16[64,1536]{1,0:T(8,128)(2,1)S(1)}, bf16[64,1536]{1,0:T(8,128)(2,1)S(1)}, u32[]{:S(2)}, u32[]{:S(2)}) collective-permute-start(bf16[64,1536]{1,0:T(8,128)(2,1)S(1)} %collective-permute-done.13.rest_10_), channel_id=1, source_target_pairs={{0,2},{1,3},{2,4},{3,5},{4,6},{5,7},{6,0},{7,1},{8,10},{9,11},{10,... | collective-permute-start | bytes 589832 | tf_op jit(solution)/shard_map/ppermute | solution.py:330
  45.8 14.9 %collective-permute-start.27 = (bf16[256,256]{1,0:T(8,128)(2,1)S(1)}, bf16[256,256]{1,0:T(8,128)(2,1)S(1)}, u32[]{:S(2)}, u32[]{:S(2)}) collective-permute-start(bf16[256,256]{1,0:T(8,128)(2,1)S(1)} %collective-permute-done.26.rest_2_), channel_id=1, source_target_pairs={{0,2},{1,3},{2,4},{3,5},{4,6},{5,7},{6,0},{7,1},{8,10},{9,11},{10,... | collective-permute-start | bytes 393224 | tf_op jit(solution)/shard_map/ppermute | solution.py:330
  45.8 16.1 %collective-permute-start.20 = (bf16[64,1536]{1,0:T(8,128)(2,1)S(1)}, bf16[64,1536]{1,0:T(8,128)(2,1)S(1)}, u32[]{:S(2)}, u32[]{:S(2)}) collective-permute-start(bf16[64,1536]{1,0:T(8,128)(2,1)S(1)} %collective-permute-done.12.rest_8_), channel_id=1, source_target_pairs={{0,1},{1,0},{2,3},{3,2},{4,5},{5,4},{6,7},{7,6},{8,9},{9,8},{10,11... | collective-permute-start | bytes 589832 | tf_op jit(solution)/shard_map/ppermute | solution.py:335
  60.7 4.0 %collective-permute-start.15 = (bf16[64,1536]{1,0:T(8,128)(2,1)S(1)}, bf16[64,1536]{1,0:T(8,128)(2,1)S(1)}, u32[]{:S(2)}, u32[]{:S(2)}) collective-permute-start(bf16[64,1536]{1,0:T(8,128)(2,1)S(1)} %collective-permute-done.14.rest_2_), channel_id=1, source_target_pairs={{0,1},{1,0},{2,3},{3,2},{4,5},{5,4},{6,7},{7,6},{8,9},{9,8},{10,11... | collective-permute-start | bytes 589832 | tf_op jit(solution)/shard_map/ppermute | solution.py:335
  61.8 4.1 %collective-permute-start.28 = (bf16[1024,256]{1,0:T(8,128)(2,1)S(1)}, bf16[1024,256]{1,0:T(8,128)(2,1)S(1)}, u32[]{:S(2)}, u32[]{:S(2)}) collective-permute-start(bf16[1024,256]{1,0:T(8,128)(2,1)S(1)} %shard_map.119.rest_0_), channel_id=1, source_target_pairs={{0,1},{1,0},{2,3},{3,2},{4,5},{5,4},{6,7},{7,6},{8,9},{9,8},{10,11... | collective-permute-start | bytes 1572872 | tf_op jit(solution)/shard_map/ppermute | solution.py:345
  61.9 4.0 %collective-permute-start.17 = (bf16[128,1536]{1,0:T(8,128)(2,1)S(1)}, bf16[128,1536]{1,0:T(8,128)(2,1)S(1)}, u32[]{:S(2)}, u32[]{:S(2)}) collective-permute-start(bf16[128,1536]{1,0:T(8,128)(2,1)S(1)} %collective-permute-done.8.rest_2_), channel_id=1, source_target_pairs={{0,1},{1,0},{2,3},{3,2},{4,5},{5,4},{6,7},{7,6},{8,9},{9,8},{10,11... | collective-permute-start | bytes 1179656 | tf_op jit(solution)/shard_map/ppermute | solution.py:335
  62.4 14.8 %collective-permute-start.29 = (bf16[1024,256]{1,0:T(8,128)(2,1)S(1)}, bf16[1024,256]{1,0:T(8,128)(2,1)S(1)}, u32[]{:S(2)}, u32[]{:S(2)}) collective-permute-start(bf16[1024,256]{1,0:T(8,128)(2,1)S(1)} %shard_map.119.rest_0_), channel_id=1, source_target_pairs={{0,8},{8,0},{16,24},{24,16},{1,9},{9,1},{17,25},{25,17},{2,10},{10... | collective-permute-start | bytes 1572872 | tf_op jit(solution)/shard_map/ppermute | solution.py:344
  63.2 24.9 %collective-permute-start.31 = (bf16[1024,256]{1,0:T(8,128)(2,1)S(1)}, bf16[1024,256]{1,0:T(8,128)(2,1)S(1)}, u32[]{:S(2)}, u32[]{:S(2)}) collective-permute-start(bf16[1024,256]{1,0:T(8,128)(2,1)S(1)} %shard_map.119.rest_0_), channel_id=1, source_target_pairs={{0,16},{8,24},{16,0},{24,8},{1,17},{9,25},{17,1},{25,9},{2,18},{10... | collective-permute-start | bytes 1572872 | tf_op jit(solution)/shard_map/ppermute | solution.py:344
  64.7 23.4 %collective-permute-start.33 = (bf16[1024,256]{1,0:T(8,128)(2,1)S(1)}, bf16[1024,256]{1,0:T(8,128)(2,1)S(1)}, u32[]{:S(2)}, u32[]{:S(2)}) collective-permute-start(bf16[1024,256]{1,0:T(8,128)(2,1)S(1)} %shard_map.119.rest_0_), channel_id=1, source_target_pairs={{0,24},{8,16},{16,8},{24,0},{1,25},{9,17},{17,9},{25,1},{2,26},{10... | collective-permute-start | bytes 1572872 | tf_op jit(solution)/shard_map/ppermute | solution.py:344
  65.9 22.7 %collective-permute-start.10 = (bf16[128,1536]{1,0:T(8,128)(2,1)S(1)}, bf16[128,1536]{1,0:T(8,128)(2,1)S(1)}, u32[]{:S(2)}, u32[]{:S(2)}) collective-permute-start(bf16[128,1536]{1,0:T(8,128)(2,1)S(1)} %collective-permute-done.9.rest_4_), channel_id=1, source_target_pairs={{0,2},{1,3},{2,4},{3,5},{4,6},{5,7},{6,0},{7,1},{8,10},{9,11},{10,... | collective-permute-start | bytes 1179656 | tf_op jit(solution)/shard_map/ppermute | solution.py:330
  65.9 22.8 %collective-permute-start.18 = (bf16[128,1536]{1,0:T(8,128)(2,1)S(1)}, bf16[128,1536]{1,0:T(8,128)(2,1)S(1)}, u32[]{:S(2)}, u32[]{:S(2)}) collective-permute-start(bf16[128,1536]{1,0:T(8,128)(2,1)S(1)} %collective-permute-done.9.rest_4_), channel_id=1, source_target_pairs={{0,1},{1,0},{2,3},{3,2},{4,5},{5,4},{6,7},{7,6},{8,9},{9,8},{10,11... | collective-permute-start | bytes 1179656 | tf_op jit(solution)/shard_map/ppermute | solution.py:335
  77.2 11.6 %collective-permute-start.30 = (bf16[1024,256]{1,0:T(8,128)(2,1)S(1)}, bf16[1024,256]{1,0:T(8,128)(2,1)S(1)}, u32[]{:S(2)}, u32[]{:S(2)}) collective-permute-start(bf16[1024,256]{1,0:T(8,128)(2,1)S(1)} %collective-permute-done.29.rest_2_), channel_id=1, source_target_pairs={{0,1},{1,0},{2,3},{3,2},{4,5},{5,4},{6,7},{7,6},{8,9},{9,8},{10,11... | collective-permute-start | bytes 1572872 | tf_op jit(solution)/shard_map/ppermute | solution.py:345
  88.0 2.0 %collective-permute-start.32 = (bf16[1024,256]{1,0:T(8,128)(2,1)S(1)}, bf16[1024,256]{1,0:T(8,128)(2,1)S(1)}, u32[]{:S(2)}, u32[]{:S(2)}) collective-permute-start(bf16[1024,256]{1,0:T(8,128)(2,1)S(1)} %collective-permute-done.31.rest_4_), channel_id=1, source_target_pairs={{0,1},{1,0},{2,3},{3,2},{4,5},{5,4},{6,7},{7,6},{8,9},{9,8},{10,11... | collective-permute-start | bytes 1572872 | tf_op jit(solution)/shard_map/ppermute | solution.py:345
  88.0 3.4 %collective-permute-start.34 = (bf16[1024,256]{1,0:T(8,128)(2,1)S(1)}, bf16[1024,256]{1,0:T(8,128)(2,1)S(1)}, u32[]{:S(2)}, u32[]{:S(2)}) collective-permute-start(bf16[1024,256]{1,0:T(8,128)(2,1)S(1)} %collective-permute-done.33.rest_6_), channel_id=1, source_target_pairs={{0,1},{1,0},{2,3},{3,2},{4,5},{5,4},{6,7},{7,6},{8,9},{9,8},{10,11... | collective-permute-start | bytes 1572872 | tf_op jit(solution)/shard_map/ppermute | solution.py:345
  88.6 5.8 %collective-permute-start.11 = (bf16[128,1536]{1,0:T(8,128)(2,1)S(1)}, bf16[128,1536]{1,0:T(8,128)(2,1)S(1)}, u32[]{:S(2)}, u32[]{:S(2)}) collective-permute-start(bf16[128,1536]{1,0:T(8,128)(2,1)S(1)} %collective-permute-done.10.rest_0_), channel_id=1, source_target_pairs={{0,1},{1,0},{2,3},{3,2},{4,5},{5,4},{6,7},{7,6},{8,9},{9,8},{10,11... | collective-permute-start | bytes 1179656 | tf_op jit(solution)/shard_map/ppermute | solution.py:335
  88.7 23.3 %collective-permute-start.38 = (s16[8,32,640]{2,1,0:T(8,128)(2,1)S(1)}, s16[8,32,640]{2,1,0:T(8,128)(2,1)S(1)}, u32[]{:S(2)}, u32[]{:S(2)}) collective-permute-start(s16[8,32,640]{2,1,0:T(8,128)(2,1)S(1)} %get-tuple-element.72), channel_id=1, source_target_pairs={{0,4},{1,5},{2,6},{3,7},{4,0},{5,1},{6,2},{7,3},{8,12},{9,13},{10,... | collective-permute-start | bytes 983048 | tf_op jit(solution)/shard_map/ppermute | solution.py:381
  88.8 7.2 %collective-permute-start.22 = (s16[144,256]{1,0:T(8,128)(2,1)S(1)}, s16[144,256]{1,0:T(8,128)(2,1)S(1)}, u32[]{:S(2)}, u32[]{:S(2)}) collective-permute-start(s16[144,256]{1,0:T(8,128)(2,1)S(1)} %get-tuple-element.50.rest_0_.known), channel_id=1, source_target_pairs={{0,8},{8,0},{16,24},{24,16},{1,9},{9,1},{17,25},{25,17},{2,10},{10... | collective-permute-start | bytes 221192 | tf_op jit(solution)/shard_map/ppermute | solution.py:372
  90.1 8.4 %collective-permute-start.23 = (s16[144,256]{1,0:T(8,128)(2,1)S(1)}, s16[144,256]{1,0:T(8,128)(2,1)S(1)}, u32[]{:S(2)}, u32[]{:S(2)}) collective-permute-start(s16[144,256]{1,0:T(8,128)(2,1)S(1)} %get-tuple-element.50.rest_0_.known), channel_id=1, source_target_pairs={{0,16},{8,24},{16,0},{24,8},{1,17},{9,25},{17,1},{25,9},{2,18},{10... | collective-permute-start | bytes 221192 | tf_op jit(solution)/shard_map/ppermute | solution.py:372
  91.5 7.0 %collective-permute-start.24 = (s16[144,256]{1,0:T(8,128)(2,1)S(1)}, s16[144,256]{1,0:T(8,128)(2,1)S(1)}, u32[]{:S(2)}, u32[]{:S(2)}) collective-permute-start(s16[144,256]{1,0:T(8,128)(2,1)S(1)} %get-tuple-element.50.rest_0_.known), channel_id=1, source_target_pairs={{0,24},{8,16},{16,8},{24,0},{1,25},{9,17},{17,9},{25,1},{2,26},{10... | collective-permute-start | bytes 221192 | tf_op jit(solution)/shard_map/ppermute | solution.py:372
  94.3 44.1 %collective-permute-start.7 = (s16[8,32,640]{2,1,0:T(8,128)(2,1)S(1)}, s16[8,32,640]{2,1,0:T(8,128)(2,1)S(1)}, u32[]{:S(2)}, u32[]{:S(2)}) collective-permute-start(s16[8,32,640]{2,1,0:T(8,128)(2,1)S(1)} %get-tuple-element.59), channel_id=1, source_target_pairs={{0,6},{1,7},{2,4},{3,5},{4,2},{5,3},{6,0},{7,1},{8,14},{9,15},{10,... | collective-permute-start | bytes 983048 | tf_op jit(solution)/shard_map/ppermute | solution.py:381
  96.0 24.1 %collective-permute-start.42 = (s16[8,32,640]{2,1,0:T(8,128)(2,1)S(1)}, s16[8,32,640]{2,1,0:T(8,128)(2,1)S(1)}, u32[]{:S(2)}, u32[]{:S(2)}) collective-permute-start(s16[8,32,640]{2,1,0:T(8,128)(2,1)S(1)} %get-tuple-element.78), channel_id=1, source_target_pairs={{0,2},{1,3},{2,0},{3,1},{4,6},{5,7},{6,4},{7,5},{8,10},{9,11},{10,... | collective-permute-start | bytes 983048 | tf_op jit(solution)/shard_map/ppermute | solution.py:381
  119.3 20.6 %collective-permute-start.39 = (bf16[4,64,512]{2,1,0:T(8,128)(2,1)S(1)}, bf16[4,64,512]{2,1,0:T(8,128)(2,1)S(1)}, u32[]{:S(2)}, u32[]{:S(2)}) collective-permute-start(bf16[4,64,512]{2,1,0:T(8,128)(2,1)S(1)} %get-tuple-element.75), channel_id=1, source_target_pairs={{0,8},{8,0},{16,24},{24,16},{1,9},{9,1},{17,25},{25,17},{2,10},{10... | collective-permute-start | bytes 786440 | tf_op jit(solution)/shard_map/ppermute | solution.py:418
  127.6 13.6 %collective-permute-start.43 = (bf16[4,64,512]{2,1,0:T(8,128)(2,1)S(1)}, bf16[4,64,512]{2,1,0:T(8,128)(2,1)S(1)}, u32[]{:S(2)}, u32[]{:S(2)}) collective-permute-start(bf16[4,64,512]{2,1,0:T(8,128)(2,1)S(1)} %get-tuple-element.81), channel_id=1, source_target_pairs={{0,8},{8,0},{16,24},{24,16},{1,9},{9,1},{17,25},{25,17},{2,10},{10... | collective-permute-start | bytes 786440 | tf_op jit(solution)/shard_map/ppermute | solution.py:418
  129.0 18.2 %collective-permute-start.44 = (bf16[4,64,512]{2,1,0:T(8,128)(2,1)S(1)}, bf16[4,64,512]{2,1,0:T(8,128)(2,1)S(1)}, u32[]{:S(2)}, u32[]{:S(2)}) collective-permute-start(bf16[4,64,512]{2,1,0:T(8,128)(2,1)S(1)} %get-tuple-element.82), channel_id=1, source_target_pairs={{0,16},{8,24},{16,0},{24,8},{1,17},{9,25},{17,1},{25,9},{2,18},{10... | collective-permute-start | bytes 786440 | tf_op jit(solution)/shard_map/ppermute | solution.py:418
  130.5 19.7 %collective-permute-start.45 = (bf16[4,64,512]{2,1,0:T(8,128)(2,1)S(1)}, bf16[4,64,512]{2,1,0:T(8,128)(2,1)S(1)}, u32[]{:S(2)}, u32[]{:S(2)}) collective-permute-start(bf16[4,64,512]{2,1,0:T(8,128)(2,1)S(1)} %get-tuple-element.83), channel_id=1, source_target_pairs={{0,24},{8,16},{16,8},{24,0},{1,25},{9,17},{17,9},{25,1},{2,26},{10... | collective-permute-start | bytes 786440 | tf_op jit(solution)/shard_map/ppermute | solution.py:418
  138.5 35.7 %collective-permute-start.40 = (bf16[4,64,512]{2,1,0:T(8,128)(2,1)S(1)}, bf16[4,64,512]{2,1,0:T(8,128)(2,1)S(1)}, u32[]{:S(2)}, u32[]{:S(2)}) collective-permute-start(bf16[4,64,512]{2,1,0:T(8,128)(2,1)S(1)} %get-tuple-element.76), channel_id=1, source_target_pairs={{0,16},{8,24},{16,0},{24,8},{1,17},{9,25},{17,1},{25,9},{2,18},{10... | collective-permute-start | bytes 786440 | tf_op jit(solution)/shard_map/ppermute | solution.py:418
  139.9 34.2 %collective-permute-start.41 = (bf16[4,64,512]{2,1,0:T(8,128)(2,1)S(1)}, bf16[4,64,512]{2,1,0:T(8,128)(2,1)S(1)}, u32[]{:S(2)}, u32[]{:S(2)}) collective-permute-start(bf16[4,64,512]{2,1,0:T(8,128)(2,1)S(1)} %get-tuple-element.77), channel_id=1, source_target_pairs={{0,24},{8,16},{16,8},{24,0},{1,25},{9,17},{17,9},{25,1},{2,26},{10... | collective-permute-start | bytes 786440 | tf_op jit(solution)/shard_map/ppermute | solution.py:418
  141.3 16.2 %collective-permute-start.46 = (bf16[4,64,512]{2,1,0:T(8,128)(2,1)S(1)}, bf16[4,64,512]{2,1,0:T(8,128)(2,1)S(1)}, u32[]{:S(2)}, u32[]{:S(2)}) collective-permute-start(bf16[4,64,512]{2,1,0:T(8,128)(2,1)S(1)} %get-tuple-element.87), channel_id=1, source_target_pairs={{0,8},{8,0},{16,24},{24,16},{1,9},{9,1},{17,25},{25,17},{2,10},{10... | collective-permute-start | bytes 786440 | tf_op jit(solution)/shard_map/ppermute | solution.py:418
  147.2 17.5 %collective-permute-start.47 = (bf16[4,64,512]{2,1,0:T(8,128)(2,1)S(1)}, bf16[4,64,512]{2,1,0:T(8,128)(2,1)S(1)}, u32[]{:S(2)}, u32[]{:S(2)}) collective-permute-start(bf16[4,64,512]{2,1,0:T(8,128)(2,1)S(1)} %get-tuple-element.88), channel_id=1, source_target_pairs={{0,16},{8,24},{16,0},{24,8},{1,17},{9,25},{17,1},{25,9},{2,18},{10... | collective-permute-start | bytes 786440 | tf_op jit(solution)/shard_map/ppermute | solution.py:418
  150.2 16.1 %collective-permute-start.48 = (bf16[4,64,512]{2,1,0:T(8,128)(2,1)S(1)}, bf16[4,64,512]{2,1,0:T(8,128)(2,1)S(1)}, u32[]{:S(2)}, u32[]{:S(2)}) collective-permute-start(bf16[4,64,512]{2,1,0:T(8,128)(2,1)S(1)} %get-tuple-element.89), channel_id=1, source_target_pairs={{0,24},{8,16},{16,8},{24,0},{1,25},{9,17},{17,9},{25,1},{2,26},{10... | collective-permute-start | bytes 786440 | tf_op jit(solution)/shard_map/ppermute | solution.py:418
  157.5 20.1 %collective-permute-start.35 = (bf16[4,64,512]{2,1,0:T(8,128)(2,1)S(1)}, bf16[4,64,512]{2,1,0:T(8,128)(2,1)S(1)}, u32[]{:S(2)}, u32[]{:S(2)}) collective-permute-start(bf16[4,64,512]{2,1,0:T(8,128)(2,1)S(1)} %get-tuple-element.69), channel_id=1, source_target_pairs={{0,8},{8,0},{16,24},{24,16},{1,9},{9,1},{17,25},{25,17},{2,10},{10... | collective-permute-start | bytes 786440 | tf_op jit(solution)/shard_map/ppermute | solution.py:418
  164.7 13.9 %collective-permute-start.36 = (bf16[4,64,512]{2,1,0:T(8,128)(2,1)S(1)}, bf16[4,64,512]{2,1,0:T(8,128)(2,1)S(1)}, u32[]{:S(2)}, u32[]{:S(2)}) collective-permute-start(bf16[4,64,512]{2,1,0:T(8,128)(2,1)S(1)} %get-tuple-element.70), channel_id=1, source_target_pairs={{0,16},{8,24},{16,0},{24,8},{1,17},{9,25},{17,1},{25,9},{2,18},{10... | collective-permute-start | bytes 786440 | tf_op jit(solution)/shard_map/ppermute | solution.py:418
  166.2 12.4 %collective-permute-start.37 = (bf16[4,64,512]{2,1,0:T(8,128)(2,1)S(1)}, bf16[4,64,512]{2,1,0:T(8,128)(2,1)S(1)}, u32[]{:S(2)}, u32[]{:S(2)}) collective-permute-start(bf16[4,64,512]{2,1,0:T(8,128)(2,1)S(1)} %get-tuple-element.71), channel_id=1, source_target_pairs={{0,24},{8,16},{16,8},{24,0},{1,25},{9,17},{17,9},{25,1},{2,26},{10... | collective-permute-start | bytes 786440 | tf_op jit(solution)/shard_map/ppermute | solution.py:418
  (8 other events, 24.7 us)

commit v3 on v2

--- a/solution.py
+++ b/solution.py
@@ -149,17 +149,40 @@
             ]
 
 
-def gru_kernel(rows, cap, nx, m, idx, x, act_table, w_s, wd_s, *rest):
+def acts_kernel(chips, rows, nx, idx, act_table, *rest):
+    given, (out, wa_s, z_s, oh_s) = rest[:nx], rest[nx:]
+    cols = wa_s.shape[1]
+    part = rows // nx
+    tail = GROUPS * STEPS
+    wa_s[...] = jnp.zeros(wa_s.shape, BF16)
+    wa_s[0 : act_table.shape[0], :] = act_table[
+        :, pl.ds(pl.multiple_of(idx[0] * cols, cols), cols)
+    ]
+    for m in range(chips):
+        spot = slice(m * part, (m + 1) * part)
+        z_s[m] = jnp.concatenate([g[tail : tail + 16, spot].astype(I32)[:8] for g in given], 1)
+    iota = lax.broadcasted_iota(I32, (CLASSES, rows), 0)
+
+    def one_chunk(m, carry):
+        z = z_s[m]
+        for step in range(STEPS):
+            hot = jnp.broadcast_to(z[step : step + 1, :], (CLASSES, rows)) == iota
+            oh_s[:, step * rows : (step + 1) * rows] = jnp.where(hot, 1.0, 0.0).astype(BF16)
+        out[m] = lax.dot_general(
+            oh_s[...], wa_s[...], (((0,), (0,)), ((), ())), preferred_element_type=F32
+        ).astype(BF16)
+        return carry
+
+    lax.fori_loop(0, chips, one_chunk, 0)
+
+
+def gru_kernel(rows, cap, nx, m, idx, x, acts, w_s, wd_s, *rest):
     given = rest[:nx]
     outs = rest[nx : 2 * nx]
-    live, wa_s, oh_s, g_s, h_s, f_s, z_s = rest[2 * nx :]
+    live, oh_s, g_s, h_s, f_s, z_s = rest[2 * nx :]
     ix, core = idx[0], idx[2]
     width = wd_s.shape[0]
-    kinds = w_s.shape[0]
-    cols = w_s.shape[1]
     part = rows // nx
-    wa_s[...] = jnp.zeros(wa_s.shape, BF16)
-    wa_s[0 : act_table.shape[0], :] = act_table[:, pl.ds(pl.multiple_of(ix * cols, cols), cols)]
     for k in range(nx):
         for l in range(2):
             got = x[k * 2 + l].astype(I32).astype(F32)
@@ -170,27 +193,23 @@
                 f_s[at, :] = got[o * cap : (o + 1) * cap, width:]
     turned = f_s[...].T
     live[...] = turned[GROUPS : GROUPS + 8, 0:part]
-    tail = GROUPS * STEPS
     z_s[0:GROUPS, :] = turned[0:GROUPS, :].astype(I32)
     spot = slice(m * part, (m + 1) * part)
     z_s[GROUPS : GROUPS * STEPS, :] = jnp.concatenate(
         [g[0 : GROUPS * (STEPS - 1), spot].astype(I32) for g in given], 1
     )
-    z_s[tail : tail + STEPS, :] = jnp.concatenate(
-        [g[tail : tail + 16, spot].astype(I32)[:STEPS] for g in given], 1
-    )
     iota = lax.broadcasted_iota(I32, (CLASSES, rows), 0)
     for step in range(STEPS):
-        for g in range(GROUPS + 1):
-            row = step * GROUPS + g if g < GROUPS else tail + step
+        for g in range(GROUPS):
+            row = step * GROUPS + g
             hot = jnp.broadcast_to(z_s[row : row + 1, :], (CLASSES, rows)) == iota
             oh_s[g * CLASSES : (g + 1) * CLASSES, step * rows : (step + 1) * rows] = jnp.where(
                 hot, 1.0, 0.0
             ).astype(BF16)
     dims = (((0,), (0,)), ((), ()))
     g_s[...] = lax.dot_general(
-        oh_s[0:kinds, :], w_s[...], dims, preferred_element_type=F32
-    ) + lax.dot_general(oh_s[kinds:, :], wa_s[...], dims, preferred_element_type=F32)
+        oh_s[...], w_s[...], dims, preferred_element_type=F32
+    ) + acts[m].astype(F32)
     keep = jnp.broadcast_to(f_s[:, GROUPS : GROUPS + 1], (rows, width)) > 0
     for step in range(STEPS):
         h = h_s[...]
@@ -248,11 +267,10 @@
         copy.wait()
 
 
-def order_kernel(chips, run, idx, *rest):
-    logps, out = rest[:-1], rest[-1]
+def order_logp(chip, chips, run, logps, out):
     slots = out.shape[2]
     part = slots // chips
-    order = slot_map(idx[1], chips, run, (slots, slots), 1)
+    order = slot_map(chip, chips, run, (slots, slots), 1)
     order = jnp.where(order, 1.0, 0.0).astype(BF16)
     for step in range(STEPS):
         value = jnp.concatenate([p[:, step * part : (step + 1) * part] for p in logps], 1)
@@ -262,6 +280,13 @@
             total = total + jnp.dot(piece, order, preferred_element_type=F32)
             value = value - piece.astype(F32)
         out[step] = total
+
+
+def last_prior_kernel(chips, nx, m, run, idx, known, live, wp_s, *rest):
+    logps, out, (st_s, logp, out_sems) = rest[nx : nx + m], rest[-4], rest[-3:]
+    states = rest[-5]
+    prior_kernel(nx, m, idx, known, live, wp_s, *rest[:nx], states, logp, st_s, out_sems)
+    order_logp(idx[1], chips, run, list(logps) + [logp], out)
 
 
 def fast_on_device(nx, ny):
@@ -395,6 +420,17 @@
             )(idx, *some, *placed)
         w_all, wd_all = placed
 
+        acts_all = call(
+            functools.partial(acts_kernel, chips, rows, nx),
+            jax.ShapeDtypeStruct((chips, STEPS * rows, cols), BF16),
+            [SMEM] + [VMEM] * (1 + nx),
+            VMEM,
+            [
+                pltpu.VMEM((CLASSES, cols), BF16),
+                pltpu.VMEM((chips, 8, rows), I32),
+                pltpu.VMEM((CLASSES, STEPS * rows), BF16),
+            ],
+        )(idx, act_table, *given)
         parts = []
         for m in range(chips):
             *outs, live = call(
@@ -404,15 +440,14 @@
                 [SMEM] + [VMEM] * (4 + nx),
                 [VMEM] * (nx + 1),
                 [
-                    pltpu.VMEM((CLASSES, cols), BF16),
-                    pltpu.VMEM((GROUPS * CLASSES + CLASSES, STEPS * rows), BF16),
+                    pltpu.VMEM((GROUPS * CLASSES, STEPS * rows), BF16),
                     pltpu.VMEM((STEPS * rows, cols), F32),
                     pltpu.VMEM((rows, width), F32),
                     pltpu.VMEM((rows, LANES), F32),
-                    pltpu.VMEM((GROUPS * STEPS + 8, rows), I32),
+                    pltpu.VMEM((GROUPS * STEPS, rows), I32),
                 ],
                 flops=2 * STEPS * rows * (GROUPS * CLASSES + width) * cols,
-            )(idx, starts[m], act_table, w_all, wd_all, *given)
+            )(idx, starts[m], acts_all, w_all, wd_all, *given)
             got = [outs[0]]
             for k in range(1, nx):
                 got.append(lax.ppermute(outs[k], "gx", swap_pairs(nx, k)))
@@ -430,29 +465,26 @@
         logps = []
         for m in range(chips):
             live, got = parts[m]
+            last = m + 1 == chips
+            kernel = functools.partial(prior_kernel, nx, m)
+            logp_shape = (GROUPS, STEPS * part)
+            scratch = [pltpu.VMEM((part, STEPS, deter), BF16), pltpu.SemaphoreType.DMA((nx,))]
+            if last:
+                kernel = functools.partial(last_prior_kernel, chips, nx, m, 2 * cap)
+                scratch.insert(1, pltpu.VMEM(logp_shape, F32))
+                logp_shape = (STEPS, GROUPS, slots)
+            more = logps if last else []
             filled, logp = call(
-                functools.partial(prior_kernel, nx, m),
-                [
-                    jax.ShapeDtypeStruct(shape, BF16),
-                    jax.ShapeDtypeStruct((GROUPS, STEPS * part), F32),
-                ],
-                [SMEM] + [VMEM] * (3 + nx) + [ANY] * len(states),
+                kernel,
+                [jax.ShapeDtypeStruct(shape, BF16), jax.ShapeDtypeStruct(logp_shape, F32)],
+                [SMEM] + [VMEM] * (3 + nx + len(more)) + [ANY] * len(states),
                 [ANY, VMEM],
-                [
-                    pltpu.VMEM((part, STEPS, deter), BF16),
-                    pltpu.SemaphoreType.DMA((nx,)),
-                ],
+                scratch,
                 flops=2 * STEPS * part * deter * GROUPS * CLASSES,
-                input_output_aliases={4 + nx: 0} if states else {},
-            )(idx, known, live, wp_all, *got, *states)
+                input_output_aliases={4 + nx + len(more): 0} if states else {},
+            )(idx, known, live, wp_all, *got, *more, *states)
             states = [filled]
             logps.append(logp)
-        logp = call(
-            functools.partial(order_kernel, chips, 2 * cap),
-            jax.ShapeDtypeStruct((STEPS, GROUPS, slots), F32),
-            [SMEM] + [VMEM] * chips,
-            VMEM,
-        )(idx, *logps)
         return (filled.reshape(slots, STEPS, deter), jnp.transpose(logp, (2, 0, 1)))
 
     return on_device

time: 184 us -> 187 us (1.016)
  waiting for transfers between devices: 82.8 us -> 77.6 us
  Pallas kernels: 52.5 us -> 57 us
  starting transfers between devices: 42 us -> 45.7 us
    ppermute x3, waiting for transfers between devices: 22.1 us -> 9.78 us  [on_device(): piece = lax.ppermute(column, 'gx', swap_pairs(nx, k)) if k else column]
    ppermute x3, waiting for transfers between devices: 0.01 us -> 9.31 us  [on_device(): given.append(lax.ppermute(known, 'gx', swap_pairs(nx, k)))]
    ppermute x12, starting transfers between devices: 15.4 us -> 20.2 us  [on_device(): got.append(lax.ppermute(outs[k], 'gx', swap_pairs(nx, k)))]
    ppermute x12, waiting for transfers between devices: 11.7 us -> 7.21 us  [on_device(): got.append(lax.ppermute(outs[k], 'gx', swap_pairs(nx, k)))]
    pallas_call x16, Pallas kernels: 52.5 us -> 57 us  [run(): pl.pallas_call(kernel, out_shape=out_shape, in_specs=ins, out_specs=outs,...]
    ppermute x7, waiting for transfers between devices: 5.62 us -> 9.39 us  [on_device(): held[n] = lax.ppermute(held[n], ('gx', 'gy'), pairs)]
  transfers between devices with their start and end apart: 49 -> 49, of which waited for: 14 -> 14; matrix products, arithmetic and copies ran while one was open for 0% -> 0% of each run, Pallas kernels for 24% -> 26%
where the time goes in v3:
time: 187 us
  waiting for transfers between devices  77.6 us (41%)
  Pallas kernels  57 us (30%)
  starting transfers between devices  45.7 us (24%)
  local copies, waits for them, and re-layouts  5.28 us (3%)
    pallas_call x16, Pallas kernels, run(): pl.pallas_call(kernel, out_shape=out_shape, in_specs=ins, out_specs=outs,...  57 us
    ppermute x9, waiting for transfers between devices, on_device(): stops[name].append(lax.ppermute(stops[name][-1], 'gy', ring))  28.1 us
    ppermute x12, starting transfers between devices, on_device(): got.append(lax.ppermute(outs[k], 'gx', swap_pairs(nx, k)))  20.2 us
    ppermute x3, waiting for transfers between devices, on_device(): starts[m] = lax.ppermute(starts[m], 'gy', swap_pairs(ny, 2 * m))  13.7 us
    ppermute x3, waiting for transfers between devices, on_device(): piece = lax.ppermute(column, 'gx', swap_pairs(nx, k)) if k else column  9.78 us
    ppermute x7, waiting for transfers between devices, on_device(): held[n] = lax.ppermute(held[n], ('gx', 'gy'), pairs)  9.39 us
    ppermute x3, waiting for transfers between devices, on_device(): given.append(lax.ppermute(known, 'gx', swap_pairs(nx, k)))  9.31 us
    ppermute x12, waiting for transfers between devices, on_device(): got.append(lax.ppermute(outs[k], 'gx', swap_pairs(nx, k)))  7.21 us
  transfers between devices with their start and end apart: 49, of which 14 were waited for; matrix products, arithmetic and copies ran while one was open for 0% of the time, Pallas kernels for 26%

profile of v3, /device:TPU:0, one launch (start us, length us, event | category | flops | bytes accessed | tf_op | source)
XLA Modules:
  0.0 186.7 jit_solution(5885462909840752460)
XLA Ops:
  0.7 1.6 copy-done
  2.3 0.9 copy-done.2
  3.2 0.8 copy-done.3
  6.0 3.3 %shard_map.113 = (s16[128,640]{1,0:T(8,128)(2,1)S(1)}, s16[128,640]{1,0:T(8,128)(2,1)S(1)}, s16[128,640]{1,0:T(8,128)(2,1)S(1)}, s16[128,640]{1,0:T(8,128)(2,1)S...) custom-call(s32[3]{0:T(128)S(1)} %pad_add_fusion.idx, ...), custom_call_target="tpu_custom_call" | custom-call | bytes 1048576 | tf_op jit(solution)/shard_map/pallas_call | solution.py:323
  9.3 4.0 %collective-permute-start.10 = (s16[144,256]{1,0:T(8,128)(2,1)S(1)}, s16[144,256]{1,0:T(8,128)(2,1)S(1)}, u32[]{:S(2)}, u32[]{:S(2)}) collective-permute-start(s16[144,256]{1,0:T(8,128)(2,1)S(1)} %get-tuple-element.50.rest_0_.known), channel_id=1, source_target_pairs={{0,24},{8,16},{16,8},{24,0},{1,25},{9,17},{17,9},{25,1},{2,26},{10... | collective-permute-start | bytes 221192 | tf_op jit(solution)/shard_map/ppermute | solution.py:397
  13.8 1.7 shard_map.116
  15.5 1.6 collective-permute-start.25
  17.7 1.3 collective-permute-start.2
  19.6 9.3 %collective-permute-done.8.rest_1_ = s16[144,256]{1,0:T(8,128)(2,1)S(1)} collective-permute-done((s16[144,256]{1,0:T(8,128)(2,1)S(1)}, s16[144,256]{1,0:T(8,128)(2,1)S(1)}, u32[]{:S(2)}, u32[]{:S(2)}) %collective-permute-start.8) | collective-permute-done | bytes 73760 | tf_op jit(solution)/shard_map/ppermute | solution.py:397
  28.9 1.5 collective-permute-start.3
  30.4 1.6 collective-permute-start.11
  32.7 1.6 collective-permute-start.15
  34.6 1.5 collective-permute-start.6
  36.2 9.0 %collective-permute-done.4.rest_5_ = s16[128,640]{1,0:T(8,128)(2,1)S(1)} collective-permute-done((s16[128,640]{1,0:T(8,128)(2,1)S(1)}, s16[128,640]{1,0:T(8,128)(2,1)S(1)}, u32[]{:S(2)}, u32[]{:S(2)}) %collective-permute-start.4) | collective-permute-done | bytes 163872 | tf_op jit(solution)/shard_map/ppermute | solution.py:394
  45.7 1.1 collective-permute-done.15.rest_8_
  47.3 0.9 collective-permute-start.26
  48.7 8.5 %collective-permute-done.26.rest_2_ = bf16[256,256]{1,0:T(8,128)(2,1)S(1)} collective-permute-done((bf16[256,256]{1,0:T(8,128)(2,1)S(1)}, bf16[256,256]{1,0:T(8,128)(2,1)S(1)}, u32[]{:S(2)}, u32[]{:S(2)}) %collective-permute-start.26) | collective-permute-done | bytes 131104 | tf_op jit(solution)/shard_map/ppermute | solution.py:355
  57.2 6.8 %collective-permute-done.27.rest_3_ = bf16[256,256]{1,0:T(8,128)(2,1)S(1)} collective-permute-done((bf16[256,256]{1,0:T(8,128)(2,1)S(1)}, bf16[256,256]{1,0:T(8,128)(2,1)S(1)}, u32[]{:S(2)}, u32[]{:S(2)}) %collective-permute-start.27) | collective-permute-done | bytes 131104 | tf_op jit(solution)/shard_map/ppermute | solution.py:355
  64.5 1.6 collective-permute-start.33
  66.6 6.9 %collective-permute-done.17.rest_2_ = bf16[64,1536]{1,0:T(8,128)(2,1)S(1)} collective-permute-done((bf16[64,1536]{1,0:T(8,128)(2,1)S(1)}, bf16[64,1536]{1,0:T(8,128)(2,1)S(1)}, u32[]{:S(2)}, u32[]{:S(2)}) %collective-permute-start.17) | collective-permute-done | bytes 196640 | tf_op jit(solution)/shard_map/ppermute | solution.py:355
  74.0 4.9 %collective-permute-done.12.rest_4_ = bf16[128,1536]{1,0:T(8,128)(2,1)S(1)} collective-permute-done((bf16[128,1536]{1,0:T(8,128)(2,1)S(1)}, bf16[128,1536]{1,0:T(8,128)(2,1)S(1)}, u32[]{:S(2)}, u32[]{:S(2)}) %collective-permute-start.12) | collective-permute-done | bytes 393248 | tf_op jit(solution)/shard_map/ppermute | solution.py:355
  78.9 1.4 collective-permute-done.33.rest_6_
  80.3 7.2 %collective-permute-done.31.rest_4_ = bf16[1024,256]{1,0:T(8,128)(2,1)S(1)} collective-permute-done((bf16[1024,256]{1,0:T(8,128)(2,1)S(1)}, bf16[1024,256]{1,0:T(8,128)(2,1)S(1)}, u32[]{:S(2)}, u32[]{:S(2)}) %collective-permute-start.31) | collective-permute-done | bytes 524320 | tf_op jit(solution)/shard_map/ppermute | solution.py:369
  87.5 1.2 collective-permute-done.29.rest_2_
  90.1 4.8 %shard_map.115.acts = bf16[4,1024,1536]{2,1,0:T(8,128)(2,1)S(1)} custom-call(s32[3]{0:T(128)S(1)} %pad_add_fusion.idx, bf16[18,6144]{1,0:T(8,128)(2,1)S(1)} %copy-done.1, s16[144,256]{1,0:T(8,128)(2,1)S(1)} %get-tuple-element.50.rest_0_.known, s16[144,256]{1,0:T(8,128)(2,1)S(1)} %collective-permute-done.8.rest_1_, ...), custom_call_target="tpu_custom_call" | custom-call | bytes 1048576 | tf_op jit(solution)/shard_map/pallas_call | solution.py:323
  95.0 0.8 shard_map.117
  95.8 3.5 %collective-permute-start.7 = (s16[8,32,640]{2,1,0:T(8,128)(2,1)S(1)}, s16[8,32,640]{2,1,0:T(8,128)(2,1)S(1)}, u32[]{:S(2)}, u32[]{:S(2)}) collective-permute-start(s16[8,32,640]{2,1,0:T(8,128)(2,1)S(1)} %get-tuple-element.59), channel_id=1, source_target_pairs={{0,6},{1,7},{2,4},{3,5},{4,2},{5,3},{6,0},{7,1},{8,14},{9,15},{10,... | collective-permute-start | bytes 983048 | tf_op jit(solution)/shard_map/ppermute | solution.py:406
  99.5 1.1 shard_map.121.wp_s
  101.3 13.7 %collective-permute-done.45.x = s16[8,32,640]{2,1,0:T(8,128)(2,1)S(1)} collective-permute-done((s16[8,32,640]{2,1,0:T(8,128)(2,1)S(1)}, s16[8,32,640]{2,1,0:T(8,128)(2,1)S(1)}, u32[]{:S(2)}, u32[]{:S(2)}) %collective-permute-start.45) | collective-permute-done | bytes 327712 | tf_op jit(solution)/shard_map/ppermute | solution.py:406
  115.1 7.3 %shard_map.126 = (bf16[4,64,512]{2,1,0:T(8,128)(2,1)S(1)}, bf16[4,64,512]{2,1,0:T(8,128)(2,1)S(1)}, bf16[4,64,512]{2,1,0:T(8,128)(2,1)S(1)}, bf16[4,64,512]{2,1,0:T(8,128)(2,1)S(1)}, f32[8,64]{1,0:T(8,128)S(1)}) custom-call(s32[3]{0:T(128)S(1)} %pad_add_fusion.idx, s16[8,32,640]{2,1,0:T(8,128)(2,1)S(1)} %collective-permute-done.45.x, ...), custom_call_target="tpu_custom_call" | custom-call | flops 4831838208 | bytes 1048576 | tf_op jit(solution)/shard_map/pallas_call | solution.py:323
  122.3 1.4 collective-permute-start.46
  123.7 7.3 %shard_map.124 = (bf16[4,64,512]{2,1,0:T(8,128)(2,1)S(1)}, bf16[4,64,512]{2,1,0:T(8,128)(2,1)S(1)}, bf16[4,64,512]{2,1,0:T(8,128)(2,1)S(1)}, bf16[4,64,512]{2,1,0:T(8,128)(2,1)S(1)}, f32[8,64]{1,0:T(8,128)S(1)}) custom-call(s32[3]{0:T(128)S(1)} %pad_add_fusion.idx, s16[8,32,640]{2,1,0:T(8,128)(2,1)S(1)} %collective-permute-done.41.x, ...), custom_call_target="tpu_custom_call" | custom-call | flops 4831838208 | bytes 1048576 | tf_op jit(solution)/shard_map/pallas_call | solution.py:323
  131.0 0.8 collective-permute-start.42
  131.8 1.6 collective-permute-start.43
  133.4 1.2 collective-permute-start.44
  134.6 7.5 %shard_map.122 = (bf16[4,64,512]{2,1,0:T(8,128)(2,1)S(1)}, bf16[4,64,512]{2,1,0:T(8,128)(2,1)S(1)}, bf16[4,64,512]{2,1,0:T(8,128)(2,1)S(1)}, bf16[4,64,512]{2,1,0:T(8,128)(2,1)S(1)}, f32[8,64]{1,0:T(8,128)S(1)}) custom-call(s32[3]{0:T(128)S(1)} %pad_add_fusion.idx, s16[8,32,640]{2,1,0:T(8,128)(2,1)S(1)} %get-tuple-element.72.x, ...), custom_call_target="tpu_custom_call" | custom-call | flops 4831838208 | bytes 1048576 | tf_op jit(solution)/shard_map/pallas_call | solution.py:323
  142.1 1.8 collective-permute-start.47
  144.4 1.3 collective-permute-start.38
  145.7 4.6 %collective-permute-start.39 = (bf16[4,64,512]{2,1,0:T(8,128)(2,1)S(1)}, bf16[4,64,512]{2,1,0:T(8,128)(2,1)S(1)}, u32[]{:S(2)}, u32[]{:S(2)}) collective-permute-start(bf16[4,64,512]{2,1,0:T(8,128)(2,1)S(1)} %get-tuple-element.76), channel_id=1, source_target_pairs={{0,16},{8,24},{16,0},{24,8},{1,17},{9,25},{17,1},{25,9},{2,18},{10... | collective-permute-start | bytes 786440 | tf_op jit(solution)/shard_map/ppermute | solution.py:453
  150.3 4.4 %collective-permute-start.40 = (bf16[4,64,512]{2,1,0:T(8,128)(2,1)S(1)}, bf16[4,64,512]{2,1,0:T(8,128)(2,1)S(1)}, u32[]{:S(2)}, u32[]{:S(2)}) collective-permute-start(bf16[4,64,512]{2,1,0:T(8,128)(2,1)S(1)} %get-tuple-element.77), channel_id=1, source_target_pairs={{0,24},{8,16},{16,8},{24,0},{1,25},{9,17},{17,9},{25,1},{2,26},{10... | collective-permute-start | bytes 786440 | tf_op jit(solution)/shard_map/ppermute | solution.py:453
  154.7 7.3 %shard_map.119 = (bf16[4,64,512]{2,1,0:T(8,128)(2,1)S(1)}, bf16[4,64,512]{2,1,0:T(8,128)(2,1)S(1)}, bf16[4,64,512]{2,1,0:T(8,128)(2,1)S(1)}, bf16[4,64,512]{2,1,0:T(8,128)(2,1)S(1)}, f32[8,64]{1,0:T(8,128)S(1)}) custom-call(s32[3]{0:T(128)S(1)} %pad_add_fusion.idx, s16[8,32,640]{2,1,0:T(8,128)(2,1)S(1)} %collective-permute-done.7.x, ...), custom_call_target="tpu_custom_call" | custom-call | flops 4831838208 | bytes 1048576 | tf_op jit(solution)/shard_map/pallas_call | solution.py:323
  162.6 5.7 %collective-permute-done.39.rest_2_ = bf16[4,64,512]{2,1,0:T(8,128)(2,1)S(1)} collective-permute-done((bf16[4,64,512]{2,1,0:T(8,128)(2,1)S(1)}, bf16[4,64,512]{2,1,0:T(8,128)(2,1)S(1)}, u32[]{:S(2)}, u32[]{:S(2)}) %collective-permute-start.39) | collective-permute-done | bytes 262176 | tf_op jit(solution)/shard_map/ppermute | solution.py:453
  168.9 1.4 collective-permute-start.37
  170.3 3.3 %shard_map.123 = (bf16[4,4,16,4,2048]{4,3,2,1,0:T(4,128)(2,1)}, f32[32,256]{1,0:T(8,128)S(1)}) custom-call(s32[3]{0:T(128)S(1)} %pad_add_fusion.idx, s16[144,256]{1,0:T(8,128)(2,1)S(1)} %get-tuple-element.50.rest_0_.known, f32[8,64]{1,0:T(8,128)S(1)} %get-tuple-element.73.live, bf16[2048,1024]{1,0:T(8,128)(2,1)S(1)} %shard_map.121.wp_s, ...), custom_call_target="tpu_custom_call" | custom-call | flops 1073741824 | bytes 1048576 | tf_op jit(solution)/shard_map/pallas_call | solution.py:323
  173.7 3.3 %shard_map.125 = (bf16[4,4,16,4,2048]{4,3,2,1,0:T(4,128)(2,1)}, f32[32,256]{1,0:T(8,128)S(1)}) custom-call(s32[3]{0:T(128)S(1)} %pad_add_fusion.idx, s16[144,256]{1,0:T(8,128)(2,1)S(1)} %get-tuple-element.50.rest_0_.known, f32[8,64]{1,0:T(8,128)S(1)} %get-tuple-element.80.live, ...), custom_call_target="tpu_custom_call", output_to_operand_aliasing={{0}: (8, {})} | custom-call | flops 1073741824 | bytes 1048576 | tf_op jit(solution)/shard_map/pallas_call | solution.py:323
  177.0 3.6 %shard_map.127 = (bf16[4,4,16,4,2048]{4,3,2,1,0:T(4,128)(2,1)}, f32[32,256]{1,0:T(8,128)S(1)}) custom-call(s32[3]{0:T(128)S(1)} %pad_add_fusion.idx, s16[144,256]{1,0:T(8,128)(2,1)S(1)} %get-tuple-element.50.rest_0_.known, f32[8,64]{1,0:T(8,128)S(1)} %get-tuple-element.88.live, ...), custom_call_target="tpu_custom_call", output_to_operand_aliasing={{0}: (8, {})} | custom-call | flops 1073741824 | bytes 1048576 | tf_op jit(solution)/shard_map/pallas_call | solution.py:323
  180.6 1.5 collective-permute-done.36.rest_2_
  182.1 4.4 %shard_map.128 = (bf16[4,4,16,4,2048]{4,3,2,1,0:T(4,128)(2,1)}, f32[4,32,256]{2,1,0:T(8,128)}) custom-call(s32[3]{0:T(128)S(1)} %pad_add_fusion.idx, s16[144,256]{1,0:T(8,128)(2,1)S(1)} %get-tuple-element.50.rest_0_.known, f32[8,64]{1,0:T(8,128)S(1)} %get-tuple-element.66.live, ...), custom_call_target="tpu_custom_call", output_to_operand_aliasing={{0}: (11, {})} | custom-call | flops 1073741824 | bytes 1048576 | tf_op jit(solution)/shard_map/pallas_call | solution.py:323
  (81 shorter events, 12.0 us)
Async XLA Ops:
  9.3 8.4 %collective-permute-start.10 = (s16[144,256]{1,0:T(8,128)(2,1)S(1)}, s16[144,256]{1,0:T(8,128)(2,1)S(1)}, u32[]{:S(2)}, u32[]{:S(2)}) collective-permute-start(s16[144,256]{1,0:T(8,128)(2,1)S(1)} %get-tuple-element.50.rest_0_.known), channel_id=1, source_target_pairs={{0,24},{8,16},{16,8},{24,0},{1,25},{9,17},{17,9},{25,1},{2,26},{10... | collective-permute-start | bytes 221192 | tf_op jit(solution)/shard_map/ppermute | solution.py:397
  13.3 5.7 %collective-permute-start.9 = (s16[144,256]{1,0:T(8,128)(2,1)S(1)}, s16[144,256]{1,0:T(8,128)(2,1)S(1)}, u32[]{:S(2)}, u32[]{:S(2)}) collective-permute-start(s16[144,256]{1,0:T(8,128)(2,1)S(1)} %get-tuple-element.50.rest_0_.known), channel_id=1, source_target_pairs={{0,16},{8,24},{16,0},{24,8},{1,17},{9,25},{17,1},{25,9},{2,18},{10... | collective-permute-start | bytes 221192 | tf_op jit(solution)/shard_map/ppermute | solution.py:397
  15.5 14.9 %collective-permute-start.25 = (bf16[256,256]{1,0:T(8,128)(2,1)S(1)}, bf16[256,256]{1,0:T(8,128)(2,1)S(1)}, u32[]{:S(2)}, u32[]{:S(2)}) collective-permute-start(bf16[256,256]{1,0:T(8,128)(2,1)S(1)} %get-tuple-element.67.rest_0_), channel_id=1, source_target_pairs={{0,2},{1,3},{2,4},{3,5},{4,6},{5,7},{6,0},{7,1},{8,10},{9,11},{10,... | collective-permute-start | bytes 393224 | tf_op jit(solution)/shard_map/ppermute | solution.py:355
  17.2 14.8 %collective-permute-start = (s16[128,640]{1,0:T(8,128)(2,1)S(1)}, s16[128,640]{1,0:T(8,128)(2,1)S(1)}, u32[]{:S(2)}, u32[]{:S(2)}) collective-permute-start(s16[128,640]{1,0:T(8,128)(2,1)S(1)} %get-tuple-element.52), channel_id=1, source_target_pairs={{0,1},{1,0},{2,3},{3,2},{4,5},{5,4},{6,7},{7,6},{8,9},{9,8},{10,11... | collective-permute-start | bytes 491528 | tf_op jit(solution)/shard_map/ppermute | solution.py:394
  17.2 14.8 %collective-permute-start.1 = (s16[128,640]{1,0:T(8,128)(2,1)S(1)}, s16[128,640]{1,0:T(8,128)(2,1)S(1)}, u32[]{:S(2)}, u32[]{:S(2)}) collective-permute-start(s16[128,640]{1,0:T(8,128)(2,1)S(1)} %get-tuple-element.53), channel_id=1, source_target_pairs={{0,8},{1,9},{2,10},{3,11},{4,12},{5,13},{6,14},{7,15},{8,0},{9,1},... | collective-permute-start | bytes 491528 | tf_op jit(solution)/shard_map/ppermute | solution.py:394
  17.7 15.0 %collective-permute-start.2 = (s16[128,640]{1,0:T(8,128)(2,1)S(1)}, s16[128,640]{1,0:T(8,128)(2,1)S(1)}, u32[]{:S(2)}, u32[]{:S(2)}) collective-permute-start(s16[128,640]{1,0:T(8,128)(2,1)S(1)} %get-tuple-element.54), channel_id=1, source_target_pairs={{0,9},{1,8},{2,11},{3,10},{4,13},{5,12},{6,15},{7,14},{8,1},{9,0},... | collective-permute-start | bytes 491528 | tf_op jit(solution)/shard_map/ppermute | solution.py:394
  19.0 9.8 %collective-permute-start.8 = (s16[144,256]{1,0:T(8,128)(2,1)S(1)}, s16[144,256]{1,0:T(8,128)(2,1)S(1)}, u32[]{:S(2)}, u32[]{:S(2)}) collective-permute-start(s16[144,256]{1,0:T(8,128)(2,1)S(1)} %get-tuple-element.50.rest_0_.known), channel_id=1, source_target_pairs={{0,8},{8,0},{16,24},{24,16},{1,9},{9,1},{17,25},{25,17},{2,10},{10... | collective-permute-start | bytes 221192 | tf_op jit(solution)/shard_map/ppermute | solution.py:397
  28.9 5.8 %collective-permute-start.3 = (s16[128,640]{1,0:T(8,128)(2,1)S(1)}, s16[128,640]{1,0:T(8,128)(2,1)S(1)}, u32[]{:S(2)}, u32[]{:S(2)}) collective-permute-start(s16[128,640]{1,0:T(8,128)(2,1)S(1)} %get-tuple-element.55), channel_id=1, source_target_pairs={{0,16},{1,17},{2,18},{3,19},{4,20},{5,21},{6,22},{7,23},{8,24},{9,... | collective-permute-start | bytes 491528 | tf_op jit(solution)/shard_map/ppermute | solution.py:394
  30.4 17.8 %collective-permute-start.11 = (bf16[128,1536]{1,0:T(8,128)(2,1)S(1)}, bf16[128,1536]{1,0:T(8,128)(2,1)S(1)}, u32[]{:S(2)}, u32[]{:S(2)}) collective-permute-start(bf16[128,1536]{1,0:T(8,128)(2,1)S(1)} %get-tuple-element.60.rest_0_), channel_id=1, source_target_pairs={{0,2},{1,3},{2,4},{3,5},{4,6},{5,7},{6,0},{7,1},{8,10},{9,11},{10,... | collective-permute-start | bytes 1179656 | tf_op jit(solution)/shard_map/ppermute | solution.py:355
  32.0 13.2 %collective-permute-start.4 = (s16[128,640]{1,0:T(8,128)(2,1)S(1)}, s16[128,640]{1,0:T(8,128)(2,1)S(1)}, u32[]{:S(2)}, u32[]{:S(2)}) collective-permute-start(s16[128,640]{1,0:T(8,128)(2,1)S(1)} %get-tuple-element.56), channel_id=1, source_target_pairs={{0,17},{1,16},{2,19},{3,18},{4,21},{5,20},{6,23},{7,22},{8,25},{9,... | collective-permute-start | bytes 491528 | tf_op jit(solution)/shard_map/ppermute | solution.py:394
  32.0 13.2 %collective-permute-start.5 = (s16[128,640]{1,0:T(8,128)(2,1)S(1)}, s16[128,640]{1,0:T(8,128)(2,1)S(1)}, u32[]{:S(2)}, u32[]{:S(2)}) collective-permute-start(s16[128,640]{1,0:T(8,128)(2,1)S(1)} %get-tuple-element.57), channel_id=1, source_target_pairs={{0,24},{1,25},{2,26},{3,27},{4,28},{5,29},{6,30},{7,31},{8,16},{9,... | collective-permute-start | bytes 491528 | tf_op jit(solution)/shard_map/ppermute | solution.py:394
  32.7 14.1 %collective-permute-start.15 = (bf16[64,1536]{1,0:T(8,128)(2,1)S(1)}, bf16[64,1536]{1,0:T(8,128)(2,1)S(1)}, u32[]{:S(2)}, u32[]{:S(2)}) collective-permute-start(bf16[64,1536]{1,0:T(8,128)(2,1)S(1)} %get-tuple-element.61.rest_6_), channel_id=1, source_target_pairs={{0,2},{1,3},{2,4},{3,5},{4,6},{5,7},{6,0},{7,1},{8,10},{9,11},{10,... | collective-permute-start | bytes 589832 | tf_op jit(solution)/shard_map/ppermute | solution.py:355
  34.6 12.6 %collective-permute-start.6 = (s16[128,640]{1,0:T(8,128)(2,1)S(1)}, s16[128,640]{1,0:T(8,128)(2,1)S(1)}, u32[]{:S(2)}, u32[]{:S(2)}) collective-permute-start(s16[128,640]{1,0:T(8,128)(2,1)S(1)} %get-tuple-element.58), channel_id=1, source_target_pairs={{0,25},{1,24},{2,27},{3,26},{4,29},{5,28},{6,31},{7,30},{8,17},{9,... | collective-permute-start | bytes 491528 | tf_op jit(solution)/shard_map/ppermute | solution.py:394
  45.2 3.0 %collective-permute-start.22 = (bf16[64,1536]{1,0:T(8,128)(2,1)S(1)}, bf16[64,1536]{1,0:T(8,128)(2,1)S(1)}, u32[]{:S(2)}, u32[]{:S(2)}) collective-permute-start(bf16[64,1536]{1,0:T(8,128)(2,1)S(1)} %get-tuple-element.61.rest_6_), channel_id=1, source_target_pairs={{0,1},{1,0},{2,3},{3,2},{4,5},{5,4},{6,7},{7,6},{8,9},{9,8},{10,11... | collective-permute-start | bytes 589832 | tf_op jit(solution)/shard_map/ppermute | solution.py:360
  45.2 21.0 %collective-permute-start.19 = (bf16[128,1536]{1,0:T(8,128)(2,1)S(1)}, bf16[128,1536]{1,0:T(8,128)(2,1)S(1)}, u32[]{:S(2)}, u32[]{:S(2)}) collective-permute-start(bf16[128,1536]{1,0:T(8,128)(2,1)S(1)} %get-tuple-element.60.rest_0_), channel_id=1, source_target_pairs={{0,1},{1,0},{2,3},{3,2},{4,5},{5,4},{6,7},{7,6},{8,9},{9,8},{10,11... | collective-permute-start | bytes 1179656 | tf_op jit(solution)/shard_map/ppermute | solution.py:360
  46.8 10.4 %collective-permute-start.16 = (bf16[64,1536]{1,0:T(8,128)(2,1)S(1)}, bf16[64,1536]{1,0:T(8,128)(2,1)S(1)}, u32[]{:S(2)}, u32[]{:S(2)}) collective-permute-start(bf16[64,1536]{1,0:T(8,128)(2,1)S(1)} %collective-permute-done.15.rest_8_), channel_id=1, source_target_pairs={{0,2},{1,3},{2,4},{3,5},{4,6},{5,7},{6,0},{7,1},{8,10},{9,11},{10,... | collective-permute-start | bytes 589832 | tf_op jit(solution)/shard_map/ppermute | solution.py:355
  47.3 9.9 %collective-permute-start.26 = (bf16[256,256]{1,0:T(8,128)(2,1)S(1)}, bf16[256,256]{1,0:T(8,128)(2,1)S(1)}, u32[]{:S(2)}, u32[]{:S(2)}) collective-permute-start(bf16[256,256]{1,0:T(8,128)(2,1)S(1)} %collective-permute-done.25.rest_1_), channel_id=1, source_target_pairs={{0,2},{1,3},{2,4},{3,5},{4,6},{5,7},{6,0},{7,1},{8,10},{9,11},{10,... | collective-permute-start | bytes 393224 | tf_op jit(solution)/shard_map/ppermute | solution.py:355
  48.2 25.9 %collective-permute-start.20 = (bf16[128,1536]{1,0:T(8,128)(2,1)S(1)}, bf16[128,1536]{1,0:T(8,128)(2,1)S(1)}, u32[]{:S(2)}, u32[]{:S(2)}) collective-permute-start(bf16[128,1536]{1,0:T(8,128)(2,1)S(1)} %collective-permute-done.11.rest_2_), channel_id=1, source_target_pairs={{0,1},{1,0},{2,3},{3,2},{4,5},{5,4},{6,7},{7,6},{8,9},{9,8},{10,11... | collective-permute-start | bytes 1179656 | tf_op jit(solution)/shard_map/ppermute | solution.py:360
  48.2 16.3 %collective-permute-start.23 = (bf16[64,1536]{1,0:T(8,128)(2,1)S(1)}, bf16[64,1536]{1,0:T(8,128)(2,1)S(1)}, u32[]{:S(2)}, u32[]{:S(2)}) collective-permute-start(bf16[64,1536]{1,0:T(8,128)(2,1)S(1)} %collective-permute-done.15.rest_8_), channel_id=1, source_target_pairs={{0,1},{1,0},{2,3},{3,2},{4,5},{5,4},{6,7},{7,6},{8,9},{9,8},{10,11... | collective-permute-start | bytes 589832 | tf_op jit(solution)/shard_map/ppermute | solution.py:360
  57.1 6.8 %collective-permute-start.27 = (bf16[256,256]{1,0:T(8,128)(2,1)S(1)}, bf16[256,256]{1,0:T(8,128)(2,1)S(1)}, u32[]{:S(2)}, u32[]{:S(2)}) collective-permute-start(bf16[256,256]{1,0:T(8,128)(2,1)S(1)} %collective-permute-done.26.rest_2_), channel_id=1, source_target_pairs={{0,2},{1,3},{2,4},{3,5},{4,6},{5,7},{6,0},{7,1},{8,10},{9,11},{10,... | collective-permute-start | bytes 393224 | tf_op jit(solution)/shard_map/ppermute | solution.py:355
  57.1 9.4 %collective-permute-start.24 = (bf16[64,1536]{1,0:T(8,128)(2,1)S(1)}, bf16[64,1536]{1,0:T(8,128)(2,1)S(1)}, u32[]{:S(2)}, u32[]{:S(2)}) collective-permute-start(bf16[64,1536]{1,0:T(8,128)(2,1)S(1)} %collective-permute-done.16.rest_10_), channel_id=1, source_target_pairs={{0,1},{1,0},{2,3},{3,2},{4,5},{5,4},{6,7},{7,6},{8,9},{9,8},{10,11... | collective-permute-start | bytes 589832 | tf_op jit(solution)/shard_map/ppermute | solution.py:360
  63.9 9.6 %collective-permute-start.17 = (bf16[64,1536]{1,0:T(8,128)(2,1)S(1)}, bf16[64,1536]{1,0:T(8,128)(2,1)S(1)}, u32[]{:S(2)}, u32[]{:S(2)}) collective-permute-start(bf16[64,1536]{1,0:T(8,128)(2,1)S(1)} %collective-permute-done.16.rest_10_), channel_id=1, source_target_pairs={{0,2},{1,3},{2,4},{3,5},{4,6},{5,7},{6,0},{7,1},{8,10},{9,11},{10,... | collective-permute-start | bytes 589832 | tf_op jit(solution)/shard_map/ppermute | solution.py:355
  64.5 15.8 %collective-permute-start.33 = (bf16[1024,256]{1,0:T(8,128)(2,1)S(1)}, bf16[1024,256]{1,0:T(8,128)(2,1)S(1)}, u32[]{:S(2)}, u32[]{:S(2)}) collective-permute-start(bf16[1024,256]{1,0:T(8,128)(2,1)S(1)} %shard_map.120.rest_0_), channel_id=1, source_target_pairs={{0,24},{8,16},{16,8},{24,0},{1,25},{9,17},{17,9},{25,1},{2,26},{10... | collective-permute-start | bytes 1572872 | tf_op jit(solution)/shard_map/ppermute | solution.py:369
  66.1 21.3 %collective-permute-start.31 = (bf16[1024,256]{1,0:T(8,128)(2,1)S(1)}, bf16[1024,256]{1,0:T(8,128)(2,1)S(1)}, u32[]{:S(2)}, u32[]{:S(2)}) collective-permute-start(bf16[1024,256]{1,0:T(8,128)(2,1)S(1)} %shard_map.120.rest_0_), channel_id=1, source_target_pairs={{0,16},{8,24},{16,0},{24,8},{1,17},{9,25},{17,1},{25,9},{2,18},{10... | collective-permute-start | bytes 1572872 | tf_op jit(solution)/shard_map/ppermute | solution.py:369
  66.6 12.3 %collective-permute-start.12 = (bf16[128,1536]{1,0:T(8,128)(2,1)S(1)}, bf16[128,1536]{1,0:T(8,128)(2,1)S(1)}, u32[]{:S(2)}, u32[]{:S(2)}) collective-permute-start(bf16[128,1536]{1,0:T(8,128)(2,1)S(1)} %collective-permute-done.11.rest_2_), channel_id=1, source_target_pairs={{0,2},{1,3},{2,4},{3,5},{4,6},{5,7},{6,0},{7,1},{8,10},{9,11},{10,... | collective-permute-start | bytes 1179656 | tf_op jit(solution)/shard_map/ppermute | solution.py:355
  73.5 15.2 %collective-permute-start.29 = (bf16[1024,256]{1,0:T(8,128)(2,1)S(1)}, bf16[1024,256]{1,0:T(8,128)(2,1)S(1)}, u32[]{:S(2)}, u32[]{:S(2)}) collective-permute-start(bf16[1024,256]{1,0:T(8,128)(2,1)S(1)} %shard_map.120.rest_0_), channel_id=1, source_target_pairs={{0,8},{8,0},{16,24},{24,16},{1,9},{9,1},{17,25},{25,17},{2,10},{10... | collective-permute-start | bytes 1572872 | tf_op jit(solution)/shard_map/ppermute | solution.py:369
  74.0 14.7 %collective-permute-start.28 = (bf16[1024,256]{1,0:T(8,128)(2,1)S(1)}, bf16[1024,256]{1,0:T(8,128)(2,1)S(1)}, u32[]{:S(2)}, u32[]{:S(2)}) collective-permute-start(bf16[1024,256]{1,0:T(8,128)(2,1)S(1)} %shard_map.120.rest_0_), channel_id=1, source_target_pairs={{0,1},{1,0},{2,3},{3,2},{4,5},{5,4},{6,7},{7,6},{8,9},{9,8},{10,11... | collective-permute-start | bytes 1572872 | tf_op jit(solution)/shard_map/ppermute | solution.py:370
  78.9 10.3 %collective-permute-start.13 = (bf16[128,1536]{1,0:T(8,128)(2,1)S(1)}, bf16[128,1536]{1,0:T(8,128)(2,1)S(1)}, u32[]{:S(2)}, u32[]{:S(2)}) collective-permute-start(bf16[128,1536]{1,0:T(8,128)(2,1)S(1)} %collective-permute-done.12.rest_4_), channel_id=1, source_target_pairs={{0,2},{1,3},{2,4},{3,5},{4,6},{5,7},{6,0},{7,1},{8,10},{9,11},{10,... | collective-permute-start | bytes 1179656 | tf_op jit(solution)/shard_map/ppermute | solution.py:355
  80.3 9.9 %collective-permute-start.34 = (bf16[1024,256]{1,0:T(8,128)(2,1)S(1)}, bf16[1024,256]{1,0:T(8,128)(2,1)S(1)}, u32[]{:S(2)}, u32[]{:S(2)}) collective-permute-start(bf16[1024,256]{1,0:T(8,128)(2,1)S(1)} %collective-permute-done.33.rest_6_), channel_id=1, source_target_pairs={{0,1},{1,0},{2,3},{3,2},{4,5},{5,4},{6,7},{7,6},{8,9},{9,8},{10,11... | collective-permute-start | bytes 1572872 | tf_op jit(solution)/shard_map/ppermute | solution.py:370
  88.7 7.0 %collective-permute-start.32 = (bf16[1024,256]{1,0:T(8,128)(2,1)S(1)}, bf16[1024,256]{1,0:T(8,128)(2,1)S(1)}, u32[]{:S(2)}, u32[]{:S(2)}) collective-permute-start(bf16[1024,256]{1,0:T(8,128)(2,1)S(1)} %collective-permute-done.31.rest_4_), channel_id=1, source_target_pairs={{0,1},{1,0},{2,3},{3,2},{4,5},{5,4},{6,7},{7,6},{8,9},{9,8},{10,11... | collective-permute-start | bytes 1572872 | tf_op jit(solution)/shard_map/ppermute | solution.py:370
  88.7 10.5 %collective-permute-start.30 = (bf16[1024,256]{1,0:T(8,128)(2,1)S(1)}, bf16[1024,256]{1,0:T(8,128)(2,1)S(1)}, u32[]{:S(2)}, u32[]{:S(2)}) collective-permute-start(bf16[1024,256]{1,0:T(8,128)(2,1)S(1)} %collective-permute-done.29.rest_2_), channel_id=1, source_target_pairs={{0,1},{1,0},{2,3},{3,2},{4,5},{5,4},{6,7},{7,6},{8,9},{9,8},{10,11... | collective-permute-start | bytes 1572872 | tf_op jit(solution)/shard_map/ppermute | solution.py:370
  89.2 11.4 %collective-permute-start.14 = (bf16[128,1536]{1,0:T(8,128)(2,1)S(1)}, bf16[128,1536]{1,0:T(8,128)(2,1)S(1)}, u32[]{:S(2)}, u32[]{:S(2)}) collective-permute-start(bf16[128,1536]{1,0:T(8,128)(2,1)S(1)} %collective-permute-done.13.rest_0_), channel_id=1, source_target_pairs={{0,1},{1,0},{2,3},{3,2},{4,5},{5,4},{6,7},{7,6},{8,9},{9,8},{10,11... | collective-permute-start | bytes 1179656 | tf_op jit(solution)/shard_map/ppermute | solution.py:360
  89.4 25.6 %collective-permute-start.45 = (s16[8,32,640]{2,1,0:T(8,128)(2,1)S(1)}, s16[8,32,640]{2,1,0:T(8,128)(2,1)S(1)}, u32[]{:S(2)}, u32[]{:S(2)}) collective-permute-start(s16[8,32,640]{2,1,0:T(8,128)(2,1)S(1)} %get-tuple-element.87), channel_id=1, source_target_pairs={{0,4},{1,5},{2,6},{3,7},{4,0},{5,1},{6,2},{7,3},{8,12},{9,13},{10,... | collective-permute-start | bytes 983048 | tf_op jit(solution)/shard_map/ppermute | solution.py:406
  90.1 10.5 %collective-permute-start.18 = (bf16[64,1536]{1,0:T(8,128)(2,1)S(1)}, bf16[64,1536]{1,0:T(8,128)(2,1)S(1)}, u32[]{:S(2)}, u32[]{:S(2)}) collective-permute-start(bf16[64,1536]{1,0:T(8,128)(2,1)S(1)} %collective-permute-done.17.rest_2_), channel_id=1, source_target_pairs={{0,1},{1,0},{2,3},{3,2},{4,5},{5,4},{6,7},{7,6},{8,9},{9,8},{10,11... | collective-permute-start | bytes 589832 | tf_op jit(solution)/shard_map/ppermute | solution.py:360
  95.8 46.3 %collective-permute-start.7 = (s16[8,32,640]{2,1,0:T(8,128)(2,1)S(1)}, s16[8,32,640]{2,1,0:T(8,128)(2,1)S(1)}, u32[]{:S(2)}, u32[]{:S(2)}) collective-permute-start(s16[8,32,640]{2,1,0:T(8,128)(2,1)S(1)} %get-tuple-element.59), channel_id=1, source_target_pairs={{0,6},{1,7},{2,4},{3,5},{4,2},{5,3},{6,0},{7,1},{8,14},{9,15},{10,... | collective-permute-start | bytes 983048 | tf_op jit(solution)/shard_map/ppermute | solution.py:406
  99.2 24.5 %collective-permute-start.41 = (s16[8,32,640]{2,1,0:T(8,128)(2,1)S(1)}, s16[8,32,640]{2,1,0:T(8,128)(2,1)S(1)}, u32[]{:S(2)}, u32[]{:S(2)}) collective-permute-start(s16[8,32,640]{2,1,0:T(8,128)(2,1)S(1)} %get-tuple-element.79), channel_id=1, source_target_pairs={{0,2},{1,3},{2,0},{3,1},{4,6},{5,7},{6,4},{7,5},{8,10},{9,11},{10,... | collective-permute-start | bytes 983048 | tf_op jit(solution)/shard_map/ppermute | solution.py:406
  122.3 21.5 %collective-permute-start.46 = (bf16[4,64,512]{2,1,0:T(8,128)(2,1)S(1)}, bf16[4,64,512]{2,1,0:T(8,128)(2,1)S(1)}, u32[]{:S(2)}, u32[]{:S(2)}) collective-permute-start(bf16[4,64,512]{2,1,0:T(8,128)(2,1)S(1)} %get-tuple-element.90), channel_id=1, source_target_pairs={{0,8},{8,0},{16,24},{24,16},{1,9},{9,1},{17,25},{25,17},{2,10},{10... | collective-permute-start | bytes 786440 | tf_op jit(solution)/shard_map/ppermute | solution.py:453
  131.0 13.3 %collective-permute-start.42 = (bf16[4,64,512]{2,1,0:T(8,128)(2,1)S(1)}, bf16[4,64,512]{2,1,0:T(8,128)(2,1)S(1)}, u32[]{:S(2)}, u32[]{:S(2)}) collective-permute-start(bf16[4,64,512]{2,1,0:T(8,128)(2,1)S(1)} %get-tuple-element.82), channel_id=1, source_target_pairs={{0,8},{8,0},{16,24},{24,16},{1,9},{9,1},{17,25},{25,17},{2,10},{10... | collective-permute-start | bytes 786440 | tf_op jit(solution)/shard_map/ppermute | solution.py:453
  131.8 13.9 %collective-permute-start.43 = (bf16[4,64,512]{2,1,0:T(8,128)(2,1)S(1)}, bf16[4,64,512]{2,1,0:T(8,128)(2,1)S(1)}, u32[]{:S(2)}, u32[]{:S(2)}) collective-permute-start(bf16[4,64,512]{2,1,0:T(8,128)(2,1)S(1)} %get-tuple-element.83), channel_id=1, source_target_pairs={{0,16},{8,24},{16,0},{24,8},{1,17},{9,25},{17,1},{25,9},{2,18},{10... | collective-permute-start | bytes 786440 | tf_op jit(solution)/shard_map/ppermute | solution.py:453
  133.4 16.9 %collective-permute-start.44 = (bf16[4,64,512]{2,1,0:T(8,128)(2,1)S(1)}, bf16[4,64,512]{2,1,0:T(8,128)(2,1)S(1)}, u32[]{:S(2)}, u32[]{:S(2)}) collective-permute-start(bf16[4,64,512]{2,1,0:T(8,128)(2,1)S(1)} %get-tuple-element.84), channel_id=1, source_target_pairs={{0,24},{8,16},{16,8},{24,0},{1,25},{9,17},{17,9},{25,1},{2,26},{10... | collective-permute-start | bytes 786440 | tf_op jit(solution)/shard_map/ppermute | solution.py:453
  142.1 34.9 %collective-permute-start.47 = (bf16[4,64,512]{2,1,0:T(8,128)(2,1)S(1)}, bf16[4,64,512]{2,1,0:T(8,128)(2,1)S(1)}, u32[]{:S(2)}, u32[]{:S(2)}) collective-permute-start(bf16[4,64,512]{2,1,0:T(8,128)(2,1)S(1)} %get-tuple-element.91), channel_id=1, source_target_pairs={{0,16},{8,24},{16,0},{24,8},{1,17},{9,25},{17,1},{25,9},{2,18},{10... | collective-permute-start | bytes 786440 | tf_op jit(solution)/shard_map/ppermute | solution.py:453
  143.9 33.1 %collective-permute-start.48 = (bf16[4,64,512]{2,1,0:T(8,128)(2,1)S(1)}, bf16[4,64,512]{2,1,0:T(8,128)(2,1)S(1)}, u32[]{:S(2)}, u32[]{:S(2)}) collective-permute-start(bf16[4,64,512]{2,1,0:T(8,128)(2,1)S(1)} %get-tuple-element.92), channel_id=1, source_target_pairs={{0,24},{8,16},{16,8},{24,0},{1,25},{9,17},{17,9},{25,1},{2,26},{10... | collective-permute-start | bytes 786440 | tf_op jit(solution)/shard_map/ppermute | solution.py:453
  144.4 17.6 %collective-permute-start.38 = (bf16[4,64,512]{2,1,0:T(8,128)(2,1)S(1)}, bf16[4,64,512]{2,1,0:T(8,128)(2,1)S(1)}, u32[]{:S(2)}, u32[]{:S(2)}) collective-permute-start(bf16[4,64,512]{2,1,0:T(8,128)(2,1)S(1)} %get-tuple-element.75), channel_id=1, source_target_pairs={{0,8},{8,0},{16,24},{24,16},{1,9},{9,1},{17,25},{25,17},{2,10},{10... | collective-permute-start | bytes 786440 | tf_op jit(solution)/shard_map/ppermute | solution.py:453
  145.7 22.6 %collective-permute-start.39 = (bf16[4,64,512]{2,1,0:T(8,128)(2,1)S(1)}, bf16[4,64,512]{2,1,0:T(8,128)(2,1)S(1)}, u32[]{:S(2)}, u32[]{:S(2)}) collective-permute-start(bf16[4,64,512]{2,1,0:T(8,128)(2,1)S(1)} %get-tuple-element.76), channel_id=1, source_target_pairs={{0,16},{8,24},{16,0},{24,8},{1,17},{9,25},{17,1},{25,9},{2,18},{10... | collective-permute-start | bytes 786440 | tf_op jit(solution)/shard_map/ppermute | solution.py:453
  150.3 18.6 %collective-permute-start.40 = (bf16[4,64,512]{2,1,0:T(8,128)(2,1)S(1)}, bf16[4,64,512]{2,1,0:T(8,128)(2,1)S(1)}, u32[]{:S(2)}, u32[]{:S(2)}) collective-permute-start(bf16[4,64,512]{2,1,0:T(8,128)(2,1)S(1)} %get-tuple-element.77), channel_id=1, source_target_pairs={{0,24},{8,16},{16,8},{24,0},{1,25},{9,17},{17,9},{25,1},{2,26},{10... | collective-permute-start | bytes 786440 | tf_op jit(solution)/shard_map/ppermute | solution.py:453
  162.0 18.6 %collective-permute-start.35 = (bf16[4,64,512]{2,1,0:T(8,128)(2,1)S(1)}, bf16[4,64,512]{2,1,0:T(8,128)(2,1)S(1)}, u32[]{:S(2)}, u32[]{:S(2)}) collective-permute-start(bf16[4,64,512]{2,1,0:T(8,128)(2,1)S(1)} %get-tuple-element.69), channel_id=1, source_target_pairs={{0,8},{8,0},{16,24},{24,16},{1,9},{9,1},{17,25},{25,17},{2,10},{10... | collective-permute-start | bytes 786440 | tf_op jit(solution)/shard_map/ppermute | solution.py:453
  168.3 13.8 %collective-permute-start.36 = (bf16[4,64,512]{2,1,0:T(8,128)(2,1)S(1)}, bf16[4,64,512]{2,1,0:T(8,128)(2,1)S(1)}, u32[]{:S(2)}, u32[]{:S(2)}) collective-permute-start(bf16[4,64,512]{2,1,0:T(8,128)(2,1)S(1)} %get-tuple-element.70), channel_id=1, source_target_pairs={{0,16},{8,24},{16,0},{24,8},{1,17},{9,25},{17,1},{25,9},{2,18},{10... | collective-permute-start | bytes 786440 | tf_op jit(solution)/shard_map/ppermute | solution.py:453
  168.9 13.2 %collective-permute-start.37 = (bf16[4,64,512]{2,1,0:T(8,128)(2,1)S(1)}, bf16[4,64,512]{2,1,0:T(8,128)(2,1)S(1)}, u32[]{:S(2)}, u32[]{:S(2)}) collective-permute-start(bf16[4,64,512]{2,1,0:T(8,128)(2,1)S(1)} %get-tuple-element.71), channel_id=1, source_target_pairs={{0,24},{8,16},{16,8},{24,0},{1,25},{9,17},{17,9},{25,1},{2,26},{10... | collective-permute-start | bytes 786440 | tf_op jit(solution)/shard_map/ppermute | solution.py:453
  (8 other events, 91.3 us)
